TPU v7x, 256 devices: a whole 4x4x8 slice. The times are simulated.
256 devices in a mesh: rep: 64 (over z, x, core), batch: 4 (over y).
Axes of the slice: x: 4, y: 4, z: 8, core: 2. Of those that a mesh axis runs over, the one named last changes fastest.
Arguments:
- embed: bfloat16 [32768, 1024], P(('rep', 'batch')), may hold values from -9 to 9
- actions: int32 [32768, 5], P(('rep', 'batch')), may hold values from 0 to 17
- rewards: float32 [32768, 5], P(('rep', 'batch')), may hold values from -1 to 1
- ends: int32 [32768, 5], P(('rep', 'batch')), may hold values 0 or 1
- behaviour: float32 [32768, 5, 18], P(('rep', 'batch')), may hold values from -5 to 5
- w_hidden: bfloat16 [1024, 1024], replicated, may hold values from -0.1875 to 0.1875
- w_action: bfloat16 [18, 1024], replicated, may hold values from -3 to 3
- w_heads: bfloat16 [1024, 36], replicated, may hold values from -0.1875 to 0.1875
Outputs:
- grad_hidden: float32 [1024, 1024], replicated
- grad_action: float32 [18, 1024], replicated
- grad_heads: float32 [1024, 36], replicated
- targets: float32 [32768, 5], P(('rep', 'batch'))
All inputs are finite; a program needn't handle non-finite values. No bound on the sum of `ends` on one device may be relied on, other than what follows from the above.
Results may differ from a plain program's by a relative error of at most 0.0057.
Values sent between devices are 32-bit elements; how exact they have to be, the bound alone decides.
No kernel may reach another device: no remote copies, remote signals or barrier semaphores. Data moves between devices by JAX's collectives and lax.ppermute only.
A program may use at most 64 MiB of HBM per device.

v0:
```python
import jax
import jax.numpy as jnp
from jax import lax
from jax.sharding import Mesh
from jax.sharding import PartitionSpec as P

REP = ("rep_0", "rep_1", "rep_2")
REP_BATCH = ("rep_0", "rep_1", "rep_2", "batch")


DISCOUNT = 0.997
TRACE_LAMBDA = 0.95
EPSILON = 1e-06


def from_everyone(array, axis):
    copies = jnp.broadcast_to(array, (lax.axis_size(axis), *array.shape))
    return lax.all_to_all(copies, axis, split_axis=0, concat_axis=0, tiled=True)


def of_everyone(array, axis):
    return from_everyone(array, axis).sum(axis=0)


def cut_along(array, dim, devices):
    shape = array.shape
    tiles = array.reshape(*shape[:dim], devices, shape[dim] // devices, *shape[dim + 1 :])
    return jnp.moveaxis(tiles, dim, 0)


def sent_and_summed(array, axis, dim):
    tiles = cut_along(array, dim, lax.axis_size(axis))
    arrived = lax.all_to_all(tiles, axis, split_axis=0, concat_axis=0, tiled=True)
    return arrived.sum(axis=0)


def sum_in_two_steps(array, axes, dim):
    far, near = axes
    tiles = cut_along(array, dim, lax.axis_size(far))
    nearer = sent_and_summed(tiles, near, dim + 1)
    arrived = lax.all_to_all(nearer, far, split_axis=0, concat_axis=0, tiled=True)
    return arrived.sum(axis=0)


def padded_to(lines, devices):
    spare = -len(lines) % devices
    return jnp.pad(lines, [(0, spare)] + [(0, 0)] * (lines.ndim - 1))


def laid_out(tiles, dim):
    tiles = jnp.moveaxis(tiles, 0, dim)
    shape = tiles.shape
    return tiles.reshape(*shape[:dim], shape[dim] * shape[dim + 1], *shape[dim + 2 :])


def whole_of(array, axes, dim):
    far, near = axes
    initial = from_everyone(array, far)
    tiles = jnp.swapaxes(from_everyone(initial, near), 0, 1)
    return laid_out(tiles.reshape(-1, *array.shape), dim)


def sum_by_parts(array, axes):
    own = sum_in_two_steps(
        padded_to(array, lax.axis_size(axes[0]) * lax.axis_size(axes[1])), axes, 0
    )
    whole = whole_of(own, axes, 0)
    return whole[: len(array)].reshape(array.shape)


def together(arrays, axis):
    ends = [0]
    for a in arrays:
        ends.append(ends[-1] + a.size)
    subtotal = sum_by_parts(jnp.concatenate([a.ravel() for a in arrays]), axis)
    return tuple((subtotal[b:e].reshape(a.shape) for a, b, e in zip(arrays, ends, ends[1:])))


def unroll(emb_block, act_block, w_hidden, w_action, w_heads):
    act_count = w_action.shape[0]
    unroll_len = act_block.shape[1]
    onehot = (
        act_block[:, :, None] == jnp.arange(act_count, dtype=jnp.int32)[None, None, :]
    ).astype(jnp.bfloat16)
    hidden_state = emb_block.astype(jnp.float32)
    rounded = []
    squashed = []
    head_out = []
    for step in range(unroll_len):
        state_bf16 = hidden_state.astype(jnp.bfloat16)
        rounded.append(state_bf16)
        head_out.append(jnp.dot(state_bf16, w_heads, preferred_element_type=jnp.float32))
        preact = jnp.dot(state_bf16, w_hidden, preferred_element_type=jnp.float32)
        preact = preact + jnp.dot(onehot[:, step], w_action, preferred_element_type=jnp.float32)
        squash = jnp.tanh(preact)
        squashed.append(squash)
        hidden_state = hidden_state + squash
    state_bf16 = hidden_state.astype(jnp.bfloat16)
    head_out.append(jnp.dot(state_bf16, w_heads, preferred_element_type=jnp.float32))
    return (jnp.stack(head_out), rounded, squashed, onehot)


def estimates(head_out, actions, rewards, ends, behaviour):
    act_count = behaviour.shape[-1]
    unroll_len = actions.shape[1]
    logits = head_out[:, :, :act_count]
    qvalues = head_out[:, :, act_count:]
    exp_logits = jnp.exp(logits)
    policy = exp_logits / jnp.sum(exp_logits, axis=-1, keepdims=True)
    values = jnp.sum(policy * qvalues, axis=-1)
    onehot_f = (
        jnp.transpose(actions)[:, :, None] == jnp.arange(act_count, dtype=jnp.int32)[None, None, :]
    ).astype(jnp.float32)
    logpol = logits[:unroll_len] - jnp.log(jnp.sum(exp_logits[:unroll_len], axis=-1, keepdims=True))
    behave = jnp.transpose(behaviour, (1, 0, 2))
    behave_log = behave - jnp.log(jnp.sum(jnp.exp(behave), axis=-1, keepdims=True))
    ratios = jnp.exp(jnp.sum(onehot_f * (logpol - behave_log), axis=-1))
    clipped = jnp.minimum(1.0, ratios)
    not_ended = 1.0 - jnp.transpose(ends).astype(jnp.float32)
    td_error = jnp.transpose(rewards) + DISCOUNT * not_ended * values[1:] - values[:unroll_len]
    carried = jnp.zeros_like(values[0])
    collected = []
    for step in range(unroll_len - 1, -1, -1):
        carried = (
            clipped[step] * td_error[step]
            + DISCOUNT * TRACE_LAMBDA * not_ended[step] * clipped[step] * carried
        )
        collected.append(carried)
    collected = jnp.stack(collected[::-1])
    targets = values[:unroll_len] + collected
    advantage = qvalues[:unroll_len] - values[:unroll_len, :, None]
    return (policy[:unroll_len], onehot_f, targets, advantage)


def objective(head_out, onehot_f, targets, cmpo_policy, taken_weight, norm_scale):
    act_count = onehot_f.shape[-1]
    unroll_len = onehot_f.shape[0]
    logits = head_out[:unroll_len, :, :act_count]
    qvalues = head_out[:unroll_len, :, act_count:]
    logpol = logits - jnp.log(jnp.sum(jnp.exp(logits), axis=-1, keepdims=True))
    q_taken = jnp.sum(onehot_f * qvalues, axis=-1)
    value_term = 0.5 * (q_taken - targets) ** 2
    policy_term = -taken_weight * jnp.sum(onehot_f * logpol, axis=-1)
    regular = -jnp.sum(cmpo_policy * logpol, axis=-1)
    return jnp.sum(value_term + policy_term + regular) * norm_scale


def backward(cotangent, rounded, squashed, onehot, w_hidden, w_heads):
    unroll_len = len(squashed)
    hid = w_hidden.shape[0]
    grad_state = jnp.zeros(squashed[0].shape, jnp.float32)
    grad_hidden = jnp.zeros((hid, hid), jnp.float32)
    grad_action = jnp.zeros((hid, onehot.shape[-1]), jnp.float32)
    grad_heads = jnp.zeros(w_heads.shape, jnp.float32)
    for step in range(unroll_len - 1, -1, -1):
        grad_pre = (grad_state * (1.0 - squashed[step] * squashed[step])).astype(jnp.bfloat16)
        head_cot = cotangent[step].astype(jnp.bfloat16)
        grad_hidden = grad_hidden + jnp.dot(
            rounded[step].T, grad_pre, preferred_element_type=jnp.float32
        )
        grad_action = grad_action + jnp.dot(
            grad_pre.T, onehot[:, step], preferred_element_type=jnp.float32
        )
        grad_heads = grad_heads + jnp.dot(
            rounded[step].T, head_cot, preferred_element_type=jnp.float32
        )
        grad_state = grad_state + jnp.dot(grad_pre, w_hidden.T, preferred_element_type=jnp.float32)
        grad_state = grad_state + jnp.dot(head_cot, w_heads.T, preferred_element_type=jnp.float32)
    return (grad_hidden, grad_action, grad_heads)


def body(embed, actions, rewards, ends, behaviour, w_hidden, w_action, w_heads):
    rows_here = embed.shape[0]
    unroll_len = actions.shape[1]
    act_count = w_action.shape[0]
    groups = lax.axis_size("batch")
    devices = lax.axis_size(REP) * groups
    head_out, rounded, squashed, onehot = unroll(embed, actions, w_hidden, w_action, w_heads)
    policy, onehot_f, targets, advantage = estimates(head_out, actions, rewards, ends, behaviour)
    spread = of_everyone(jnp.sum(advantage * advantage), "batch")
    spread_scale = jnp.sqrt(spread / (groups * rows_here * unroll_len * act_count) + EPSILON)
    weights = jnp.exp(jnp.clip(advantage / spread_scale, -1.0, 1.0))
    norm_mass = jnp.sum(policy * weights, axis=-1)
    mass_sum = of_everyone(jnp.sum(norm_mass), "batch")
    mean_mass = mass_sum / (groups * rows_here * unroll_len)
    cmpo_policy = policy * weights / norm_mass[:, :, None]
    taken_weight = jnp.sum(onehot_f * weights, axis=-1) / mean_mass
    cotangent = jax.grad(objective)(
        head_out,
        onehot_f,
        targets,
        cmpo_policy,
        taken_weight,
        1.0 / (devices * rows_here * unroll_len),
    )
    grad_hidden, grad_action, grad_heads = backward(
        cotangent, rounded, squashed, onehot, w_hidden, w_heads
    )
    grad_hidden, grad_action, grad_heads = together(
        (grad_hidden, grad_action, grad_heads), (("rep_0", "rep_1"), ("rep_2", "batch"))
    )
    return (grad_hidden, grad_action.T, grad_heads, targets.T)


def solution(mesh):
    torus = Mesh(
        mesh.devices.reshape(8, 4, 2, mesh.shape["batch"]), ("rep_0", "rep_1", "rep_2", "batch")
    )
    return jax.shard_map(
        body,
        mesh=torus,
        in_specs=(
            P(REP_BATCH, None),
            P(REP_BATCH, None),
            P(REP_BATCH, None),
            P(REP_BATCH, None),
            P(REP_BATCH, None, None),
            P(),
            P(),
            P(),
        ),
        out_specs=(P(), P(), P(), P(REP_BATCH, None)),
        check_vma=False,
    )
```

profile of v0, /device:TPU:1, one launch (start us, length us, event | category | flops | bytes accessed | tf_op | source)
XLA Modules:
  0.0 279.7 jit_solution(2779072188944931606)
XLA Ops:
  1.5 1.1 constant_dynamic-update-slice_fusion.9
  2.7 1.4 fusion.52
  4.1 1.3 fusion.23
  6.6 1.1 fusion.48
  11.7 1.2 broadcast_in_dim.44
  12.9 5.0 %all-to-all-start = ((f32[4,1,1]{2,1,0:T(1,128)}), f32[4,1,1]{2,1,0:T(1,128)S(1)}, u32[]{:S(2)}, u32[]{:S(2)}) async-start(f32[4,1,1]{2,1,0:T(1,128)} %broadcast_in_dim.44), calls=%async_computation | async-start | bytes 4096 | tf_op jit(solution)/shard_map/all_to_all | solution.py:18
  18.7 1.6 fusion.45
  20.4 3.6 %fusion.46 = f32[1024,1024]{1,0:T(8,128)} fusion(bf16[128,1024]{1,0:T(8,128)(2,1)} %copy-done.10, f32[128,1024]{1,0:T(8,128)S(1)} %fusion.5), kind=kOutput, calls=%fused_computation.127 | convolution fusion | flops 268959744 | bytes 4980736 | tf_op jit(solution)/shard_map/dot_general | solution.py:158
  25.6 1.6 select_reduce_fusion.1
  27.8 8.2 %all_to_all.40 = f32[4,1,1]{2,1,0:T(1,128)S(1)} all-to-all(f32[4,1,1]{2,1,0:T(1,128)S(1)} %broadcast_in_dim.46), channel_id=1, replica_groups=mesh['rep_0'=8,'rep_1'=4,'rep_2'=2,'batch'=4] {'batch'}, dimensions={0} | all-to-all | bytes 32 | tf_op jit(solution)/shard_map/all_to_all | solution.py:18
  38.9 1.1 fusion.60
  40.1 1.1 convolution_add_fusion.14
  41.2 1.1 convolution_add_fusion.13
  42.3 1.1 convolution_add_fusion.12
  44.7 2.1 reshape.61
  46.8 1.5 multiply_convert_fusion.2
  48.3 2.7 fusion.57
  52.2 2.7 fusion.58
  56.0 2.7 fusion.59
  61.1 6.9 %fusion.3 = f32[128,8,8,128]{3,2,1,0:T(8,128)S(1)} fusion(f32[1024,1024]{1,0:T(8,128)} %fusion.59, f32[1024,1024]{1,0:T(8,128)} %fusion.58, f32[1024,1024]{1,0:T(8,128)} %fusion.46, f32[1024,1024]{1,0:T(8,128)} %fusion.57, bf16[128,1024]{1,0:T(8,128)(2,1)S(1)} %fusion.10, bf16[128,1024]{1,0:T(8,128)(2,1)S(1)} %copy-done.2), kind=kOutput, calls=%fused_computation.5 | convolution fusion | flops 272629760 | bytes 21495808 | tf_op jit(solution)/shard_map/dot_general | solution.py:158
  69.0 4.6 %pad_maximum_fusion = f32[1103872]{0:T(1024)} fusion(f32[36864]{0:T(1024)S(1)} %copy-done.18, f32[18432]{0:T(1024)S(1)} %reshape.60, f32[1048576]{0:T(1024)S(1)} %bitcast.153), kind=kLoop, calls=%fused_computation.3 | loop fusion | flops 2207744 | bytes 8830976 | tf_op jit(solution)/shard_map/concatenate | solution.py:75
  73.6 6.7 %reshape_reshape.6 = f32[32,8,4312]{2,1,0:T(8,128)} reshape(f32[1103872]{0:T(1024)} %pad_maximum_fusion) | data formatting | bytes 8830976 | tf_op jit(solution)/shard_map/reshape;reshape | solution.py:27
  80.3 3.7 %copy.45 = f32[8,32,4312]{2,1,0:T(8,128)S(1)} copy(f32[8,32,4312]{2,0,1:T(8,128)} %bitcast.151) | data formatting | bytes 8830976 | tf_op jit(solution)/shard_map/transpose | solution.py:28
  84.0 57.8 %all_to_all.41 = f32[8,32,4312]{2,1,0:T(8,128)} all-to-all(f32[8,32,4312]{2,1,0:T(8,128)S(1)} %copy.45), channel_id=1, replica_groups=mesh['rep_0'=8,'rep_1'=4,'rep_2'=2,'batch'=4] {'rep_2','batch'}, dimensions={0} | all-to-all | bytes 8830976 | tf_op jit(solution)/shard_map/all_to_all | solution.py:33
  141.8 2.5 reduce_sum.162
  144.7 27.5 %all_to_all.42 = f32[32,1,4312]{2,1,0:T(1,128)S(1)} all-to-all(f32[32,1,4312]{2,1,0:T(1,128)S(1)} %all_to_all.29), channel_id=1, replica_groups=mesh['rep_0'=8,'rep_1'=4,'rep_2'=2,'batch'=4] {'rep_0','rep_1'}, dimensions={0} | all-to-all | bytes 1103872 | tf_op jit(solution)/shard_map/all_to_all | solution.py:41
  172.9 20.7 %all_to_all.43 = f32[32,1,4312]{2,1,0:T(1,128)S(1)} all-to-all(f32[32,1,4312]{2,1,0:T(1,128)S(1)} %broadcast_in_dim.49), channel_id=1, replica_groups=mesh['rep_0'=8,'rep_1'=4,'rep_2'=2,'batch'=4] {'rep_0','rep_1'}, dimensions={0} | all-to-all | bytes 1103872 | tf_op jit(solution)/shard_map/all_to_all | solution.py:18
  194.0 57.6 %all_to_all.44 = f32[8,32,4312]{2,1,0:T(8,128)S(1)} all-to-all(f32[8,32,4312]{2,1,0:T(8,128)S(1)} %broadcast_in_dim.50), channel_id=1, replica_groups=mesh['rep_0'=8,'rep_1'=4,'rep_2'=2,'batch'=4] {'rep_2','batch'}, dimensions={0} | all-to-all | bytes 8830976 | tf_op jit(solution)/shard_map/all_to_all | solution.py:18
  251.6 4.6 %copy.46 = f32[32,8,4312]{2,1,0:T(8,128)} copy(f32[32,8,4312]{2,0,1:T(8,128)S(1)} %bitcast.152) | data formatting | bytes 8830976 | tf_op jit(solution)/shard_map/transpose | solution.py:59
  256.2 6.9 %reshape_reshape.7 = f32[1103872]{0:T(1024)} reshape(f32[32,8,4312]{2,1,0:T(8,128)} %copy.46) | data formatting | bytes 8830976 | tf_op jit(solution)/shard_map/reshape;reshape | solution.py:53
  263.1 8.8 %slice.169 = f32[1078,1024]{1,0:T(8,128)} reshape(f32[32,8,4312]{2,1,0:T(8,128)} %copy.46) | data formatting | bytes 8830976 | tf_op jit(solution)/shard_map/slice | solution.py:76
  271.9 4.9 %slice.184 = f32[1024,1024]{1,0:T(8,128)} slice(f32[1078,1024]{1,0:T(8,128)} %slice.169), slice={[0:1024], [0:1024]} | slice | bytes 8388608 | tf_op jit(solution)/shard_map/slice | solution.py:76
  (111 shorter events, 21.5 us)
Async XLA Ops:
  0.6 2.1 copy-start
  0.6 5.2 %copy-start.2 = (bf16[128,1024]{1,0:T(8,128)(2,1)S(1)}, bf16[128,1024]{1,0:T(8,128)(2,1)}, u32[]{:S(2)}) copy-start(bf16[128,1024]{1,0:T(8,128)(2,1)} %param.8) | copy-start | bytes 786436
  0.7 5.2 %copy-start.15 = (bf16[18,1024]{1,0:T(8,128)(2,1)S(1)}, bf16[18,1024]{1,0:T(8,128)(2,1)}, u32[]{:S(2)}) copy-start(bf16[18,1024]{1,0:T(8,128)(2,1)} %param.14) | copy-start | bytes 110596
  5.4 3.9 %copy-start.8 = (bf16[128,1024]{1,0:T(8,128)(2,1)}, bf16[128,1024]{1,0:T(8,128)(2,1)S(1)}, u32[]{:S(2)}) copy-start(bf16[128,1024]{1,0:T(8,128)(2,1)S(1)} %get-tuple-element.58) | copy-start | bytes 786436
  6.1 2.0 copy-start.11
  6.2 3.3 %copy-start.4 = (bf16[128,1024]{1,0:T(8,128)(2,1)}, bf16[128,1024]{1,0:T(8,128)(2,1)S(1)}, u32[]{:S(2)}) copy-start(bf16[128,1024]{1,0:T(8,128)(2,1)S(1)} %get-tuple-element.60) | copy-start | bytes 786436
  7.7 2.0 copy-start.6
  7.7 1.5 copy-start.3
  8.5 1.4 copy-start.10
  8.5 1.6 copy-start.13
  8.5 2.6 copy-start.23
  8.5 2.6 copy-start.24
  10.1 1.0 copy-start.16
  12.9 11.4 %all-to-all-start = ((f32[4,1,1]{2,1,0:T(1,128)}), f32[4,1,1]{2,1,0:T(1,128)S(1)}, u32[]{:S(2)}, u32[]{:S(2)}) async-start(f32[4,1,1]{2,1,0:T(1,128)} %broadcast_in_dim.44), calls=%async_computation | async-start | bytes 4096 | tf_op jit(solution)/shard_map/all_to_all | solution.py:18
  18.7 5.3 %copy-start.21 = (f32[128,5,18]{0,2,1:T(8,128)S(1)}, f32[128,5,18]{0,2,1:T(8,128)}, u32[]{:S(2)}) copy-start(f32[128,5,18]{0,2,1:T(8,128)} %param.12) | copy-start | bytes 138244
  18.7 5.4 %copy-start.17 = (f32[5,128,36]{1,2,0:T(8,128)S(1)}, f32[5,128,36]{1,2,0:T(8,128)}, u32[]{:S(2)}) copy-start(f32[5,128,36]{1,2,0:T(8,128)} %copy-done.16) | copy-start | bytes 276484
  18.7 5.4 %copy-start.20 = (s32[128,5]{0,1:T(8,128)S(1)}, s32[128,5]{0,1:T(8,128)}, u32[]{:S(2)}) copy-start(s32[128,5]{0,1:T(8,128)} %param.9) | copy-start | bytes 7684
  18.7 5.4 %copy-start.22 = (f32[6,128,18]{1,2,0:T(8,128)S(1)}, f32[6,128,18]{1,2,0:T(8,128)}, u32[]{:S(2)}) copy-start(f32[6,128,18]{1,2,0:T(8,128)} %get-tuple-element.40) | copy-start | bytes 165892
  24.0 24.3 %copy-start.7 = (bf16[128,1024]{1,0:T(8,128)(2,1)S(1)}, bf16[128,1024]{1,0:T(8,128)(2,1)}, u32[]{:S(2)}) copy-start(bf16[128,1024]{1,0:T(8,128)(2,1)} %copy-done.6) | copy-start | bytes 786436
  48.3 3.6 %copy-start.14 = (f32[128,1024]{1,0:T(8,128)S(1)}, f32[128,1024]{1,0:T(8,128)}, u32[]{:S(2)}) copy-start(f32[128,1024]{1,0:T(8,128)} %get-tuple-element.62) | copy-start | bytes 1572868
  48.3 3.8 %copy-start.5 = (bf16[128,1024]{1,0:T(8,128)(2,1)S(1)}, bf16[128,1024]{1,0:T(8,128)(2,1)}, u32[]{:S(2)}) copy-start(bf16[128,1024]{1,0:T(8,128)(2,1)} %copy-done.4) | copy-start | bytes 786436
  52.1 3.6 %copy-start.12 = (f32[128,1024]{1,0:T(8,128)S(1)}, f32[128,1024]{1,0:T(8,128)}, u32[]{:S(2)}) copy-start(f32[128,1024]{1,0:T(8,128)} %copy-done.11) | copy-start | bytes 1572868
  52.1 3.8 %copy-start.9 = (bf16[128,1024]{1,0:T(8,128)(2,1)S(1)}, bf16[128,1024]{1,0:T(8,128)(2,1)}, u32[]{:S(2)}) copy-start(bf16[128,1024]{1,0:T(8,128)(2,1)} %copy-done.8) | copy-start | bytes 786436
  56.0 3.9 %copy-start.19 = (f32[1024,18]{0,1:T(8,128)S(1)}, f32[1024,18]{0,1:T(8,128)}, u32[]{:S(2)}) copy-start(f32[1024,18]{0,1:T(8,128)} %fusion.41) | copy-start | bytes 221188
  68.0 1.0 copy-start.18
  271.9 7.8 %copy-start.1 = (bf16[1024,1024]{1,0:T(8,128)(2,1)S(1)}, bf16[1024,1024]{1,0:T(8,128)(2,1)}, u32[]{:S(2)}) copy-start(bf16[1024,1024]{1,0:T(8,128)(2,1)} %param.13) | copy-start | bytes 6291460
  271.9 4.9 %slice-start.1 = ((f32[1103872]{0:T(1024)}), f32[36864]{0:T(1024)S(1)}, s32[]{:S(2)}) async-start(f32[1103872]{0:T(1024)} %reshape_reshape.7), calls=%async_computation.7 | async-start | bytes 294912 | tf_op jit(solution)/shard_map/slice | solution.py:76
  271.9 6.4 %slice-start = ((f32[1103872]{0:T(1024)}), f32[18432]{0:T(1024)S(1)}, s32[]{:S(2)}) async-start(f32[1103872]{0:T(1024)} %reshape_reshape.7), calls=%async_computation.6 | async-start | bytes 147456 | tf_op jit(solution)/shard_map/slice | solution.py:76
where the time goes:
time: 281 us; the launch traced here: 280 us
  blocking collectives  172 us (61%)
  local copies, waits for them, and re-layouts  46.3 us (16%)
  matrix products  39.6 us (14%)
  other arithmetic  14.3 us (5%)
  starting transfers between devices  5 us (2%)
    all_to_all x3, blocking collectives, from_everyone(): return lax.all_to_all(copies, axis, split_axis=0, concat_axis=0, tiled=True)  86.5 us
    all_to_all x1, blocking collectives, sent_and_summed(): lax.all_to_all(tiles, axis, split_axis=0, concat_axis=0, tiled=True)  57.8 us
    all_to_all x1, blocking collectives, sum_in_two_steps(): lax.all_to_all(nearer, far, split_axis=0, concat_axis=0, tiled=True)  27.5 us
    dot_general x5, matrix products, backward(): jnp.dot(rounded[step].T, grad_pre, preferred_element_type=jnp.float32)  18.7 us
    slice x6, local copies, waits for them, and re-layouts, together(): subtotal[b:e].reshape(a.shape)  13.7 us
    another operation x1, local copies, waits for them, and re-layouts, laid_out(): tiles.reshape(*shape[:dim], shape[dim] * shape[dim + 1], *shape[dim + 2:])  6.86 us
    another operation x1, local copies, waits for them, and re-layouts, cut_along(): array.reshape(*shape[:dim], devices, shape[dim] // devices, *shape[dim +...  6.65 us
  transfers between devices with their start and end apart: 1, of which 0 were waited for; matrix products, arithmetic and copies ran while one was open for 2% of the time, Pallas kernels for 0%

commit v1 on v0

v1 whole, which is shorter than its diff:
```python
import jax
import jax.numpy as jnp
from jax import lax
from jax.experimental import pallas as pl
from jax.experimental.pallas import tpu as pltpu
from jax.sharding import Mesh
from jax.sharding import PartitionSpec as P

ALL = ("z", "x", "core", "y")
PLANE = ("x", "y")

DISCOUNT = 0.997
TRACE_LAMBDA = 0.95
EPSILON = 1e-06

LANES = 128
F32 = jnp.float32
BF16 = jnp.bfloat16

VMEM = pl.BlockSpec(memory_space=pltpu.VMEM)
SMEM = pl.BlockSpec(memory_space=pltpu.SMEM)


def dot(a, b):
    return jnp.dot(a, b, preferred_element_type=F32)


def dot_nt(a, b):
    return lax.dot_general(a, b, (((1,), (1,)), ((), ())), preferred_element_type=F32)


def dot_tn(a, b):
    return lax.dot_general(a, b, (((0,), (0,)), ((), ())), preferred_element_type=F32)


def kernel_call(body, outs, inputs, scratch=(), scalars=0):
    return pl.pallas_call(
        body,
        out_shape=tuple(jax.ShapeDtypeStruct(s, d) for s, d in outs),
        in_specs=[SMEM] * scalars + [VMEM] * (len(inputs) - scalars),
        out_specs=tuple(VMEM for _ in outs),
        scratch_shapes=list(scratch),
        name=body.__name__,
        compiler_params=pltpu.CompilerParams(vmem_limit_bytes=48 * 1024 * 1024),
    )(*inputs)


def lanes_of(rows):
    return lax.broadcasted_iota(jnp.int32, (rows, LANES), 1)


def onehot_of(act_ref, step):
    rows = act_ref.shape[0]
    return lanes_of(rows) == act_ref[:, step : step + 1]


def pad_rows(dst, src):
    dst[...] = jnp.zeros_like(dst)
    dst[: src.shape[0], :] = src[...]


def pad_lanes(dst, src):
    dst[...] = jnp.zeros_like(dst)
    dst[:, : src.shape[1]] = src[...]


def policy_of(out, count):
    valid = lanes_of(out.shape[0]) < count
    q = jnp.where(valid, pltpu.roll(out, LANES - count, 1), 0.0)
    logits = jnp.where(valid, out, 0.0)
    e = jnp.where(valid, jnp.exp(logits), 0.0)
    total = jnp.sum(e, axis=1, keepdims=True)
    pi = e / total
    v = jnp.sum(pi * q, axis=1, keepdims=True)
    return valid, logits, q, pi, total, v


def unroll_kernel(emb, act, wh, wa, whd, s_out, t_out, st_out, o_out, ssq_out, wap, whp):
    count = wa.shape[0]
    steps = act.shape[1]
    rows = emb.shape[0]
    pad_rows(wap, wa)
    pad_lanes(whp, whd)
    state = emb[...].astype(F32)
    for k in range(steps):
        s = state.astype(BF16)
        s_out[k * rows : (k + 1) * rows, :] = s
        if k < steps - 1:
            oh = onehot_of(act, k).astype(F32).astype(BF16)
            t = jnp.tanh(dot(s, wh[...]) + dot(oh, wap[...]))
            t_out[k * rows : (k + 1) * rows, :] = t
            state = state + t
    st_out[...] = state
    out = dot(s_out[...], whp[...])
    o_out[...] = out
    valid, _, q, _, _, v = policy_of(out, count)
    adv = jnp.where(valid, q - v, 0.0)
    part = jnp.sum(jnp.sum(adv * adv, axis=0, keepdims=True), axis=1, keepdims=True)
    ssq_out[...] = jnp.broadcast_to(part, ssq_out.shape)


def targets_kernel(act, rew, ends, beh, wh, wa, whd, s, st, o, tg_out, sT_out, wap, whp):
    count = wa.shape[0]
    steps = act.shape[1]
    rows = st.shape[0]
    pad_rows(wap, wa)
    pad_lanes(whp, whd)
    last = steps - 1
    oh = onehot_of(act, last).astype(F32).astype(BF16)
    t = jnp.tanh(dot(s[last * rows :, :], wh[...]) + dot(oh, wap[...]))
    final = (st[...] + t).astype(BF16)
    v_next = policy_of(dot(final, whp[...]), count)[-1]
    lane = lanes_of(rows)
    carried = jnp.zeros((rows, 1), F32)
    tg = jnp.zeros((rows, LANES), F32)
    for k in range(last, -1, -1):
        valid, logits, _, _, total, v = policy_of(o[k * rows : (k + 1) * rows, :], count)
        b = beh[k * rows : (k + 1) * rows, :]
        b_total = jnp.sum(jnp.where(valid, jnp.exp(b), 0.0), axis=1, keepdims=True)
        gap = (logits - jnp.log(total)) - (b - jnp.log(b_total))
        ratio = jnp.exp(jnp.sum(jnp.where(onehot_of(act, k), gap, 0.0), axis=1, keepdims=True))
        clipped = jnp.minimum(1.0, ratio)
        open_ = 1.0 - ends[:, k : k + 1].astype(F32)
        td = rew[:, k : k + 1] + DISCOUNT * open_ * v_next - v
        carried = clipped * td + DISCOUNT * TRACE_LAMBDA * open_ * clipped * carried
        tg = jnp.where(lane == k, v + carried, tg)
        v_next = v
    tg_out[...] = tg[:, :steps]
    for k in range(steps):
        sT_out[:, k * rows : (k + 1) * rows] = s[k * rows : (k + 1) * rows, :].T


def weights_kernel(groups, devices, act, o, tg, ssq0, ssq1, ssq2, ssq3, a_out, b_out, mass_out):
    steps = act.shape[1]
    rows = act.shape[0]
    count = ACTIONS
    spread = ssq0[0:1, 0:1] + ssq1[0:1, 0:1] + ssq2[0:1, 0:1] + ssq3[0:1, 0:1]
    scale = jnp.sqrt(spread / (groups * rows * steps * count) + EPSILON)
    norm = 1.0 / (devices * rows * steps)
    mass_sum = jnp.zeros((1, 1), F32)
    for k in range(steps):
        valid, _, q, pi, _, v = policy_of(o[k * rows : (k + 1) * rows, :], count)
        oh = onehot_of(act, k)
        w = jnp.exp(jnp.clip((q - v) / scale, -1.0, 1.0))
        pw = pi * w
        mass = jnp.sum(pw, axis=1, keepdims=True)
        mass_sum = mass_sum + jnp.sum(mass, axis=0, keepdims=True)
        cmpo = pw / mass
        whole = jnp.sum(cmpo, axis=1, keepdims=True)
        taken = jnp.sum(jnp.where(oh, w, 0.0), axis=1, keepdims=True)
        dq = jnp.where(oh, q - tg[:, k : k + 1], 0.0)
        a = (pi * whole - cmpo) + pltpu.roll(dq, count, 1)
        b = taken * (pi - jnp.where(oh, 1.0, 0.0))
        a_out[k * rows : (k + 1) * rows, :] = a * norm
        b_out[k * rows : (k + 1) * rows, :] = b * norm
    mass_out[...] = jnp.broadcast_to(mass_sum, mass_out.shape)


def gradient_kernel(
    groups, core, act, a, b, m0, m1, m2, m3, s, sT, t, wh, whd, mine, other, whp, g, x, oh, e
):
    steps = act.shape[1]
    rows = act.shape[0]
    pad_lanes(whp, whd)
    total = m0[0:1, 0:1] + m1[0:1, 0:1] + m2[0:1, 0:1] + m3[0:1, 0:1]
    mean = total / (groups * rows * steps)
    g[...] = (a[...] + b[...] / mean).astype(BF16)
    last = steps - 1
    r = dot_nt(g[last * rows :, :], whp[...])
    for k in range(last - 1, -1, -1):
        here = slice(k * rows, (k + 1) * rows)
        tk = t[here, :]
        xk = (r * (1.0 - tk * tk)).astype(BF16)
        x[here, :] = xk
        oh[here, :] = onehot_of(act, k).astype(F32).astype(BF16)
        if k > 0:
            r = r + (dot_nt(xk, wh[...]) + dot_nt(g[here, :], whp[...]))
    inner = last * rows
    heads = dot_tn(g[...], s[...])
    taken = dot_tn(oh[...], x[...])
    e[0:40, :] = heads[0:40, :]
    e[40:64, :] = taken[0:24, :]
    hid = sT.shape[0]
    half = hid // 2
    units = mine.shape[0]
    which = core[0]
    for out, h in ((other, 1 - which), (mine, which)):
        at = pl.multiple_of(h * half, half)
        left = sT[pl.ds(at, half), :inner]
        for j in range(0, hid, 256):
            block = dot(left, x[:, j : j + 256])
            for c in range(2):
                n = j // LANES + c
                out[:, n * 32 : (n + 1) * 32, :] = block[:, c * LANES : (c + 1) * LANES].reshape(
                    units, 32, LANES
                )
        for i in range(4):
            rows8 = e[pl.ds(pl.multiple_of(h * 32 + i * 8, 8), 8), :]
            for n in range(8):
                at8 = 256 + (n % 2) * 8
                out[i * 4 + n // 2, at8 : at8 + 8, :] = rows8[:, n * LANES : (n + 1) * LANES]


def plane_sum_kernel(arrived, out):
    total = arrived[0]
    for i in range(1, arrived.shape[0]):
        total = total + arrived[i]
    out[...] = jnp.zeros_like(out)
    for n in range(8):
        out[n, 0:32, :] = total[n * 32 : (n + 1) * 32, :]
        out[n, 32:34, :] = total[256 + n * 2 : 258 + n * 2, :]


def line_sum_kernel(arrived, out):
    total = arrived[0]
    for i in range(1, arrived.shape[0]):
        total = total + arrived[i]
    for i in range(out.shape[0]):
        out[i] = total


def unpack_kernel(arrived, out, unit):
    for n in range(8):
        unit[n * 32 : (n + 1) * 32, :] = arrived[n, 0:32, :]
        unit[256 + n * 2 : 258 + n * 2, :] = arrived[n, 32:34, :]
    whole = unit[...]
    for i in range(out.shape[0]):
        out[i] = whole


def assemble_kernel(core, mine, other, gh, ga, gd, e):
    half = gh.shape[0] // 2
    which = core[0]
    for part, h in ((mine, which), (other, 1 - which)):
        at = pl.multiple_of(h * half, half)
        for n in range(8):
            gh[pl.ds(at, half), n * LANES : (n + 1) * LANES] = part[
                :, n * 32 : (n + 1) * 32, :
            ].reshape(half, LANES)
        for i in range(4):
            for n in range(8):
                at8 = 256 + (n % 2) * 8
                e[pl.ds(pl.multiple_of(h * 32 + i * 8, 8), 8), n * LANES : (n + 1) * LANES] = part[
                    i * 4 + n // 2, at8 : at8 + 8, :
                ]
    ga[...] = e[40 : 40 + ga.shape[0], :]
    gd[...] = e[0:40, :].T[:, : gd.shape[1]]


ACTIONS = 18


def shifted(array, axis, by):
    size = lax.axis_size(axis)
    return lax.ppermute(array, axis, [(i, (i + by) % size) for i in range(size)])


def of_group(part):
    return [part] + [shifted(part, "y", by) for by in (2, 1, 3)]


def swapped(tiles, axis):
    return lax.all_to_all(tiles, axis, split_axis=0, concat_axis=0, tiled=True)


def body(embed, actions, rewards, ends, behaviour, w_hidden, w_action, w_heads):
    rows, hid = embed.shape
    steps = actions.shape[1]
    groups = lax.axis_size("y")
    devices = lax.axis_size(ALL)
    core = lax.axis_index("core").astype(jnp.int32).reshape(1)

    wap = pltpu.VMEM((LANES, hid), BF16)
    whp = pltpu.VMEM((hid, LANES), BF16)
    s, t, state, out, ssq = kernel_call(
        unroll_kernel,
        [
            ((steps * rows, hid), BF16),
            (((steps - 1) * rows, hid), F32),
            ((rows, hid), F32),
            ((steps * rows, LANES), F32),
            ((8, LANES), F32),
        ],
        (embed, actions, w_hidden, w_action, w_heads),
        (wap, whp),
    )
    ssqs = of_group(ssq)
    beh = jnp.pad(
        jnp.transpose(behaviour, (1, 0, 2)), ((0, 0), (0, 0), (0, LANES - behaviour.shape[2]))
    ).reshape(steps * rows, LANES)
    targets, sT = kernel_call(
        targets_kernel,
        [((rows, steps), F32), ((hid, steps * rows), BF16)],
        (actions, rewards, ends, beh, w_hidden, w_action, w_heads, s, state, out),
        (wap, whp),
    )

    def weights_body(*refs):
        weights_kernel(groups, devices, *refs)

    a, b, mass = kernel_call(
        weights_body,
        [((steps * rows, LANES), F32), ((steps * rows, LANES), F32), ((8, LANES), F32)],
        (actions, out, targets, *ssqs),
    )
    masses = of_group(mass)

    def gradient_body(*refs):
        gradient_kernel(groups, *refs)

    unit = ((16, 272, LANES), F32)
    mine, other = kernel_call(
        gradient_body,
        [unit, unit],
        (core, actions, a, b, *masses, s, sT, t, w_hidden, w_heads),
        (
            whp,
            pltpu.VMEM((steps * rows, LANES), BF16),
            pltpu.VMEM(((steps - 1) * rows, hid), BF16),
            pltpu.VMEM(((steps - 1) * rows, LANES), BF16),
            pltpu.VMEM((64, hid), F32),
        ),
        scalars=1,
    )
    chip = mine + shifted(other, "core", 1)
    (line,) = kernel_call(plane_sum_kernel, [((8, 40, LANES), F32)], (swapped(chip, PLANE),))
    (total,) = kernel_call(line_sum_kernel, [((8, 40, LANES), F32)], (swapped(line, "z"),))
    (plane,) = kernel_call(
        unpack_kernel, [unit], (swapped(total, "z"),), (pltpu.VMEM((272, LANES), F32),)
    )
    mine = swapped(plane, PLANE)
    other = shifted(mine, "core", 1)
    grad_hidden, grad_action, grad_heads = kernel_call(
        assemble_kernel,
        [((hid, hid), F32), (w_action.shape, F32), (w_heads.shape, F32)],
        (core, mine, other),
        (pltpu.VMEM((64, hid), F32),),
        scalars=1,
    )
    return (grad_hidden, grad_action, grad_heads, targets)


def solution(mesh):
    torus = Mesh(mesh.devices.reshape(8, 4, 2, mesh.shape["batch"]), ALL)
    return jax.shard_map(
        body,
        mesh=torus,
        in_specs=(
            P(ALL, None),
            P(ALL, None),
            P(ALL, None),
            P(ALL, None),
            P(ALL, None, None),
            P(),
            P(),
            P(),
        ),
        out_specs=(P(), P(), P(), P(ALL, None)),
        check_vma=False,
    )
```

time: 281 us -> 157 us (0.56)
  blocking collectives: 172 us -> 89.9 us
  matrix products: 39.6 us -> 0 us
  local copies, waits for them, and re-layouts: 46.3 us -> 13.8 us
  Pallas kernels: 0 us -> 22.8 us
  other arithmetic: 14.3 us -> 1.85 us
  starting transfers between devices: 5 us -> 17.1 us
  waiting for transfers between devices: 0.01 us -> 9.8 us
    all_to_all x5 -> x4, blocking collectives: 172 us -> 89.9 us  [swapped(): return lax.all_to_all(tiles, axis, split_axis=0, concat_axis=0, tiled=True)]
    dot_general x39 -> x0, matrix products: 39.6 us -> none  [the longest x5 18.7 us: backward(): jnp.dot(rounded[step].T, grad_pre, preferred_element_type=jnp.float32)]
    pallas_call x0 -> x8, Pallas kernels: none -> 22.8 us  [kernel_call(): pl.pallas_call(body, out_shape=tuple((jax.ShapeDtypeStruct(s, d) for s, d...]
    ppermute x0 -> x8, starting transfers between devices: none -> 17.1 us  [shifted(): lax.ppermute(array, axis, [(i, (i + by) % size) for i in range(size)])]
    slice x6 -> x0, local copies, waits for them, and re-layouts: 13.7 us -> none  [together(): subtotal[b:e].reshape(a.shape)]
    another operation x3 -> x0, local copies, waits for them, and re-layouts: 13.5 us -> none  [the longest x1 6.86 us: laid_out(): tiles.reshape(*shape[:dim], shape[dim] * shape[dim + 1], *shape[dim + 2:])]
    unnamed x54 -> x35, local copies, waits for them, and re-layouts: 2.95 us -> 13.7 us
    ppermute x0 -> x8, waiting for transfers between devices: none -> 9.8 us  [shifted(): lax.ppermute(array, axis, [(i, (i + by) % size) for i in range(size)])]
  transfers between devices with their start and end apart: 1 -> 8, of which waited for: 0 -> 4; matrix products, arithmetic and copies ran while one was open for 2% -> 1% of each run, Pallas kernels for 0% -> 3%
where the time goes in v1:
time: 157 us; the launch traced here: 156 us
  blocking collectives  89.9 us (57%)
  Pallas kernels  22.8 us (15%)
  starting transfers between devices  17.1 us (11%)
  local copies, waits for them, and re-layouts  13.8 us (9%)
  waiting for transfers between devices  9.8 us (6%)
  other arithmetic  1.85 us (1%)
    all_to_all x4, blocking collectives, swapped(): return lax.all_to_all(tiles, axis, split_axis=0, concat_axis=0, tiled=True)  89.9 us
    pallas_call x8, Pallas kernels, kernel_call(): pl.pallas_call(body, out_shape=tuple((jax.ShapeDtypeStruct(s, d) for s, d...  22.8 us
    ppermute x8, starting transfers between devices, shifted(): lax.ppermute(array, axis, [(i, (i + by) % size) for i in range(size)])  17.1 us
    unnamed x35, local copies, waits for them, and re-layouts  13.7 us
    ppermute x8, waiting for transfers between devices, shifted(): lax.ppermute(array, axis, [(i, (i + by) % size) for i in range(size)])  9.8 us
  transfers between devices with their start and end apart: 8, of which 4 were waited for; matrix products, arithmetic and copies ran while one was open for 1% of the time, Pallas kernels for 3%

profile of v1, /device:TPU:1, one launch (start us, length us, event | category | flops | bytes accessed | tf_op | source)
XLA Modules:
  0.0 156.0 jit_solution(5217476894432577117)
XLA Ops:
  0.7 0.8 copy.20.act.refs_0_.refs_1_
  1.5 1.1 copy.13.whd.refs_12_
  2.6 0.9 copy-done.8
  3.5 0.8 copy-done.9
  4.3 4.8 %unroll_kernel.1 = (bf16[640,1024]{1,0:T(8,128)(2,1)S(1)}, f32[512,1024]{1,0:T(8,128)S(1)}, f32[128,1024]{1,0:T(8,128)S(1)}, f32[640,128]{1,0:T(8,128)S(1)}, f32[8,128]{1,0:T(8,128)S(1)}) custom-call(bf16[128,1024]{1,0:T(8,128)(2,1)S(1)} %copy-done.8, s32[128,5]{1,0:T(8,128)S(1)} %copy.20.act.refs_0_.refs_1_, bf16[1024,1024]{1,0:T(8,128)(2,1)} %refs_11_.1, ...), custom_call_target="tpu_custom_call" | custom-call | tf_op jit(solution)/shard_map/unroll_kernel/pallas_call | solution.py:37
  9.1 1.3 copy-done
  10.4 0.8 copy-done.2
  11.2 3.6 %collective-permute-start.2 = (f32[8,128]{1,0:T(8,128)S(1)}, f32[8,128]{1,0:T(8,128)S(1)}, u32[]{:S(2)}, u32[]{:S(2)}) collective-permute-start(f32[8,128]{1,0:T(8,128)S(1)} %get-tuple-element.23.refs_3_), channel_id=1, source_target_pairs={{0,3},{1,0},{2,1},{3,2},{4,7},{5,4},{6,5},{7,6},{8,11},{9,8},{10,9... | collective-permute-start | bytes 12296 | tf_op jit(solution)/shard_map/ppermute | solution.py:255
  14.8 1.6 %collective-permute-start = (f32[8,128]{1,0:T(8,128)S(1)}, f32[8,128]{1,0:T(8,128)S(1)}, u32[]{:S(2)}, u32[]{:S(2)}) collective-permute-start(f32[8,128]{1,0:T(8,128)S(1)} %get-tuple-element.23.refs_3_), channel_id=1, source_target_pairs={{0,2},{1,3},{2,0},{3,1},{4,6},{5,7},{6,4},{7,5},{8,10},{9,11},{10,... | collective-permute-start | bytes 12296 | tf_op jit(solution)/shard_map/ppermute | solution.py:255
  16.9 1.0 copy-done.3
  18.0 3.9 %targets_kernel.1 = (f32[128,5]{1,0:T(8,128)S(1)}, bf16[1024,640]{1,0:T(8,128)(2,1)S(1)}) custom-call(s32[128,5]{1,0:T(8,128)S(1)} %copy.20.act.refs_0_.refs_1_, f32[128,5]{1,0:T(8,128)S(1)} %copy.16.rew, s32[128,5]{1,0:T(8,128)S(1)} %copy.17.ends, f32[640,128]{1,0:T(8,128)S(1)} %bitcast.3, bf16[1024,1024]{1,0:T(8,128)(2,1)} %refs_11_.1, ...), custom_call_target="tpu_custom_call" | custom-call | tf_op jit(solution)/shard_map/targets_kernel/pallas_call | solution.py:37
  22.0 2.3 %weights_body.1 = (f32[640,128]{1,0:T(8,128)S(1)}, f32[640,128]{1,0:T(8,128)S(1)}, f32[8,128]{1,0:T(8,128)S(1)}) custom-call(s32[128,5]{1,0:T(8,128)S(1)} %copy.20.act.refs_0_.refs_1_, f32[640,128]{1,0:T(8,128)S(1)} %get-tuple-element.19.o.refs_1_, f32[128,5]{1,0:T(8,128)S(1)} %get-tuple-element.37.refs_2_, f32[8,128]{1,0:T(8,128)S(1)} %get-tuple-element.23.refs_3_, ...), custom_call_target="tpu_custom_call" | custom-call | tf_op jit(solution)/shard_map/weights_body/pallas_call | solution.py:37
  24.3 0.7 copy-done.4
  25.7 1.0 collective-permute-start.5
  27.3 1.8 %collective-permute-start.3 = (f32[8,128]{1,0:T(8,128)S(1)}, f32[8,128]{1,0:T(8,128)S(1)}, u32[]{:S(2)}, u32[]{:S(2)}) collective-permute-start(f32[8,128]{1,0:T(8,128)S(1)} %get-tuple-element.26.refs_4_), channel_id=1, source_target_pairs={{0,2},{1,3},{2,0},{3,1},{4,6},{5,7},{6,4},{7,5},{8,10},{9,11},{10,... | collective-permute-start | bytes 12296 | tf_op jit(solution)/shard_map/ppermute | solution.py:255
  29.1 1.3 collective-permute-done.4.refs_6_
  30.4 0.9 collective-permute-done.3.refs_5_
  31.3 1.6 %copy-done.1 = f32[512,1024]{1,0:T(8,128)S(1)} copy-done((f32[512,1024]{1,0:T(8,128)S(1)}, f32[512,1024]{1,0:T(8,128)}, u32[]{:S(2)}) %copy-start.1) | copy-done | bytes 2097176
  32.9 1.0 copy-done.5
  33.9 1.0 copy-done.7
  34.8 7.2 %gradient_body.1 = (f32[16,272,128]{2,1,0:T(8,128)}, f32[16,272,128]{2,1,0:T(8,128)}) custom-call(s32[1]{0:T(128)} %bitcast.refs_0_.core, s32[128,5]{1,0:T(8,128)S(1)} %copy.20.act.refs_0_.refs_1_, f32[640,128]{1,0:T(8,128)S(1)} %copy-done.5, f32[640,128]{1,0:T(8,128)S(1)} %copy-done.7, f32[8,128]{1,0:T(8,128)S(1)} %get-tuple-element.26.refs_4_, ...), custom_call_target="tpu_custom_call" | custom-call | tf_op jit(solution)/shard_map/gradient_body/pallas_call | solution.py:37
  42.0 3.0 %collective-permute-start.6 = (f32[16,272,128]{2,1,0:T(8,128)}, f32[16,272,128]{2,1,0:T(8,128)S(1)}, u32[]{:S(2)}, u32[]{:S(2)}) collective-permute-start(f32[16,272,128]{2,1,0:T(8,128)} %get-tuple-element.30), channel_id=1, source_target_pairs={{0,4},{4,0},{1,5},{5,1},{2,6},{6,2},{3,7},{7,3},{8,12},{12,8},{9,1... | collective-permute-start | bytes 6684680 | tf_op jit(solution)/shard_map/ppermute | solution.py:255
  45.1 4.2 %collective-permute-done.6 = f32[16,272,128]{2,1,0:T(8,128)S(1)} collective-permute-done((f32[16,272,128]{2,1,0:T(8,128)}, f32[16,272,128]{2,1,0:T(8,128)S(1)}, u32[]{:S(2)}, u32[]{:S(2)}) %collective-permute-start.6) | collective-permute-done | bytes 2228256 | tf_op jit(solution)/shard_map/ppermute | solution.py:255
  49.3 1.9 %add.5 = f32[16,272,128]{2,1,0:T(8,128)S(1)} add(f32[16,272,128]{2,1,0:T(8,128)} %get-tuple-element.29, f32[16,272,128]{2,1,0:T(8,128)S(1)} %collective-permute-done.6) | non-fusion elementwise | flops 557056 | bytes 6684672 | tf_op jit(solution)/shard_map/add | solution.py:325
  51.1 34.5 %all_to_all.20.arrived = f32[16,272,128]{2,1,0:T(8,128)S(1)} all-to-all(f32[16,272,128]{2,1,0:T(8,128)S(1)} %add.5), channel_id=1, replica_groups=mesh['z'=8,'x'=4,'core'=2,'y'=4] {'x','y'}, dimensions={0} | all-to-all | bytes 4456448 | tf_op jit(solution)/shard_map/all_to_all | solution.py:263
  85.7 16.3 %all_to_all.21.arrived = f32[8,40,128]{2,1,0:T(8,128)S(1)} all-to-all(f32[8,40,128]{2,1,0:T(8,128)S(1)} %plane_sum_kernel.1), channel_id=1, replica_groups=mesh['z'=8,'x'=4,'core'=2,'y'=4] {'z'}, dimensions={0} | all-to-all | bytes 327680 | tf_op jit(solution)/shard_map/all_to_all | solution.py:263
  102.0 10.7 %all_to_all.22.arrived = f32[8,40,128]{2,1,0:T(8,128)S(1)} all-to-all(f32[8,40,128]{2,1,0:T(8,128)S(1)} %line_sum_kernel.1), channel_id=1, replica_groups=mesh['z'=8,'x'=4,'core'=2,'y'=4] {'z'}, dimensions={0} | all-to-all | bytes 327680 | tf_op jit(solution)/shard_map/all_to_all | solution.py:263
  112.9 28.5 %all_to_all.23.mine = f32[16,272,128]{2,1,0:T(8,128)S(1)} all-to-all(f32[16,272,128]{2,1,0:T(8,128)S(1)} %unpack_kernel.1), channel_id=1, replica_groups=mesh['z'=8,'x'=4,'core'=2,'y'=4] {'x','y'}, dimensions={0} | all-to-all | bytes 4456448 | tf_op jit(solution)/shard_map/all_to_all | solution.py:263
  141.3 5.4 %collective-permute-start.7 = (f32[16,272,128]{2,1,0:T(8,128)S(1)}, f32[16,272,128]{2,1,0:T(8,128)}, u32[]{:S(2)}, u32[]{:S(2)}) collective-permute-start(f32[16,272,128]{2,1,0:T(8,128)S(1)} %all_to_all.23.mine), channel_id=1, source_target_pairs={{0,4},{4,0},{1,5},{5,1},{2,6},{6,2},{3,7},{7,3},{8,12},{12,8},{9,1... | collective-permute-start | bytes 6684680 | tf_op jit(solution)/shard_map/ppermute | solution.py:255
  147.4 3.4 %collective-permute-done.7.other = f32[16,272,128]{2,1,0:T(8,128)} collective-permute-done((f32[16,272,128]{2,1,0:T(8,128)S(1)}, f32[16,272,128]{2,1,0:T(8,128)}, u32[]{:S(2)}, u32[]{:S(2)}) %collective-permute-start.7) | collective-permute-done | bytes 2228256 | tf_op jit(solution)/shard_map/ppermute | solution.py:255
  150.9 4.3 %assemble_kernel.1 = (f32[1024,1024]{1,0:T(8,128)}, f32[18,1024]{1,0:T(8,128)}, f32[1024,36]{1,0:T(8,128)S(1)}) custom-call(s32[1]{0:T(128)} %bitcast.refs_0_.core, f32[16,272,128]{2,1,0:T(8,128)S(1)} %all_to_all.23.mine, f32[16,272,128]{2,1,0:T(8,128)} %collective-permute-done.7.other), custom_call_target="tpu_custom_call" | custom-call | tf_op jit(solution)/shard_map/assemble_kernel/pallas_call | solution.py:37
  155.1 0.9 copy.22
  (33 shorter events, 2.7 us)
Async XLA Ops:
  0.6 16.3 %copy-start.10 = (bf16[18,1024]{1,0:T(8,128)(2,1)S(1)}, bf16[18,1024]{1,0:T(8,128)(2,1)}, u32[]{:S(2)}) copy-start(bf16[18,1024]{1,0:T(8,128)(2,1)} %wa.3) | copy-start | bytes 110596
  0.6 15.8 %copy-start.12 = (f32[128,5]{0,1:T(8,128)S(1)}, f32[128,5]{0,1:T(8,128)}, u32[]{:S(2)}) copy-start(f32[128,5]{0,1:T(8,128)} %param.10) | copy-start | bytes 7684
  0.7 15.9 %copy-start.13 = (s32[128,5]{0,1:T(8,128)S(1)}, s32[128,5]{0,1:T(8,128)}, u32[]{:S(2)}) copy-start(s32[128,5]{0,1:T(8,128)} %param.11) | copy-start | bytes 7684
  0.7 16.0 %copy-start.11 = (f32[128,5,18]{0,2,1:T(8,128)S(1)}, f32[128,5,18]{0,2,1:T(8,128)}, u32[]{:S(2)}) copy-start(f32[128,5,18]{0,2,1:T(8,128)} %param.12) | copy-start | bytes 138244
  2.6 1.0 copy-start.8
  3.5 0.8 copy-start.9
  9.1 1.3 copy-start
  10.4 0.8 copy-start.2
  11.2 10.7 %collective-permute-start.2 = (f32[8,128]{1,0:T(8,128)S(1)}, f32[8,128]{1,0:T(8,128)S(1)}, u32[]{:S(2)}, u32[]{:S(2)}) collective-permute-start(f32[8,128]{1,0:T(8,128)S(1)} %get-tuple-element.23.refs_3_), channel_id=1, source_target_pairs={{0,3},{1,0},{2,1},{3,2},{4,7},{5,4},{6,5},{7,6},{8,11},{9,8},{10,9... | collective-permute-start | bytes 12296 | tf_op jit(solution)/shard_map/ppermute | solution.py:255
  14.8 7.1 %collective-permute-start.1 = (f32[8,128]{1,0:T(8,128)S(1)}, f32[8,128]{1,0:T(8,128)S(1)}, u32[]{:S(2)}, u32[]{:S(2)}) collective-permute-start(f32[8,128]{1,0:T(8,128)S(1)} %get-tuple-element.23.refs_3_), channel_id=1, source_target_pairs={{0,1},{1,2},{2,3},{3,0},{4,5},{5,6},{6,7},{7,4},{8,9},{9,10},{10,1... | collective-permute-start | bytes 12296 | tf_op jit(solution)/shard_map/ppermute | solution.py:255
  14.8 7.1 %collective-permute-start = (f32[8,128]{1,0:T(8,128)S(1)}, f32[8,128]{1,0:T(8,128)S(1)}, u32[]{:S(2)}, u32[]{:S(2)}) collective-permute-start(f32[8,128]{1,0:T(8,128)S(1)} %get-tuple-element.23.refs_3_), channel_id=1, source_target_pairs={{0,2},{1,3},{2,0},{3,1},{4,6},{5,7},{6,4},{7,5},{8,10},{9,11},{10,... | collective-permute-start | bytes 12296 | tf_op jit(solution)/shard_map/ppermute | solution.py:255
  16.9 1.0 copy-start.3
  24.3 0.7 copy-start.4
  25.0 0.7 copy-start.6
  25.7 3.4 %collective-permute-start.5 = (f32[8,128]{1,0:T(8,128)S(1)}, f32[8,128]{1,0:T(8,128)S(1)}, u32[]{:S(2)}, u32[]{:S(2)}) collective-permute-start(f32[8,128]{1,0:T(8,128)S(1)} %get-tuple-element.26.refs_4_), channel_id=1, source_target_pairs={{0,3},{1,0},{2,1},{3,2},{4,7},{5,4},{6,5},{7,6},{8,11},{9,8},{10,9... | collective-permute-start | bytes 12296 | tf_op jit(solution)/shard_map/ppermute | solution.py:255
  26.8 3.7 %collective-permute-start.4 = (f32[8,128]{1,0:T(8,128)S(1)}, f32[8,128]{1,0:T(8,128)S(1)}, u32[]{:S(2)}, u32[]{:S(2)}) collective-permute-start(f32[8,128]{1,0:T(8,128)S(1)} %get-tuple-element.26.refs_4_), channel_id=1, source_target_pairs={{0,1},{1,2},{2,3},{3,0},{4,5},{5,6},{6,7},{7,4},{8,9},{9,10},{10,1... | collective-permute-start | bytes 12296 | tf_op jit(solution)/shard_map/ppermute | solution.py:255
  27.3 4.0 %collective-permute-start.3 = (f32[8,128]{1,0:T(8,128)S(1)}, f32[8,128]{1,0:T(8,128)S(1)}, u32[]{:S(2)}, u32[]{:S(2)}) collective-permute-start(f32[8,128]{1,0:T(8,128)S(1)} %get-tuple-element.26.refs_4_), channel_id=1, source_target_pairs={{0,2},{1,3},{2,0},{3,1},{4,6},{5,7},{6,4},{7,5},{8,10},{9,11},{10,... | collective-permute-start | bytes 12296 | tf_op jit(solution)/shard_map/ppermute | solution.py:255
  31.3 1.6 %copy-start.1 = (f32[512,1024]{1,0:T(8,128)S(1)}, f32[512,1024]{1,0:T(8,128)}, u32[]{:S(2)}) copy-start(f32[512,1024]{1,0:T(8,128)} %copy-done) | copy-start | bytes 6291460
  32.9 1.0 copy-start.5
  33.9 1.0 copy-start.7
  42.0 7.2 %collective-permute-start.6 = (f32[16,272,128]{2,1,0:T(8,128)}, f32[16,272,128]{2,1,0:T(8,128)S(1)}, u32[]{:S(2)}, u32[]{:S(2)}) collective-permute-start(f32[16,272,128]{2,1,0:T(8,128)} %get-tuple-element.30), channel_id=1, source_target_pairs={{0,4},{4,0},{1,5},{5,1},{2,6},{6,2},{3,7},{7,3},{8,12},{12,8},{9,1... | collective-permute-start | bytes 6684680 | tf_op jit(solution)/shard_map/ppermute | solution.py:255
  141.3 9.5 %collective-permute-start.7 = (f32[16,272,128]{2,1,0:T(8,128)S(1)}, f32[16,272,128]{2,1,0:T(8,128)}, u32[]{:S(2)}, u32[]{:S(2)}) collective-permute-start(f32[16,272,128]{2,1,0:T(8,128)S(1)} %all_to_all.23.mine), channel_id=1, source_target_pairs={{0,4},{4,0},{1,5},{5,1},{2,6},{6,2},{3,7},{7,3},{8,12},{12,8},{9,1... | collective-permute-start | bytes 6684680 | tf_op jit(solution)/shard_map/ppermute | solution.py:255

commit v2 on v1

v2 whole, which is shorter than its diff:
```python
import jax
import jax.numpy as jnp
from jax import lax
from jax.experimental import pallas as pl
from jax.experimental.pallas import tpu as pltpu
from jax.sharding import Mesh
from jax.sharding import PartitionSpec as P

ALL = ("zh", "zp", "x", "core", "y")
NEAR = ("zp", "x", "y")
LINE = ("zh", "zp")

DISCOUNT = 0.997
TRACE_LAMBDA = 0.95
EPSILON = 1e-06

LANES = 128
Q_ROW = 24
A_ROW = 40
F32 = jnp.float32
BF16 = jnp.bfloat16

VMEM = pl.BlockSpec(memory_space=pltpu.VMEM)
SMEM = pl.BlockSpec(memory_space=pltpu.SMEM)


def dot(a, b):
    return jnp.dot(a, b, preferred_element_type=F32)


def dot_nt(a, b):
    return lax.dot_general(a, b, (((1,), (1,)), ((), ())), preferred_element_type=F32)


def dot_tn(a, b):
    return lax.dot_general(a, b, (((0,), (0,)), ((), ())), preferred_element_type=F32)


def kernel_call(body, outs, inputs, scratch=(), scalars=0):
    return pl.pallas_call(
        body,
        out_shape=tuple(jax.ShapeDtypeStruct(s, d) for s, d in outs),
        in_specs=[SMEM] * scalars + [VMEM] * (len(inputs) - scalars),
        out_specs=tuple(VMEM for _ in outs),
        scratch_shapes=list(scratch),
        name=body.__name__,
        compiler_params=pltpu.CompilerParams(vmem_limit_bytes=12 * 1024 * 1024),
    )(*inputs)


def chosen(act, step, count):
    columns = act.shape[1]
    return lax.broadcasted_iota(jnp.int32, (count, columns), 0) == act[step : step + 1, :]


def onehot_of(act, step):
    return chosen(act, step, 32).astype(F32).astype(BF16)


def policy_of(out, at, count):
    logits = out[0:count, at]
    q = out[Q_ROW : Q_ROW + count, at]
    e = jnp.exp(logits)
    total = jnp.sum(e, axis=0, keepdims=True)
    pi = e / total
    v = jnp.sum(pi * q, axis=0, keepdims=True)
    return logits, q, pi, total, v


def unroll_kernel(emb, act, wh, wa, whd, s_out, t_out, st_out, o_out, ssq_out, wap, whp, wide, rows40):
    count = wa.shape[0]
    steps = act.shape[0]
    rows = emb.shape[0]
    wap[...] = jnp.zeros_like(wap)
    wap[:count, :] = wa[...]
    rows40[0 : 2 * count, :] = whd[...].astype(F32)
    wide[...] = jnp.zeros_like(wide)
    wide[0:count, :] = rows40[0:count, :]
    wide[Q_ROW : Q_ROW + count, :] = rows40[count : 2 * count, :]
    whp[...] = wide[...].astype(BF16)
    state = emb[...].astype(F32)
    for k in range(steps):
        s = state.astype(BF16)
        s_out[k * rows : (k + 1) * rows, :] = s
        if k < steps - 1:
            t = jnp.tanh(dot(s, wh[...]) + dot_tn(onehot_of(act, k), wap[...]))
            t_out[k * rows : (k + 1) * rows, :] = t
            state = state + t
    st_out[...] = state
    o_out[...] = dot_nt(whp[...], s_out[...])
    _, q, _, _, v = policy_of(o_out, slice(None), count)
    adv = q - v
    part = jnp.sum(jnp.sum(adv * adv, axis=1, keepdims=True), axis=0, keepdims=True)
    ssq_out[...] = jnp.broadcast_to(part, ssq_out.shape)


def targets_kernel(act, rew, ends, beh, wh, wap, whp, s, st, o, tg_out, sT_out, last_out):
    steps = act.shape[0]
    rows = st.shape[0]
    count = beh.shape[1]
    last = steps - 1
    t = jnp.tanh(dot(s[last * rows :, :], wh[...]) + dot_tn(onehot_of(act, last), wap[...]))
    last_out[...] = dot_nt(whp[...], (st[...] + t).astype(BF16))
    v_next = policy_of(last_out, slice(None), count)[-1]
    carried = jnp.zeros((1, rows), F32)
    for k in range(last, -1, -1):
        logits, _, _, total, v = policy_of(o, slice(k * rows, (k + 1) * rows), count)
        b = beh[k]
        b_total = jnp.sum(jnp.exp(b), axis=0, keepdims=True)
        gap = (logits - jnp.log(total)) - (b - jnp.log(b_total))
        ratio = jnp.exp(jnp.sum(jnp.where(chosen(act, k, count), gap, 0.0), axis=0, keepdims=True))
        clipped = jnp.minimum(1.0, ratio)
        open_ = 1.0 - ends[k : k + 1, :].astype(F32)
        td = rew[k : k + 1, :] + DISCOUNT * open_ * v_next - v
        carried = clipped * td + DISCOUNT * TRACE_LAMBDA * open_ * clipped * carried
        tg_out[k : k + 1, :] = v + carried
        v_next = v
    for k in range(steps):
        sT_out[:, k * rows : (k + 1) * rows] = s[k * rows : (k + 1) * rows, :].T


def weights_kernel(groups, devices, count, act, o, tg, ssq0, ssq1, ssq2, ssq3, a_out, b_out, mass_out):
    steps, rows = act.shape
    spread = ssq0[0:1, 0:1] + ssq1[0:1, 0:1] + ssq2[0:1, 0:1] + ssq3[0:1, 0:1]
    scale = jnp.sqrt(spread / (groups * rows * steps * count) + EPSILON)
    norm = 1.0 / (devices * rows * steps)
    mass_sum = jnp.zeros((1, rows), F32)
    a_out[...] = jnp.zeros_like(a_out)
    b_out[...] = jnp.zeros_like(b_out)
    for k in range(steps):
        at = slice(k * rows, (k + 1) * rows)
        _, q, pi, _, v = policy_of(o, at, count)
        oh = chosen(act, k, count)
        w = jnp.exp(jnp.clip((q - v) / scale, -1.0, 1.0))
        pw = pi * w
        mass = jnp.sum(pw, axis=0, keepdims=True)
        mass_sum = mass_sum + mass
        cmpo = pw / mass
        whole = jnp.sum(cmpo, axis=0, keepdims=True)
        taken = jnp.sum(jnp.where(oh, w, 0.0), axis=0, keepdims=True)
        a_out[0:count, at] = (pi * whole - cmpo) * norm
        a_out[Q_ROW : Q_ROW + count, at] = jnp.where(oh, q - tg[k : k + 1, :], 0.0) * norm
        b_out[0:count, at] = taken * (pi - jnp.where(oh, 1.0, 0.0)) * norm
    mass_out[...] = jnp.broadcast_to(jnp.sum(mass_sum, axis=1, keepdims=True), mass_out.shape)


def gradient_kernel(
    groups, count, place, act, a, b, m0, m1, m2, m3, s, sT, t, wh, whp, mine, other, gf, g, x, oh, e
):
    steps, rows = act.shape
    total = m0[0:1, 0:1] + m1[0:1, 0:1] + m2[0:1, 0:1] + m3[0:1, 0:1]
    mean = total / (groups * rows * steps)
    gf[...] = a[...]
    gf[0:Q_ROW, :] = a[0:Q_ROW, :] + b[...] / mean
    g[...] = gf[...].astype(BF16)
    last = steps - 1
    r = dot_tn(g[:, last * rows :], whp[...])
    for k in range(last - 1, -1, -1):
        here = slice(k * rows, (k + 1) * rows)
        tk = t[here, :]
        xk = (r * (1.0 - tk * tk)).astype(BF16)
        x[here, :] = xk
        oh[:, here] = onehot_of(act, k)
        if k > 0:
            r = r + (dot_nt(xk, wh[...]) + dot_tn(g[:, here], whp[...]))
    inner = last * rows
    e[...] = jnp.zeros_like(e)
    heads = dot(g[...], s[...])
    e[0:count, :] = heads[0:count, :]
    e[count : 2 * count, :] = heads[Q_ROW : Q_ROW + count, :]
    e[A_ROW : A_ROW + count, :] = dot(oh[...], x[...])[0:count, :]
    hid = sT.shape[0]
    half = hid // 2
    core, flip = place[0], place[1]
    for out, h in ((other, 1 - core), (mine, core)):
        left = sT[pl.ds(pl.multiple_of(h * half, half), half), :inner]
        for j in range(0, hid, 256):
            block = dot(left, x[:, j : j + 256])
            for p in range(2):
                slot = pl.ds((flip + p - 2 * flip * p) * 16, 16)
                for c in range(2):
                    n = j // LANES + c
                    out[slot, n * 16 : (n + 1) * 16, :] = block[
                        p * 256 : (p + 1) * 256, c * LANES : (c + 1) * LANES
                    ].reshape(16, 16, LANES)
        for i in range(4):
            p = i // 2
            slot = (flip + p - 2 * flip * p) * 16 + (i % 2) * 8
            rows8 = e[pl.ds(pl.multiple_of(h * 32 + i * 8, 8), 8), :]
            for n in range(8):
                out[slot + n, 128:136, :] = rows8[:, n * LANES : (n + 1) * LANES]


def plane_sum_kernel(arrived, out):
    total = arrived[0]
    for i in range(1, arrived.shape[0]):
        total = total + arrived[i]
    out[...] = total


def line_sum_kernel(own, near, far, both, out):
    total = (own[...] + near[...]) + (far[...] + both[...])
    for i in range(out.shape[0]):
        out[i] = total


def assemble_kernel(place, mine, other, gh, ga, gd, e):
    half = gh.shape[0] // 2
    core, flip = place[0], place[1]
    for part, h in ((mine, core), (other, 1 - core)):
        for p in range(2):
            slot = pl.ds((flip + p - 2 * flip * p) * 16, 16)
            at = pl.ds(pl.multiple_of(h * half + p * 256, 256), 256)
            for n in range(8):
                gh[at, n * LANES : (n + 1) * LANES] = part[
                    slot, n * 16 : (n + 1) * 16, :
                ].reshape(256, LANES)
        for i in range(4):
            p = i // 2
            slot = (flip + p - 2 * flip * p) * 16 + (i % 2) * 8
            at8 = pl.ds(pl.multiple_of(h * 32 + i * 8, 8), 8)
            for n in range(8):
                e[at8, n * LANES : (n + 1) * LANES] = part[slot + n, 128:136, :]
    ga[...] = e[A_ROW : A_ROW + ga.shape[0], :]
    gd[...] = e[0 : gd.shape[0], :]


def shifted(array, axis, by):
    size = lax.axis_size(axis)
    return lax.ppermute(array, axis, [(i, (i + by) % size) for i in range(size)])


def of_group(part):
    return [part] + [shifted(part, "y", by) for by in (2, 1, 3)]


def swapped(tiles, axis):
    return lax.all_to_all(tiles, axis, split_axis=0, concat_axis=0, tiled=True)


def along_z(array, to):
    return lax.ppermute(array, LINE, [(z, to(z)) for z in range(8)])


def beside(z):
    return (z + 1 if z % 2 else z - 1) % 8


def across(z):
    return (z + 4) % 8


def body(embed, actions, rewards, ends, behaviour, w_hidden, w_action, w_heads):
    rows, hid = embed.shape
    steps = actions.shape[1]
    count = w_action.shape[0]
    groups = lax.axis_size("y")
    devices = lax.axis_size(ALL)
    place = jnp.stack([lax.axis_index("core"), lax.axis_index("zh") % 2]).astype(jnp.int32)
    act = actions.T

    s, t, state, out, ssq, wap, whp = kernel_call(
        unroll_kernel,
        [
            ((steps * rows, hid), BF16),
            (((steps - 1) * rows, hid), F32),
            ((rows, hid), F32),
            ((48, steps * rows), F32),
            ((8, LANES), F32),
            ((32, hid), BF16),
            ((48, hid), BF16),
        ],
        (embed, act, w_hidden, w_action, w_heads.T),
        (pltpu.VMEM((48, hid), F32), pltpu.VMEM((40, hid), F32)),
    )
    ssqs = of_group(ssq)
    targets, sT = kernel_call(
        targets_kernel,
        [((steps, rows), F32), ((hid, steps * rows), BF16)],
        (
            act,
            rewards.T,
            ends.T,
            jnp.transpose(behaviour, (1, 2, 0)),
            w_hidden,
            wap,
            whp,
            s,
            state,
            out,
        ),
        (pltpu.VMEM((48, rows), F32),),
    )

    def weights_body(*refs):
        weights_kernel(groups, devices, count, *refs)

    a, b, mass = kernel_call(
        weights_body,
        [((48, steps * rows), F32), ((Q_ROW, steps * rows), F32), ((8, LANES), F32)],
        (act, out, targets, *ssqs),
    )
    masses = of_group(mass)

    def gradient_body(*refs):
        gradient_kernel(groups, count, *refs)

    parts = ((32, 136, LANES), F32)
    mine, other = kernel_call(
        gradient_body,
        [parts, parts],
        (place, act, a, b, *masses, s, sT, t, w_hidden, whp),
        (
            pltpu.VMEM((48, steps * rows), F32),
            pltpu.VMEM((48, steps * rows), BF16),
            pltpu.VMEM(((steps - 1) * rows, hid), BF16),
            pltpu.VMEM((32, (steps - 1) * rows), BF16),
            pltpu.VMEM((64, hid), F32),
        ),
        scalars=1,
    )
    chip = mine + shifted(other, "core", 1)
    (own,) = kernel_call(plane_sum_kernel, [((136, LANES), F32)], (swapped(chip, NEAR),))
    far = along_z(own, across)
    both = along_z(own, lambda z: across(beside(z)))
    near = along_z(own, beside)
    (whole,) = kernel_call(line_sum_kernel, [parts], (own, near, far, both))
    mine = swapped(whole, NEAR)
    other = shifted(mine, "core", 1)
    grad_hidden, grad_action, grad_heads = kernel_call(
        assemble_kernel,
        [((hid, hid), F32), (w_action.shape, F32), (w_heads.shape[::-1], F32)],
        (place, mine, other),
        (pltpu.VMEM((64, hid), F32),),
        scalars=1,
    )
    return (grad_hidden, grad_action, grad_heads.T, targets.T)


def solution(mesh):
    torus = Mesh(mesh.devices.reshape(4, 2, 4, 2, mesh.shape["batch"]), ALL)
    return jax.shard_map(
        body,
        mesh=torus,
        in_specs=(
            P(ALL, None),
            P(ALL, None),
            P(ALL, None),
            P(ALL, None),
            P(ALL, None, None),
            P(),
            P(),
            P(),
        ),
        out_specs=(P(), P(), P(), P(ALL, None)),
        check_vma=False,
    )
```

time: 157 us -> 134 us (0.85)
  blocking collectives: 89.9 us -> 66.3 us
  Pallas kernels: 22.8 us -> 12 us
  starting transfers between devices: 17.1 us -> 24.8 us
  waiting for transfers between devices: 9.8 us -> 15.6 us
    all_to_all x4 -> x2, blocking collectives: 89.9 us -> 66.3 us  [swapped(): return lax.all_to_all(tiles, axis, split_axis=0, concat_axis=0, tiled=True)]
    pallas_call x8 -> x7, Pallas kernels: 22.8 us -> 12 us  [kernel_call(): pl.pallas_call(body, out_shape=tuple((jax.ShapeDtypeStruct(s, d) for s, d...]
    ppermute x0 -> x3, starting transfers between devices: none -> 8.11 us  [along_z(): return lax.ppermute(array, LINE, [(z, to(z)) for z in range(8)])]
    ppermute x0 -> x3, waiting for transfers between devices: none -> 5.45 us  [along_z(): return lax.ppermute(array, LINE, [(z, to(z)) for z in range(8)])]
    add x1, other arithmetic: 1.85 us -> 0.23 us  [body(): chip = mine + shifted(other, 'core', 1)]
    unnamed x35 -> x38, local copies, waits for them, and re-layouts: 13.7 us -> 13.3 us
  transfers between devices with their start and end apart: 8 -> 11, of which waited for: 4 -> 6; matrix products, arithmetic and copies ran while one was open for 1% -> 0% of each run, Pallas kernels for 3% -> 1%
where the time goes in v2:
time: 134 us; the launch traced here: 133 us
  blocking collectives  66.3 us (49%)
  starting transfers between devices  24.8 us (19%)
  waiting for transfers between devices  15.6 us (12%)
  local copies, waits for them, and re-layouts  13.3 us (10%)
  Pallas kernels  12 us (9%)
    all_to_all x2, blocking collectives, swapped(): return lax.all_to_all(tiles, axis, split_axis=0, concat_axis=0, tiled=True)  66.3 us
    ppermute x8, starting transfers between devices, shifted(): lax.ppermute(array, axis, [(i, (i + by) % size) for i in range(size)])  16.7 us
    unnamed x38, local copies, waits for them, and re-layouts  13.3 us
    pallas_call x7, Pallas kernels, kernel_call(): pl.pallas_call(body, out_shape=tuple((jax.ShapeDtypeStruct(s, d) for s, d...  12 us
    ppermute x8, waiting for transfers between devices, shifted(): lax.ppermute(array, axis, [(i, (i + by) % size) for i in range(size)])  10.1 us
    ppermute x3, starting transfers between devices, along_z(): return lax.ppermute(array, LINE, [(z, to(z)) for z in range(8)])  8.11 us
    ppermute x3, waiting for transfers between devices, along_z(): return lax.ppermute(array, LINE, [(z, to(z)) for z in range(8)])  5.45 us
  transfers between devices with their start and end apart: 11, of which 6 were waited for; matrix products, arithmetic and copies ran while one was open for 0% of the time, Pallas kernels for 1%

profile of v2, /device:TPU:1, one launch (start us, length us, event | category | flops | bytes accessed | tf_op | source)
XLA Modules:
  0.0 133.0 jit_solution(15119319757851356313)
XLA Ops:
  0.6 1.6 %copy-done = bf16[1024,1024]{1,0:T(8,128)(2,1)S(1)} copy-done((bf16[1024,1024]{1,0:T(8,128)(2,1)S(1)}, bf16[1024,1024]{1,0:T(8,128)(2,1)}, u32[]{:S(2)}) %copy-start) | copy-done | bytes 2097176
  2.2 0.9 copy-done.8
  3.2 0.9 copy-done.9
  4.1 0.7 copy-done.12
  4.8 0.8 copy-done.15
  5.6 2.2 %unroll_kernel.1 = (bf16[640,1024]{1,0:T(8,128)(2,1)S(1)}, f32[512,1024]{1,0:T(8,128)S(1)}, f32[128,1024]{1,0:T(8,128)S(1)}, f32[48,640]{1,0:T(8,128)S(1)}, f32[...) custom-call(bf16[128,1024]{1,0:T(8,128)(2,1)S(1)} %copy-done.8, ...), custom_call_target="tpu_custom_call" | custom-call | tf_op jit(solution)/shard_map/unroll_kernel/pallas_call | solution.py:40
  7.7 1.3 copy-done.2
  9.0 0.8 copy-done.4
  11.1 3.6 %collective-permute-start.2 = (f32[8,128]{1,0:T(8,128)S(1)}, f32[8,128]{1,0:T(8,128)S(1)}, u32[]{:S(2)}, u32[]{:S(2)}) collective-permute-start(f32[8,128]{1,0:T(8,128)S(1)} %get-tuple-element.27.refs_3_), channel_id=1, source_target_pairs={{0,3},{1,0},{2,1},{3,2},{4,7},{5,4},{6,5},{7,6},{8,11},{9,8},{10,9... | collective-permute-start | bytes 12296 | tf_op jit(solution)/shard_map/ppermute | solution.py:230
  14.7 1.6 %collective-permute-start = (f32[8,128]{1,0:T(8,128)S(1)}, f32[8,128]{1,0:T(8,128)S(1)}, u32[]{:S(2)}, u32[]{:S(2)}) collective-permute-start(f32[8,128]{1,0:T(8,128)S(1)} %get-tuple-element.27.refs_3_), channel_id=1, source_target_pairs={{0,2},{1,3},{2,0},{3,1},{4,6},{5,7},{6,4},{7,5},{8,10},{9,11},{10,... | collective-permute-start | bytes 12296 | tf_op jit(solution)/shard_map/ppermute | solution.py:230
  16.3 1.0 copy-done.5
  17.4 0.9 copy-done.7
  18.3 0.8 copy-done.11
  19.1 0.8 copy-done.14
  19.9 0.7 copy-done.18
  20.6 1.4 %targets_kernel.1 = (f32[5,128]{1,0:T(8,128)}, bf16[1024,640]{1,0:T(8,128)(2,1)S(1)}) custom-call(s32[5,128]{1,0:T(8,128)S(1)} %bitcast.11, f32[5,128]{1,0:T(8,128)S(1)} %bitcast.16, s32[5,128]{1,0:T(8,128)S(1)} %bitcast.17, f32[5,18,128]{2,1,0:T(8,128)S(1)} %bitcast.14, bf16[1024,1024]{1,0:T(8,128)(2,1)S(1)} %copy-done.1, bf16[32,1024]{1,0:T(8,128)(2,1)S(1)} %copy-done.11, ...), custom_call_target="tpu_custom_call" | custom-call | tf_op jit(solution)/shard_map/targets_kernel/pallas_call | solution.py:40
  22.9 1.1 collective-permute-start.5
  24.6 1.7 %collective-permute-start.3 = (f32[8,128]{1,0:T(8,128)S(1)}, f32[8,128]{1,0:T(8,128)S(1)}, u32[]{:S(2)}, u32[]{:S(2)}) collective-permute-start(f32[8,128]{1,0:T(8,128)S(1)} %get-tuple-element.30.refs_4_), channel_id=1, source_target_pairs={{0,2},{1,3},{2,0},{3,1},{4,6},{5,7},{6,4},{7,5},{8,10},{9,11},{10,... | collective-permute-start | bytes 12296 | tf_op jit(solution)/shard_map/ppermute | solution.py:230
  26.3 1.2 collective-permute-done.4.refs_6_
  27.6 0.9 collective-permute-done.3.refs_5_
  28.5 4.9 %gradient_body.1 = (f32[32,136,128]{2,1,0:T(8,128)S(1)}, f32[32,136,128]{2,1,0:T(8,128)S(1)}) custom-call(s32[2]{0:T(128)S(1)} %pad_add_fusion.refs_0_.place, s32[5,128]{1,0:T(8,128)S(1)} %bitcast.13, f32[48,640]{1,0:T(8,128)S(1)} %get-tuple-element.28.refs_2_, f32[24,640]{1,0:T(8,128)S(1)} %get-tuple-element.29.refs_3_, ...), custom_call_target="tpu_custom_call" | custom-call | tf_op jit(solution)/shard_map/gradient_body/pallas_call | solution.py:40
  33.4 3.1 %collective-permute-start.6 = (f32[32,136,128]{2,1,0:T(8,128)S(1)}, f32[32,136,128]{2,1,0:T(8,128)S(1)}, u32[]{:S(2)}, u32[]{:S(2)}) collective-permute-start(f32[32,136,128]{2,1,0:T(8,128)S(1)} %get-tuple-element.34), channel_id=1, source_target_pairs={{0,4},{4,0},{1,5},{5,1},{2,6},{6,2},{3,7},{7,3},{8,12},{12,8},{9,1... | collective-permute-start | bytes 6684680 | tf_op jit(solution)/shard_map/ppermute | solution.py:230
  36.5 4.0 %collective-permute-done.6 = f32[32,136,128]{2,1,0:T(8,128)S(1)} collective-permute-done((f32[32,136,128]{2,1,0:T(8,128)S(1)}, f32[32,136,128]{2,1,0:T(8,128)S(1)}, u32[]{:S(2)}, u32[]{:S(2)}) %collective-permute-start.6) | collective-permute-done | bytes 2228256 | tf_op jit(solution)/shard_map/ppermute | solution.py:230
  40.7 36.6 %all_to_all.10.arrived = f32[32,136,128]{2,1,0:T(8,128)S(1)} all-to-all(f32[32,136,128]{2,1,0:T(8,128)S(1)} %add.8), channel_id=1, replica_groups=mesh['zh'=4,'zp'=2,'x'=4,'core'=2,'y'=4] {'zp','x','y'}, dimensions={0} | all-to-all | bytes 4456448 | tf_op jit(solution)/shard_map/all_to_all | solution.py:238
  77.4 3.9 %collective-permute-start.9 = (f32[136,128]{1,0:T(8,128)S(1)}, f32[136,128]{1,0:T(8,128)S(1)}, u32[]{:S(2)}, u32[]{:S(2)}) collective-permute-start(f32[136,128]{1,0:T(8,128)S(1)} %plane_sum_kernel.1.own), channel_id=1, source_target_pairs={{0,96},{32,192},{64,160},{96,0},{128,224},{160,64},{192,32},{224,1... | collective-permute-start | bytes 208904 | tf_op jit(solution)/shard_map/ppermute | solution.py:242
  81.3 4.2 %collective-permute-start.8 = (f32[136,128]{1,0:T(8,128)S(1)}, f32[136,128]{1,0:T(8,128)S(1)}, u32[]{:S(2)}, u32[]{:S(2)}) collective-permute-start(f32[136,128]{1,0:T(8,128)S(1)} %plane_sum_kernel.1.own), channel_id=1, source_target_pairs={{0,128},{32,160},{64,192},{96,224},{128,0},{160,32},{192,64},{224,... | collective-permute-start | bytes 208904 | tf_op jit(solution)/shard_map/ppermute | solution.py:242
  85.5 3.1 %collective-permute-done.8.far = f32[136,128]{1,0:T(8,128)S(1)} collective-permute-done((f32[136,128]{1,0:T(8,128)S(1)}, f32[136,128]{1,0:T(8,128)S(1)}, u32[]{:S(2)}, u32[]{:S(2)}) %collective-permute-start.8) | collective-permute-done | bytes 69664 | tf_op jit(solution)/shard_map/ppermute | solution.py:242
  88.7 2.3 %collective-permute-done.7.near = f32[136,128]{1,0:T(8,128)S(1)} collective-permute-done((f32[136,128]{1,0:T(8,128)S(1)}, f32[136,128]{1,0:T(8,128)S(1)}, u32[]{:S(2)}, u32[]{:S(2)}) %collective-permute-start.7) | collective-permute-done | bytes 69664 | tf_op jit(solution)/shard_map/ppermute | solution.py:242
  91.1 29.7 %all_to_all.11.mine = f32[32,136,128]{2,1,0:T(8,128)S(1)} all-to-all(f32[32,136,128]{2,1,0:T(8,128)S(1)} %line_sum_kernel.1), channel_id=1, replica_groups=mesh['zh'=4,'zp'=2,'x'=4,'core'=2,'y'=4] {'zp','x','y'}, dimensions={0} | all-to-all | bytes 4456448 | tf_op jit(solution)/shard_map/all_to_all | solution.py:238
  120.9 5.0 %collective-permute-start.10 = (f32[32,136,128]{2,1,0:T(8,128)S(1)}, f32[32,136,128]{2,1,0:T(8,128)S(1)}, u32[]{:S(2)}, u32[]{:S(2)}) collective-permute-start(f32[32,136,128]{2,1,0:T(8,128)S(1)} %all_to_all.11.mine), channel_id=1, source_target_pairs={{0,4},{4,0},{1,5},{5,1},{2,6},{6,2},{3,7},{7,3},{8,12},{12,8},{9,1... | collective-permute-start | bytes 6684680 | tf_op jit(solution)/shard_map/ppermute | solution.py:230
  125.9 4.0 %collective-permute-done.10.other = f32[32,136,128]{2,1,0:T(8,128)S(1)} collective-permute-done((f32[32,136,128]{2,1,0:T(8,128)S(1)}, f32[32,136,128]{2,1,0:T(8,128)S(1)}, u32[]{:S(2)}, u32[]{:S(2)}) %collective-permute-start.10) | collective-permute-done | bytes 2228256 | tf_op jit(solution)/shard_map/ppermute | solution.py:230
  129.8 3.1 %assemble_kernel.1 = (f32[1024,1024]{1,0:T(8,128)}, f32[18,1024]{1,0:T(8,128)}, f32[36,1024]{1,0:T(8,128)}) custom-call(s32[2]{0:T(128)S(1)} %pad_add_fusion.refs_0_.place, f32[32,136,128]{2,1,0:T(8,128)S(1)} %all_to_all.11.mine, f32[32,136,128]{2,1,0:T(8,128)S(1)} %collective-permute-done.10.other), custom_call_target="tpu_custom_call" | custom-call | tf_op jit(solution)/shard_map/assemble_kernel/pallas_call | solution.py:40
  (39 shorter events, 3.4 us)
Async XLA Ops:
  0.6 1.6 %copy-start = (bf16[1024,1024]{1,0:T(8,128)(2,1)S(1)}, bf16[1024,1024]{1,0:T(8,128)(2,1)}, u32[]{:S(2)}) copy-start(bf16[1024,1024]{1,0:T(8,128)(2,1)} %refs_11_.1) | copy-start | bytes 6291460
  2.2 0.9 copy-start.8
  3.2 0.9 copy-start.9
  4.1 0.7 copy-start.12
  4.8 0.8 copy-start.15
  5.5 10.8 %copy-start.1 = (bf16[1024,1024]{1,0:T(8,128)(2,1)S(1)}, bf16[1024,1024]{1,0:T(8,128)(2,1)}, u32[]{:S(2)}) copy-start(bf16[1024,1024]{1,0:T(8,128)(2,1)} %refs_11_.1) | copy-start | bytes 6291460
  5.6 10.8 %copy-start.13 = (s32[128,5]{0,1:T(8,128)S(1)}, s32[128,5]{0,1:T(8,128)}, u32[]{:S(2)}) copy-start(s32[128,5]{0,1:T(8,128)} %param.9) | copy-start | bytes 7684
  5.6 10.8 %copy-start.17 = (f32[128,5]{0,1:T(8,128)S(1)}, f32[128,5]{0,1:T(8,128)}, u32[]{:S(2)}) copy-start(f32[128,5]{0,1:T(8,128)} %param.10) | copy-start | bytes 7684
  7.7 1.3 copy-start.2
  9.0 0.8 copy-start.4
  9.8 0.6 copy-start.6
  10.5 0.6 copy-start.10
  11.1 10.9 %collective-permute-start.2 = (f32[8,128]{1,0:T(8,128)S(1)}, f32[8,128]{1,0:T(8,128)S(1)}, u32[]{:S(2)}, u32[]{:S(2)}) collective-permute-start(f32[8,128]{1,0:T(8,128)S(1)} %get-tuple-element.27.refs_3_), channel_id=1, source_target_pairs={{0,3},{1,0},{2,1},{3,2},{4,7},{5,4},{6,5},{7,6},{8,11},{9,8},{10,9... | collective-permute-start | bytes 12296 | tf_op jit(solution)/shard_map/ppermute | solution.py:230
  14.7 7.3 %collective-permute-start.1 = (f32[8,128]{1,0:T(8,128)S(1)}, f32[8,128]{1,0:T(8,128)S(1)}, u32[]{:S(2)}, u32[]{:S(2)}) collective-permute-start(f32[8,128]{1,0:T(8,128)S(1)} %get-tuple-element.27.refs_3_), channel_id=1, source_target_pairs={{0,1},{1,2},{2,3},{3,0},{4,5},{5,6},{6,7},{7,4},{8,9},{9,10},{10,1... | collective-permute-start | bytes 12296 | tf_op jit(solution)/shard_map/ppermute | solution.py:230
  14.7 7.3 %collective-permute-start = (f32[8,128]{1,0:T(8,128)S(1)}, f32[8,128]{1,0:T(8,128)S(1)}, u32[]{:S(2)}, u32[]{:S(2)}) collective-permute-start(f32[8,128]{1,0:T(8,128)S(1)} %get-tuple-element.27.refs_3_), channel_id=1, source_target_pairs={{0,2},{1,3},{2,0},{3,1},{4,6},{5,7},{6,4},{7,5},{8,10},{9,11},{10,... | collective-permute-start | bytes 12296 | tf_op jit(solution)/shard_map/ppermute | solution.py:230
  16.3 1.0 copy-start.5
  17.4 0.9 copy-start.7
  18.3 0.8 copy-start.11
  19.1 0.8 copy-start.14
  19.9 0.7 copy-start.18
  20.6 7.9 %copy-start.3 = (f32[512,1024]{1,0:T(8,128)S(1)}, f32[512,1024]{1,0:T(8,128)}, u32[]{:S(2)}) copy-start(f32[512,1024]{1,0:T(8,128)} %copy-done.2) | copy-start | bytes 6291460
  22.0 0.7 copy-start.16
  22.9 3.5 %collective-permute-start.5 = (f32[8,128]{1,0:T(8,128)S(1)}, f32[8,128]{1,0:T(8,128)S(1)}, u32[]{:S(2)}, u32[]{:S(2)}) collective-permute-start(f32[8,128]{1,0:T(8,128)S(1)} %get-tuple-element.30.refs_4_), channel_id=1, source_target_pairs={{0,3},{1,0},{2,1},{3,2},{4,7},{5,4},{6,5},{7,6},{8,11},{9,8},{10,9... | collective-permute-start | bytes 12296 | tf_op jit(solution)/shard_map/ppermute | solution.py:230
  23.9 3.7 %collective-permute-start.4 = (f32[8,128]{1,0:T(8,128)S(1)}, f32[8,128]{1,0:T(8,128)S(1)}, u32[]{:S(2)}, u32[]{:S(2)}) collective-permute-start(f32[8,128]{1,0:T(8,128)S(1)} %get-tuple-element.30.refs_4_), channel_id=1, source_target_pairs={{0,1},{1,2},{2,3},{3,0},{4,5},{5,6},{6,7},{7,4},{8,9},{9,10},{10,1... | collective-permute-start | bytes 12296 | tf_op jit(solution)/shard_map/ppermute | solution.py:230
  24.6 4.0 %collective-permute-start.3 = (f32[8,128]{1,0:T(8,128)S(1)}, f32[8,128]{1,0:T(8,128)S(1)}, u32[]{:S(2)}, u32[]{:S(2)}) collective-permute-start(f32[8,128]{1,0:T(8,128)S(1)} %get-tuple-element.30.refs_4_), channel_id=1, source_target_pairs={{0,2},{1,3},{2,0},{3,1},{4,6},{5,7},{6,4},{7,5},{8,10},{9,11},{10,... | collective-permute-start | bytes 12296 | tf_op jit(solution)/shard_map/ppermute | solution.py:230
  33.4 7.1 %collective-permute-start.6 = (f32[32,136,128]{2,1,0:T(8,128)S(1)}, f32[32,136,128]{2,1,0:T(8,128)S(1)}, u32[]{:S(2)}, u32[]{:S(2)}) collective-permute-start(f32[32,136,128]{2,1,0:T(8,128)S(1)} %get-tuple-element.34), channel_id=1, source_target_pairs={{0,4},{4,0},{1,5},{5,1},{2,6},{6,2},{3,7},{7,3},{8,12},{12,8},{9,1... | collective-permute-start | bytes 6684680 | tf_op jit(solution)/shard_map/ppermute | solution.py:230
  77.4 8.1 %collective-permute-start.9 = (f32[136,128]{1,0:T(8,128)S(1)}, f32[136,128]{1,0:T(8,128)S(1)}, u32[]{:S(2)}, u32[]{:S(2)}) collective-permute-start(f32[136,128]{1,0:T(8,128)S(1)} %plane_sum_kernel.1.own), channel_id=1, source_target_pairs={{0,96},{32,192},{64,160},{96,0},{128,224},{160,64},{192,32},{224,1... | collective-permute-start | bytes 208904 | tf_op jit(solution)/shard_map/ppermute | solution.py:242
  81.3 7.3 %collective-permute-start.8 = (f32[136,128]{1,0:T(8,128)S(1)}, f32[136,128]{1,0:T(8,128)S(1)}, u32[]{:S(2)}, u32[]{:S(2)}) collective-permute-start(f32[136,128]{1,0:T(8,128)S(1)} %plane_sum_kernel.1.own), channel_id=1, source_target_pairs={{0,128},{32,160},{64,192},{96,224},{128,0},{160,32},{192,64},{224,... | collective-permute-start | bytes 208904 | tf_op jit(solution)/shard_map/ppermute | solution.py:242
  85.5 5.4 %collective-permute-start.7 = (f32[136,128]{1,0:T(8,128)S(1)}, f32[136,128]{1,0:T(8,128)S(1)}, u32[]{:S(2)}, u32[]{:S(2)}) collective-permute-start(f32[136,128]{1,0:T(8,128)S(1)} %plane_sum_kernel.1.own), channel_id=1, source_target_pairs={{0,224},{32,64},{64,32},{96,128},{128,96},{160,192},{192,160},{224... | collective-permute-start | bytes 208904 | tf_op jit(solution)/shard_map/ppermute | solution.py:242
  120.9 9.0 %collective-permute-start.10 = (f32[32,136,128]{2,1,0:T(8,128)S(1)}, f32[32,136,128]{2,1,0:T(8,128)S(1)}, u32[]{:S(2)}, u32[]{:S(2)}) collective-permute-start(f32[32,136,128]{2,1,0:T(8,128)S(1)} %all_to_all.11.mine), channel_id=1, source_target_pairs={{0,4},{4,0},{1,5},{5,1},{2,6},{6,2},{3,7},{7,3},{8,12},{12,8},{9,1... | collective-permute-start | bytes 6684680 | tf_op jit(solution)/shard_map/ppermute | solution.py:230

commit v3 on v2

--- a/solution.py
+++ b/solution.py
@@ -22,6 +22,7 @@
 
 VMEM = pl.BlockSpec(memory_space=pltpu.VMEM)
 SMEM = pl.BlockSpec(memory_space=pltpu.SMEM)
+HBM = pl.BlockSpec(memory_space=pltpu.MemorySpace.HBM)
 
 
 def dot(a, b):
@@ -36,16 +37,25 @@
     return lax.dot_general(a, b, (((0,), (0,)), ((), ())), preferred_element_type=F32)
 
 
-def kernel_call(body, outs, inputs, scratch=(), scalars=0):
+def kernel_call(body, outs, inputs, scratch=(), scalars=0, far=(), far_outs=(), aliases=None):
     return pl.pallas_call(
         body,
         out_shape=tuple(jax.ShapeDtypeStruct(s, d) for s, d in outs),
-        in_specs=[SMEM] * scalars + [VMEM] * (len(inputs) - scalars),
-        out_specs=tuple(VMEM for _ in outs),
+        in_specs=[
+            SMEM if i < scalars else HBM if i in far else VMEM for i in range(len(inputs))
+        ],
+        out_specs=tuple(HBM if i in far_outs else VMEM for i in range(len(outs))),
         scratch_shapes=list(scratch),
+        input_output_aliases=aliases or {},
         name=body.__name__,
-        compiler_params=pltpu.CompilerParams(vmem_limit_bytes=12 * 1024 * 1024),
+        compiler_params=pltpu.CompilerParams(vmem_limit_bytes=16 * 1024 * 1024),
     )(*inputs)
+
+
+def started(source, target, sem):
+    copy = pltpu.make_async_copy(source, target, sem)
+    copy.start()
+    return copy
 
 
 def chosen(act, step, count):
@@ -67,43 +77,66 @@
     return logits, q, pi, total, v
 
 
-def unroll_kernel(emb, act, wh, wa, whd, s_out, t_out, st_out, o_out, ssq_out, wap, whp, wide, rows40):
+def unroll_kernel(
+    emb_far, act_far, wh_far, wa_far, whd_far,
+    s_out, t_far, o_out, ssq_out, act, whp,
+    emb, wh, wa, whd, t_buf, wap, wide, rows40, sem, t_sem,
+):
+    loads = [
+        started(source, target, sem.at[i])
+        for i, (source, target) in enumerate(
+            ((wh_far, wh), (emb_far, emb), (act_far, act), (wa_far, wa), (whd_far, whd))
+        )
+    ]
     count = wa.shape[0]
     steps = act.shape[0]
     rows = emb.shape[0]
     wap[...] = jnp.zeros_like(wap)
+    wide[...] = jnp.zeros_like(wide)
+    for load in loads[1:]:
+        load.wait()
     wap[:count, :] = wa[...]
     rows40[0 : 2 * count, :] = whd[...].astype(F32)
-    wide[...] = jnp.zeros_like(wide)
     wide[0:count, :] = rows40[0:count, :]
     wide[Q_ROW : Q_ROW + count, :] = rows40[count : 2 * count, :]
     whp[...] = wide[...].astype(BF16)
     state = emb[...].astype(F32)
+    loads[0].wait()
+    stores = []
     for k in range(steps):
+        here = slice(k * rows, (k + 1) * rows)
         s = state.astype(BF16)
-        s_out[k * rows : (k + 1) * rows, :] = s
+        s_out[here, :] = s
+        t = jnp.tanh(dot(s, wh[...]) + dot_tn(onehot_of(act, k), wap[...]))
         if k < steps - 1:
-            t = jnp.tanh(dot(s, wh[...]) + dot_tn(onehot_of(act, k), wap[...]))
-            t_out[k * rows : (k + 1) * rows, :] = t
-            state = state + t
-    st_out[...] = state
-    o_out[...] = dot_nt(whp[...], s_out[...])
-    _, q, _, _, v = policy_of(o_out, slice(None), count)
+            t_buf[here, :] = t
+            stores.append(started(t_buf.at[here, :], t_far.at[here, :], t_sem.at[k]))
+        state = state + t
+    inner = steps * rows
+    o_out[:, :inner] = dot_nt(whp[...], s_out[...])
+    o_out[:, inner:] = dot_nt(whp[...], state.astype(BF16))
+    _, q, _, _, v = policy_of(o_out, slice(0, inner), count)
     adv = q - v
     part = jnp.sum(jnp.sum(adv * adv, axis=1, keepdims=True), axis=0, keepdims=True)
     ssq_out[...] = jnp.broadcast_to(part, ssq_out.shape)
-
-
-def targets_kernel(act, rew, ends, beh, wh, wap, whp, s, st, o, tg_out, sT_out, last_out):
-    steps = act.shape[0]
-    rows = st.shape[0]
+    for store in stores:
+        store.wait()
+
+
+def targets_kernel(rew_far, ends_far, beh_far, act, s, o, tg_far, tg_out, sT_out, rew, ends, beh, sem):
+    loads = [
+        started(source, target, sem.at[i])
+        for i, (source, target) in enumerate(((rew_far, rew), (ends_far, ends), (beh_far, beh)))
+    ]
+    steps, rows = act.shape
     count = beh.shape[1]
-    last = steps - 1
-    t = jnp.tanh(dot(s[last * rows :, :], wh[...]) + dot_tn(onehot_of(act, last), wap[...]))
-    last_out[...] = dot_nt(whp[...], (st[...] + t).astype(BF16))
-    v_next = policy_of(last_out, slice(None), count)[-1]
+    for k in range(steps):
+        sT_out[:, k * rows : (k + 1) * rows] = s[k * rows : (k + 1) * rows, :].T
+    for load in loads:
+        load.wait()
+    v_next = policy_of(o, slice(steps * rows, (steps + 1) * rows), count)[-1]
     carried = jnp.zeros((1, rows), F32)
-    for k in range(last, -1, -1):
+    for k in range(steps - 1, -1, -1):
         logits, _, _, total, v = policy_of(o, slice(k * rows, (k + 1) * rows), count)
         b = beh[k]
         b_total = jnp.sum(jnp.exp(b), axis=0, keepdims=True)
@@ -115,8 +148,7 @@
         carried = clipped * td + DISCOUNT * TRACE_LAMBDA * open_ * clipped * carried
         tg_out[k : k + 1, :] = v + carried
         v_next = v
-    for k in range(steps):
-        sT_out[:, k * rows : (k + 1) * rows] = s[k * rows : (k + 1) * rows, :].T
+    started(tg_out, tg_far, sem.at[3]).wait()
 
 
 def weights_kernel(groups, devices, count, act, o, tg, ssq0, ssq1, ssq2, ssq3, a_out, b_out, mass_out):
@@ -145,29 +177,39 @@
 
 
 def gradient_kernel(
-    groups, count, place, act, a, b, m0, m1, m2, m3, s, sT, t, wh, whp, mine, other, gf, g, x, oh, e
+    groups, count, place, act, a, b, m0, m1, m2, m3, sT, t_far, wh_far, whp,
+    mine, other, gf, g, x, oh, e, t, wh, sem,
 ):
     steps, rows = act.shape
+    last = steps - 1
+    spans = [slice(k * rows, (k + 1) * rows) for k in range(steps)]
+    loads = {}
+    for k in range(last - 1, -1, -1):
+        loads[k] = started(t_far.at[spans[k], :], t.at[spans[k], :], sem.at[k])
+        if k == last - 1:
+            whole = started(wh_far, wh, sem.at[last])
     total = m0[0:1, 0:1] + m1[0:1, 0:1] + m2[0:1, 0:1] + m3[0:1, 0:1]
     mean = total / (groups * rows * steps)
     gf[...] = a[...]
     gf[0:Q_ROW, :] = a[0:Q_ROW, :] + b[...] / mean
     g[...] = gf[...].astype(BF16)
-    last = steps - 1
-    r = dot_tn(g[:, last * rows :], whp[...])
-    for k in range(last - 1, -1, -1):
-        here = slice(k * rows, (k + 1) * rows)
-        tk = t[here, :]
-        xk = (r * (1.0 - tk * tk)).astype(BF16)
-        x[here, :] = xk
-        oh[:, here] = onehot_of(act, k)
-        if k > 0:
-            r = r + (dot_nt(xk, wh[...]) + dot_tn(g[:, here], whp[...]))
-    inner = last * rows
+    for k in range(last):
+        oh[:, spans[k]] = onehot_of(act, k)
     e[...] = jnp.zeros_like(e)
-    heads = dot(g[...], s[...])
+    heads = dot_nt(g[...], sT[...])
     e[0:count, :] = heads[0:count, :]
     e[count : 2 * count, :] = heads[Q_ROW : Q_ROW + count, :]
+    r = dot_tn(g[:, spans[last]], whp[...])
+    for k in range(last - 1, -1, -1):
+        loads[k].wait()
+        tk = t[spans[k], :]
+        xk = (r * (1.0 - tk * tk)).astype(BF16)
+        x[spans[k], :] = xk
+        if k == last - 1:
+            whole.wait()
+        if k > 0:
+            r = r + (dot_nt(xk, wh[...]) + dot_tn(g[:, spans[k]], whp[...]))
+    inner = last * rows
     e[A_ROW : A_ROW + count, :] = dot(oh[...], x[...])[0:count, :]
     hid = sT.shape[0]
     half = hid // 2
@@ -204,25 +246,40 @@
         out[i] = total
 
 
-def assemble_kernel(place, mine, other, gh, ga, gd, e):
-    half = gh.shape[0] // 2
-    core, flip = place[0], place[1]
-    for part, h in ((mine, core), (other, 1 - core)):
-        for p in range(2):
-            slot = pl.ds((flip + p - 2 * flip * p) * 16, 16)
-            at = pl.ds(pl.multiple_of(h * half + p * 256, 256), 256)
-            for n in range(8):
-                gh[at, n * LANES : (n + 1) * LANES] = part[
-                    slot, n * 16 : (n + 1) * 16, :
-                ].reshape(256, LANES)
-        for i in range(4):
-            p = i // 2
-            slot = (flip + p - 2 * flip * p) * 16 + (i % 2) * 8
-            at8 = pl.ds(pl.multiple_of(h * 32 + i * 8, 8), 8)
-            for n in range(8):
-                e[at8, n * LANES : (n + 1) * LANES] = part[slot + n, 128:136, :]
+def lay_out(place, part, h, gh_far, buf, e, sem):
+    half = gh_far.shape[0] // 2
+    flip = place[1]
+    copies = []
+    for p in range(2):
+        slot = pl.ds((flip + p - 2 * flip * p) * 16, 16)
+        here = slice(p * 256, (p + 1) * 256)
+        for n in range(8):
+            buf[here, n * LANES : (n + 1) * LANES] = part[
+                slot, n * 16 : (n + 1) * 16, :
+            ].reshape(256, LANES)
+        at = pl.ds(pl.multiple_of(h * half + p * 256, 256), 256)
+        copies.append(started(buf.at[here, :], gh_far.at[at, :], sem.at[p]))
+    for i in range(4):
+        p = i // 2
+        slot = (flip + p - 2 * flip * p) * 16 + (i % 2) * 8
+        at8 = pl.ds(pl.multiple_of(h * 32 + i * 8, 8), 8)
+        for n in range(8):
+            e[at8, n * LANES : (n + 1) * LANES] = part[slot + n, 128:136, :]
+    return copies
+
+
+def first_half_kernel(place, mine, gh_far, e, buf, sem):
+    for copy in lay_out(place, mine, place[0], gh_far, buf, e, sem):
+        copy.wait()
+
+
+def second_half_kernel(place, other, e_in, gh_in, gh_far, ga, gd, buf, e, sem):
+    e[...] = e_in[...]
+    copies = lay_out(place, other, 1 - place[0], gh_far, buf, e, sem)
     ga[...] = e[A_ROW : A_ROW + ga.shape[0], :]
     gd[...] = e[0 : gd.shape[0], :]
+    for copy in copies:
+        copy.wait()
 
 
 def shifted(array, axis, by):
@@ -257,39 +314,46 @@
     groups = lax.axis_size("y")
     devices = lax.axis_size(ALL)
     place = jnp.stack([lax.axis_index("core"), lax.axis_index("zh") % 2]).astype(jnp.int32)
-    act = actions.T
-
-    s, t, state, out, ssq, wap, whp = kernel_call(
+
+    s, t, out, ssq, act, whp = kernel_call(
         unroll_kernel,
         [
             ((steps * rows, hid), BF16),
             (((steps - 1) * rows, hid), F32),
-            ((rows, hid), F32),
-            ((48, steps * rows), F32),
+            ((48, (steps + 1) * rows), F32),
             ((8, LANES), F32),
-            ((32, hid), BF16),
+            ((steps, rows), jnp.int32),
             ((48, hid), BF16),
         ],
-        (embed, act, w_hidden, w_action, w_heads.T),
-        (pltpu.VMEM((48, hid), F32), pltpu.VMEM((40, hid), F32)),
+        (embed, actions.T, w_hidden, w_action, w_heads.T),
+        (
+            pltpu.VMEM((rows, hid), BF16),
+            pltpu.VMEM((hid, hid), BF16),
+            pltpu.VMEM((count, hid), BF16),
+            pltpu.VMEM((2 * count, hid), BF16),
+            pltpu.VMEM(((steps - 1) * rows, hid), F32),
+            pltpu.VMEM((32, hid), BF16),
+            pltpu.VMEM((48, hid), F32),
+            pltpu.VMEM((40, hid), F32),
+            pltpu.SemaphoreType.DMA((5,)),
+            pltpu.SemaphoreType.DMA((steps - 1,)),
+        ),
+        far=range(5),
+        far_outs=(1,),
     )
     ssqs = of_group(ssq)
-    targets, sT = kernel_call(
+    targets, tg, sT = kernel_call(
         targets_kernel,
-        [((steps, rows), F32), ((hid, steps * rows), BF16)],
+        [((steps, rows), F32), ((steps, rows), F32), ((hid, steps * rows), BF16)],
+        (rewards.T, ends.T, jnp.transpose(behaviour, (1, 2, 0)), act, s, out),
         (
-            act,
-            rewards.T,
-            ends.T,
-            jnp.transpose(behaviour, (1, 2, 0)),
-            w_hidden,
-            wap,
-            whp,
-            s,
-            state,
-            out,
+            pltpu.VMEM((steps, rows), F32),
+            pltpu.VMEM((steps, rows), jnp.int32),
+            pltpu.VMEM((steps, count, rows), F32),
+            pltpu.SemaphoreType.DMA((4,)),
         ),
-        (pltpu.VMEM((48, rows), F32),),
+        far=range(3),
+        far_outs=(0,),
     )
 
     def weights_body(*refs):
@@ -298,7 +362,7 @@
     a, b, mass = kernel_call(
         weights_body,
         [((48, steps * rows), F32), ((Q_ROW, steps * rows), F32), ((8, LANES), F32)],
-        (act, out, targets, *ssqs),
+        (act, out, tg, *ssqs),
     )
     masses = of_group(mass)
 
@@ -309,15 +373,19 @@
     mine, other = kernel_call(
         gradient_body,
         [parts, parts],
-        (place, act, a, b, *masses, s, sT, t, w_hidden, whp),
+        (place, act, a, b, *masses, sT, t, w_hidden, whp),
         (
             pltpu.VMEM((48, steps * rows), F32),
             pltpu.VMEM((48, steps * rows), BF16),
             pltpu.VMEM(((steps - 1) * rows, hid), BF16),
             pltpu.VMEM((32, (steps - 1) * rows), BF16),
             pltpu.VMEM((64, hid), F32),
+            pltpu.VMEM(((steps - 1) * rows, hid), F32),
+            pltpu.VMEM((hid, hid), BF16),
+            pltpu.SemaphoreType.DMA((steps,)),
         ),
         scalars=1,
+        far=(9, 10),
     )
     chip = mine + shifted(other, "core", 1)
     (own,) = kernel_call(plane_sum_kernel, [((136, LANES), F32)], (swapped(chip, NEAR),))
@@ -327,12 +395,24 @@
     (whole,) = kernel_call(line_sum_kernel, [parts], (own, near, far, both))
     mine = swapped(whole, NEAR)
     other = shifted(mine, "core", 1)
+    staging = (pltpu.VMEM((hid // 2, hid), F32), pltpu.SemaphoreType.DMA((2,)))
+    partly, extra = kernel_call(
+        first_half_kernel,
+        [((hid, hid), F32), ((64, hid), F32)],
+        (place, mine),
+        staging,
+        scalars=1,
+        far_outs=(0,),
+    )
     grad_hidden, grad_action, grad_heads = kernel_call(
-        assemble_kernel,
+        second_half_kernel,
         [((hid, hid), F32), (w_action.shape, F32), (w_heads.shape[::-1], F32)],
-        (place, mine, other),
-        (pltpu.VMEM((64, hid), F32),),
+        (place, other, extra, partly),
+        (staging[0], pltpu.VMEM((64, hid), F32), staging[1]),
         scalars=1,
+        far=(3,),
+        far_outs=(0,),
+        aliases={3: 0},
     )
     return (grad_hidden, grad_action, grad_heads.T, targets.T)
 

time: 134 us -> 138 us (1.030)
  Pallas kernels: 12 us -> 17.5 us
  waiting for transfers between devices: 15.6 us -> 13.5 us
    pallas_call x7 -> x8, Pallas kernels: 12 us -> 17.5 us  [kernel_call(): pl.pallas_call(body, out_shape=tuple((jax.ShapeDtypeStruct(s, d) for s, d...]
    ppermute x8, waiting for transfers between devices: 10.1 us -> 8.13 us  [shifted(): lax.ppermute(array, axis, [(i, (i + by) % size) for i in range(size)])]
    unnamed x38 -> x30, local copies, waits for them, and re-layouts: 13.3 us -> 12.8 us
  transfers between devices with their start and end apart: 11 -> 11, of which waited for: 6 -> 6; matrix products, arithmetic and copies ran while one was open for 0% -> 0% of each run, Pallas kernels for 1% -> 2%
where the time goes in v3:
time: 138 us
  blocking collectives  67.3 us (49%)
  starting transfers between devices  25.4 us (18%)
  Pallas kernels  17.5 us (13%)
  waiting for transfers between devices  13.5 us (10%)
  local copies, waits for them, and re-layouts  12.8 us (9%)
    all_to_all x2, blocking collectives, swapped(): return lax.all_to_all(tiles, axis, split_axis=0, concat_axis=0, tiled=True)  67.3 us
    pallas_call x8, Pallas kernels, kernel_call(): pl.pallas_call(body, out_shape=tuple((jax.ShapeDtypeStruct(s, d) for s, d...  17.5 us
    ppermute x8, starting transfers between devices, shifted(): lax.ppermute(array, axis, [(i, (i + by) % size) for i in range(size)])  17.1 us
    unnamed x30, local copies, waits for them, and re-layouts  12.8 us
    ppermute x3, starting transfers between devices, along_z(): return lax.ppermute(array, LINE, [(z, to(z)) for z in range(8)])  8.31 us
    ppermute x8, waiting for transfers between devices, shifted(): lax.ppermute(array, axis, [(i, (i + by) % size) for i in range(size)])  8.13 us
    ppermute x3, waiting for transfers between devices, along_z(): return lax.ppermute(array, LINE, [(z, to(z)) for z in range(8)])  5.4 us
  transfers between devices with their start and end apart: 11, of which 6 were waited for; matrix products, arithmetic and copies ran while one was open for 0% of the time, Pallas kernels for 2%

profile of v3, /device:TPU:1, one launch (start us, length us, event | category | flops | bytes accessed | tf_op | source)
XLA Modules:
  0.0 137.8 jit_solution(4994946456169869444)
XLA Ops:
  0.6 1.6 %copy-done = bf16[1024,1024]{1,0:T(8,128)(2,1)S(1)} copy-done((bf16[1024,1024]{1,0:T(8,128)(2,1)S(1)}, bf16[1024,1024]{1,0:T(8,128)(2,1)}, u32[]{:S(2)}) %copy-start) | copy-done | bytes 2097176
  2.2 0.9 copy-done.4
  3.2 0.9 copy-done.7
  4.1 0.8 copy-done.9
  4.9 0.7 copy-done.12
  5.6 4.5 %unroll_kernel.1 = (bf16[640,1024]{1,0:T(8,128)(2,1)S(1)}, f32[512,1024]{1,0:T(8,128)S(1)}, f32[48,768]{1,0:T(8,128)S(1)}, f32[8,128]{1,0:T(8,128)}, s32[5,128]{1,0:T(8,128)S(1)}, /*index=5*/bf16[48,1024]{1,0:T(8,128)(2,1)S(1)}) custom-call(bf16[128,1024]{1,0:T(8,128)(2,1)S(1)} %copy-done.4, s32[5,128]{1,0:T(8,128)S(1)} %bitcast.11, ...), custom_call_target="tpu_custom_call" | custom-call | tf_op jit(solution)/shard_map/unroll_kernel/pallas_call | solution.py:41
  10.1 1.3 copy-done.2
  12.6 3.6 %collective-permute-start.2 = (f32[8,128]{1,0:T(8,128)}, f32[8,128]{1,0:T(8,128)}, u32[]{:S(2)}, u32[]{:S(2)}) collective-permute-start(f32[8,128]{1,0:T(8,128)} %get-tuple-element.27.refs_3_), channel_id=1, source_target_pairs={{0,3},{1,0},{2,1},{3,2},{4,7},{5,4},{6,5},{7,6},{8,11},{9,8},{10,9... | collective-permute-start | bytes 12296 | tf_op jit(solution)/shard_map/ppermute | solution.py:287
  16.3 1.6 %collective-permute-start = (f32[8,128]{1,0:T(8,128)}, f32[8,128]{1,0:T(8,128)}, u32[]{:S(2)}, u32[]{:S(2)}) collective-permute-start(f32[8,128]{1,0:T(8,128)} %get-tuple-element.27.refs_3_), channel_id=1, source_target_pairs={{0,2},{1,3},{2,0},{3,1},{4,6},{5,7},{6,4},{7,5},{8,10},{9,11},{10,... | collective-permute-start | bytes 12296 | tf_op jit(solution)/shard_map/ppermute | solution.py:287
  17.9 0.8 copy-done.8
  18.7 0.7 copy-done.11
  20.8 1.1 targets_kernel.1
  21.9 0.9 weights_body.1
  22.8 1.3 collective-permute-start.5
  24.6 1.7 %collective-permute-start.3 = (f32[8,128]{1,0:T(8,128)S(1)}, f32[8,128]{1,0:T(8,128)S(1)}, u32[]{:S(2)}, u32[]{:S(2)}) collective-permute-start(f32[8,128]{1,0:T(8,128)S(1)} %get-tuple-element.30.refs_4_), channel_id=1, source_target_pairs={{0,2},{1,3},{2,0},{3,1},{4,6},{5,7},{6,4},{7,5},{8,10},{9,11},{10,... | collective-permute-start | bytes 12296 | tf_op jit(solution)/shard_map/ppermute | solution.py:287
  26.3 1.5 %collective-permute-done.4.refs_6_ = f32[8,128]{1,0:T(8,128)S(1)} collective-permute-done((f32[8,128]{1,0:T(8,128)S(1)}, f32[8,128]{1,0:T(8,128)S(1)}, u32[]{:S(2)}, u32[]{:S(2)}) %collective-permute-start.4) | collective-permute-done | bytes 4128 | tf_op jit(solution)/shard_map/ppermute | solution.py:287
  27.8 0.7 collective-permute-done.3.refs_5_
  28.5 1.6 %copy-done.3 = f32[512,1024]{1,0:T(8,128)S(1)} copy-done((f32[512,1024]{1,0:T(8,128)S(1)}, f32[512,1024]{1,0:T(8,128)}, u32[]{:S(2)}) %copy-start.3) | copy-done | bytes 2097176
  30.1 0.9 copy-done.6
  31.0 6.0 %gradient_body.1 = (f32[32,136,128]{2,1,0:T(8,128)S(1)}, f32[32,136,128]{2,1,0:T(8,128)S(1)}) custom-call(s32[2]{0:T(128)S(1)} %pad_add_fusion.refs_0_.place, s32[5,128]{1,0:T(8,128)S(1)} %copy-done.11, f32[48,640]{1,0:T(8,128)S(1)} %get-tuple-element.28.refs_2_, f32[24,640]{1,0:T(8,128)S(1)} %get-tuple-element.29.refs_3_, ...), custom_call_target="tpu_custom_call" | custom-call | tf_op jit(solution)/shard_map/gradient_body/pallas_call | solution.py:41
  37.0 3.4 %collective-permute-start.6 = (f32[32,136,128]{2,1,0:T(8,128)S(1)}, f32[32,136,128]{2,1,0:T(8,128)S(1)}, u32[]{:S(2)}, u32[]{:S(2)}) collective-permute-start(f32[32,136,128]{2,1,0:T(8,128)S(1)} %get-tuple-element.35), channel_id=1, source_target_pairs={{0,4},{4,0},{1,5},{5,1},{2,6},{6,2},{3,7},{7,3},{8,12},{12,8},{9,1... | collective-permute-start | bytes 6684680 | tf_op jit(solution)/shard_map/ppermute | solution.py:287
  40.5 4.0 %collective-permute-done.6 = f32[32,136,128]{2,1,0:T(8,128)S(1)} collective-permute-done((f32[32,136,128]{2,1,0:T(8,128)S(1)}, f32[32,136,128]{2,1,0:T(8,128)S(1)}, u32[]{:S(2)}, u32[]{:S(2)}) %collective-permute-start.6) | collective-permute-done | bytes 2228256 | tf_op jit(solution)/shard_map/ppermute | solution.py:287
  44.7 37.5 %all_to_all.10.arrived = f32[32,136,128]{2,1,0:T(8,128)S(1)} all-to-all(f32[32,136,128]{2,1,0:T(8,128)S(1)} %add.8), channel_id=1, replica_groups=mesh['zh'=4,'zp'=2,'x'=4,'core'=2,'y'=4] {'zp','x','y'}, dimensions={0} | all-to-all | bytes 4456448 | tf_op jit(solution)/shard_map/all_to_all | solution.py:295
  82.3 4.1 %collective-permute-start.9 = (f32[136,128]{1,0:T(8,128)S(1)}, f32[136,128]{1,0:T(8,128)S(1)}, u32[]{:S(2)}, u32[]{:S(2)}) collective-permute-start(f32[136,128]{1,0:T(8,128)S(1)} %plane_sum_kernel.1.own), channel_id=1, source_target_pairs={{0,96},{32,192},{64,160},{96,0},{128,224},{160,64},{192,32},{224,1... | collective-permute-start | bytes 208904 | tf_op jit(solution)/shard_map/ppermute | solution.py:299
  86.4 4.2 %collective-permute-start.8 = (f32[136,128]{1,0:T(8,128)S(1)}, f32[136,128]{1,0:T(8,128)S(1)}, u32[]{:S(2)}, u32[]{:S(2)}) collective-permute-start(f32[136,128]{1,0:T(8,128)S(1)} %plane_sum_kernel.1.own), channel_id=1, source_target_pairs={{0,128},{32,160},{64,192},{96,224},{128,0},{160,32},{192,64},{224,... | collective-permute-start | bytes 208904 | tf_op jit(solution)/shard_map/ppermute | solution.py:299
  90.6 3.1 %collective-permute-done.8.far = f32[136,128]{1,0:T(8,128)S(1)} collective-permute-done((f32[136,128]{1,0:T(8,128)S(1)}, f32[136,128]{1,0:T(8,128)S(1)}, u32[]{:S(2)}, u32[]{:S(2)}) %collective-permute-start.8) | collective-permute-done | bytes 69664 | tf_op jit(solution)/shard_map/ppermute | solution.py:299
  93.7 2.3 %collective-permute-done.7.near = f32[136,128]{1,0:T(8,128)S(1)} collective-permute-done((f32[136,128]{1,0:T(8,128)S(1)}, f32[136,128]{1,0:T(8,128)S(1)}, u32[]{:S(2)}, u32[]{:S(2)}) %collective-permute-start.7) | collective-permute-done | bytes 69664 | tf_op jit(solution)/shard_map/ppermute | solution.py:299
  96.2 29.8 %all_to_all.11.mine = f32[32,136,128]{2,1,0:T(8,128)S(1)} all-to-all(f32[32,136,128]{2,1,0:T(8,128)S(1)} %line_sum_kernel.1), channel_id=1, replica_groups=mesh['zh'=4,'zp'=2,'x'=4,'core'=2,'y'=4] {'zp','x','y'}, dimensions={0} | all-to-all | bytes 4456448 | tf_op jit(solution)/shard_map/all_to_all | solution.py:295
  126.0 5.0 %collective-permute-start.10 = (f32[32,136,128]{2,1,0:T(8,128)S(1)}, f32[32,136,128]{2,1,0:T(8,128)S(1)}, u32[]{:S(2)}, u32[]{:S(2)}) collective-permute-start(f32[32,136,128]{2,1,0:T(8,128)S(1)} %all_to_all.11.mine), channel_id=1, source_target_pairs={{0,4},{4,0},{1,5},{5,1},{2,6},{6,2},{3,7},{7,3},{8,12},{12,8},{9,1... | collective-permute-start | bytes 6684680 | tf_op jit(solution)/shard_map/ppermute | solution.py:287
  131.0 2.0 %first_half_kernel.1 = (f32[1024,1024]{1,0:T(8,128)}, f32[64,1024]{1,0:T(8,128)S(1)}) custom-call(s32[2]{0:T(128)S(1)} %pad_add_fusion.refs_0_.place, f32[32,136,128]{2,1,0:T(8,128)S(1)} %all_to_all.11.mine), custom_call_target="tpu_custom_call" | custom-call | tf_op jit(solution)/shard_map/first_half_kernel/pallas_call | solution.py:41
  133.0 2.0 %collective-permute-done.10.other = f32[32,136,128]{2,1,0:T(8,128)S(1)} collective-permute-done((f32[32,136,128]{2,1,0:T(8,128)S(1)}, f32[32,136,128]{2,1,0:T(8,128)S(1)}, u32[]{:S(2)}, u32[]{:S(2)}) %collective-permute-start.10) | collective-permute-done | bytes 2228256 | tf_op jit(solution)/shard_map/ppermute | solution.py:287
  134.9 2.7 %second_half_kernel.1 = (f32[1024,1024]{1,0:T(8,128)}, f32[18,1024]{1,0:T(8,128)}, f32[36,1024]{1,0:T(8,128)}) custom-call(s32[2]{0:T(128)S(1)} %pad_add_fusion.refs_0_.place, f32[32,136,128]{2,1,0:T(8,128)S(1)} %collective-permute-done.10.other, f32[64,1024]{1,0:T(8,128)S(1)} %get-tuple-element.36.e_in, ...), custom_call_target="tpu_custom_call", output_to_operand_aliasing={{0}: (3, {})} | custom-call | tf_op jit(solution)/shard_map/second_half_kernel/pallas_call | solution.py:41
  (32 shorter events, 3.6 us)
Async XLA Ops:
  0.6 1.6 %copy-start = (bf16[1024,1024]{1,0:T(8,128)(2,1)S(1)}, bf16[1024,1024]{1,0:T(8,128)(2,1)}, u32[]{:S(2)}) copy-start(bf16[1024,1024]{1,0:T(8,128)(2,1)} %refs_10_.1) | copy-start | bytes 6291460
  2.2 0.9 copy-start.4
  3.2 0.9 copy-start.7
  4.1 0.8 copy-start.9
  4.9 0.7 copy-start.12
  5.5 23.0 %copy-start.1 = (bf16[1024,1024]{1,0:T(8,128)(2,1)S(1)}, bf16[1024,1024]{1,0:T(8,128)(2,1)}, u32[]{:S(2)}) copy-start(bf16[1024,1024]{1,0:T(8,128)(2,1)} %refs_10_.1) | copy-start | bytes 6291460
  10.1 1.3 copy-start.2
  11.4 0.6 copy-start.5
  12.0 0.6 copy-start.10
  12.6 9.3 %collective-permute-start.2 = (f32[8,128]{1,0:T(8,128)}, f32[8,128]{1,0:T(8,128)}, u32[]{:S(2)}, u32[]{:S(2)}) collective-permute-start(f32[8,128]{1,0:T(8,128)} %get-tuple-element.27.refs_3_), channel_id=1, source_target_pairs={{0,3},{1,0},{2,1},{3,2},{4,7},{5,4},{6,5},{7,6},{8,11},{9,8},{10,9... | collective-permute-start | bytes 12296 | tf_op jit(solution)/shard_map/ppermute | solution.py:287
  16.3 5.7 %collective-permute-start.1 = (f32[8,128]{1,0:T(8,128)}, f32[8,128]{1,0:T(8,128)}, u32[]{:S(2)}, u32[]{:S(2)}) collective-permute-start(f32[8,128]{1,0:T(8,128)} %get-tuple-element.27.refs_3_), channel_id=1, source_target_pairs={{0,1},{1,2},{2,3},{3,0},{4,5},{5,6},{6,7},{7,4},{8,9},{9,10},{10,1... | collective-permute-start | bytes 12296 | tf_op jit(solution)/shard_map/ppermute | solution.py:287
  16.3 5.7 %collective-permute-start = (f32[8,128]{1,0:T(8,128)}, f32[8,128]{1,0:T(8,128)}, u32[]{:S(2)}, u32[]{:S(2)}) collective-permute-start(f32[8,128]{1,0:T(8,128)} %get-tuple-element.27.refs_3_), channel_id=1, source_target_pairs={{0,2},{1,3},{2,0},{3,1},{4,6},{5,7},{6,4},{7,5},{8,10},{9,11},{10,... | collective-permute-start | bytes 12296 | tf_op jit(solution)/shard_map/ppermute | solution.py:287
  17.9 0.8 copy-start.8
  18.7 0.7 copy-start.11
  19.4 0.7 copy-start.13
  20.1 0.7 copy-start.14
  22.8 3.5 %collective-permute-start.5 = (f32[8,128]{1,0:T(8,128)S(1)}, f32[8,128]{1,0:T(8,128)S(1)}, u32[]{:S(2)}, u32[]{:S(2)}) collective-permute-start(f32[8,128]{1,0:T(8,128)S(1)} %get-tuple-element.30.refs_4_), channel_id=1, source_target_pairs={{0,3},{1,0},{2,1},{3,2},{4,7},{5,4},{6,5},{7,6},{8,11},{9,8},{10,9... | collective-permute-start | bytes 12296 | tf_op jit(solution)/shard_map/ppermute | solution.py:287
  24.1 3.7 %collective-permute-start.4 = (f32[8,128]{1,0:T(8,128)S(1)}, f32[8,128]{1,0:T(8,128)S(1)}, u32[]{:S(2)}, u32[]{:S(2)}) collective-permute-start(f32[8,128]{1,0:T(8,128)S(1)} %get-tuple-element.30.refs_4_), channel_id=1, source_target_pairs={{0,1},{1,2},{2,3},{3,0},{4,5},{5,6},{6,7},{7,4},{8,9},{9,10},{10,1... | collective-permute-start | bytes 12296 | tf_op jit(solution)/shard_map/ppermute | solution.py:287
  24.6 4.0 %collective-permute-start.3 = (f32[8,128]{1,0:T(8,128)S(1)}, f32[8,128]{1,0:T(8,128)S(1)}, u32[]{:S(2)}, u32[]{:S(2)}) collective-permute-start(f32[8,128]{1,0:T(8,128)S(1)} %get-tuple-element.30.refs_4_), channel_id=1, source_target_pairs={{0,2},{1,3},{2,0},{3,1},{4,6},{5,7},{6,4},{7,5},{8,10},{9,11},{10,... | collective-permute-start | bytes 12296 | tf_op jit(solution)/shard_map/ppermute | solution.py:287
  28.5 1.6 %copy-start.3 = (f32[512,1024]{1,0:T(8,128)S(1)}, f32[512,1024]{1,0:T(8,128)}, u32[]{:S(2)}) copy-start(f32[512,1024]{1,0:T(8,128)} %copy-done.2) | copy-start | bytes 6291460
  30.1 0.9 copy-start.6
  37.0 7.4 %collective-permute-start.6 = (f32[32,136,128]{2,1,0:T(8,128)S(1)}, f32[32,136,128]{2,1,0:T(8,128)S(1)}, u32[]{:S(2)}, u32[]{:S(2)}) collective-permute-start(f32[32,136,128]{2,1,0:T(8,128)S(1)} %get-tuple-element.35), channel_id=1, source_target_pairs={{0,4},{4,0},{1,5},{5,1},{2,6},{6,2},{3,7},{7,3},{8,12},{12,8},{9,1... | collective-permute-start | bytes 6684680 | tf_op jit(solution)/shard_map/ppermute | solution.py:287
  82.3 8.3 %collective-permute-start.9 = (f32[136,128]{1,0:T(8,128)S(1)}, f32[136,128]{1,0:T(8,128)S(1)}, u32[]{:S(2)}, u32[]{:S(2)}) collective-permute-start(f32[136,128]{1,0:T(8,128)S(1)} %plane_sum_kernel.1.own), channel_id=1, source_target_pairs={{0,96},{32,192},{64,160},{96,0},{128,224},{160,64},{192,32},{224,1... | collective-permute-start | bytes 208904 | tf_op jit(solution)/shard_map/ppermute | solution.py:299
  86.4 7.3 %collective-permute-start.8 = (f32[136,128]{1,0:T(8,128)S(1)}, f32[136,128]{1,0:T(8,128)S(1)}, u32[]{:S(2)}, u32[]{:S(2)}) collective-permute-start(f32[136,128]{1,0:T(8,128)S(1)} %plane_sum_kernel.1.own), channel_id=1, source_target_pairs={{0,128},{32,160},{64,192},{96,224},{128,0},{160,32},{192,64},{224,... | collective-permute-start | bytes 208904 | tf_op jit(solution)/shard_map/ppermute | solution.py:299
  90.6 5.4 %collective-permute-start.7 = (f32[136,128]{1,0:T(8,128)S(1)}, f32[136,128]{1,0:T(8,128)S(1)}, u32[]{:S(2)}, u32[]{:S(2)}) collective-permute-start(f32[136,128]{1,0:T(8,128)S(1)} %plane_sum_kernel.1.own), channel_id=1, source_target_pairs={{0,224},{32,64},{64,32},{96,128},{128,96},{160,192},{192,160},{224... | collective-permute-start | bytes 208904 | tf_op jit(solution)/shard_map/ppermute | solution.py:299
  126.0 9.0 %collective-permute-start.10 = (f32[32,136,128]{2,1,0:T(8,128)S(1)}, f32[32,136,128]{2,1,0:T(8,128)S(1)}, u32[]{:S(2)}, u32[]{:S(2)}) collective-permute-start(f32[32,136,128]{2,1,0:T(8,128)S(1)} %all_to_all.11.mine), channel_id=1, source_target_pairs={{0,4},{4,0},{1,5},{5,1},{2,6},{6,2},{3,7},{7,3},{8,12},{12,8},{9,1... | collective-permute-start | bytes 6684680 | tf_op jit(solution)/shard_map/ppermute | solution.py:287

commit v4 on v3

--- a/solution.py
+++ b/solution.py
@@ -22,7 +22,8 @@
 
 VMEM = pl.BlockSpec(memory_space=pltpu.VMEM)
 SMEM = pl.BlockSpec(memory_space=pltpu.SMEM)
-HBM = pl.BlockSpec(memory_space=pltpu.MemorySpace.HBM)
+FAR = pltpu.MemorySpace.HBM
+HBM = pl.BlockSpec(memory_space=FAR)
 
 
 def dot(a, b):
@@ -40,7 +41,10 @@
 def kernel_call(body, outs, inputs, scratch=(), scalars=0, far=(), far_outs=(), aliases=None):
     return pl.pallas_call(
         body,
-        out_shape=tuple(jax.ShapeDtypeStruct(s, d) for s, d in outs),
+        out_shape=tuple(
+            FAR(s, d) if i in far_outs else jax.ShapeDtypeStruct(s, d)
+            for i, (s, d) in enumerate(outs)
+        ),
         in_specs=[
             SMEM if i < scalars else HBM if i in far else VMEM for i in range(len(inputs))
         ],
@@ -49,7 +53,7 @@
         input_output_aliases=aliases or {},
         name=body.__name__,
         compiler_params=pltpu.CompilerParams(vmem_limit_bytes=16 * 1024 * 1024),
-    )(*inputs)
+    )(*(pltpu.with_memory_space_constraint(x, FAR) if i in far else x for i, x in enumerate(inputs)))
 
 
 def started(source, target, sem):

time: 138 us -> 127 us (0.920)
  local copies, waits for them, and re-layouts: 12.8 us -> 0 us
    unnamed x30 -> x0, local copies, waits for them, and re-layouts: 12.8 us -> none
  transfers between devices with their start and end apart: 11 -> 11, of which waited for: 6 -> 8; matrix products, arithmetic and copies ran while one was open for 0% -> 0% of each run, Pallas kernels for 2% -> 3%
where the time goes in v4:
time: 127 us
  blocking collectives  67.3 us (53%)
  starting transfers between devices  26.2 us (21%)
  Pallas kernels  17.8 us (14%)
  waiting for transfers between devices  14.8 us (12%)
    all_to_all x2, blocking collectives, swapped(): return lax.all_to_all(tiles, axis, split_axis=0, concat_axis=0, tiled=True)  67.3 us
    ppermute x8, starting transfers between devices, shifted(): lax.ppermute(array, axis, [(i, (i + by) % size) for i in range(size)])  18.1 us
    pallas_call x8, Pallas kernels, kernel_call(): pl.pallas_call(body, out_shape=tuple((FAR(s, d) if i in far_outs else jax...  17.8 us
    ppermute x8, waiting for transfers between devices, shifted(): lax.ppermute(array, axis, [(i, (i + by) % size) for i in range(size)])  9.33 us
    ppermute x3, starting transfers between devices, along_z(): return lax.ppermute(array, LINE, [(z, to(z)) for z in range(8)])  8.11 us
    ppermute x3, waiting for transfers between devices, along_z(): return lax.ppermute(array, LINE, [(z, to(z)) for z in range(8)])  5.48 us
  transfers between devices with their start and end apart: 11, of which 8 were waited for; matrix products, arithmetic and copies ran while one was open for 0% of the time, Pallas kernels for 3%

profile of v4, /device:TPU:1, one launch (start us, length us, event | category | flops | bytes accessed | tf_op | source)
XLA Modules:
  0.0 127.2 jit_solution(2963129048375536344)
XLA Ops:
  0.6 4.3 %unroll_kernel.1 = (bf16[640,1024]{1,0:T(8,128)(2,1)S(1)}, f32[512,1024]{1,0:T(8,128)}, f32[48,768]{1,0:T(8,128)S(1)}, f32[8,128]{1,0:T(8,128)S(1)}, s32[5,128]{1,0:T(8,128)S(1)}, /*index=5*/bf16[48,1024]{1,0:T(8,128)(2,1)S(1)}) custom-call(bf16[128,1024]{1,0:T(8,128)(2,1)} %emb_far.1, s32[5,128]{1,0:T(8,128)} %bitcast.11, bf16[1024,1024]{1,0:T(8,128)(2,1)} %refs_10_.1, ...), custom_call_target="tpu_custom_call" | custom-call | tf_op jit(solution)/shard_map/unroll_kernel/pallas_call | solution.py:42
  5.0 3.6 %collective-permute-start.2 = (f32[8,128]{1,0:T(8,128)S(1)}, f32[8,128]{1,0:T(8,128)S(1)}, u32[]{:S(2)}, u32[]{:S(2)}) collective-permute-start(f32[8,128]{1,0:T(8,128)S(1)} %get-tuple-element.27.refs_3_), channel_id=1, source_target_pairs={{0,3},{1,0},{2,1},{3,2},{4,7},{5,4},{6,5},{7,6},{8,11},{9,8},{10,9... | collective-permute-start | bytes 12296 | tf_op jit(solution)/shard_map/ppermute | solution.py:291
  8.6 0.0 collective-permute-start.1
  8.6 1.6 %collective-permute-start = (f32[8,128]{1,0:T(8,128)S(1)}, f32[8,128]{1,0:T(8,128)S(1)}, u32[]{:S(2)}, u32[]{:S(2)}) collective-permute-start(f32[8,128]{1,0:T(8,128)S(1)} %get-tuple-element.27.refs_3_), channel_id=1, source_target_pairs={{0,2},{1,3},{2,0},{3,1},{4,6},{5,7},{6,4},{7,5},{8,10},{9,11},{10,... | collective-permute-start | bytes 12296 | tf_op jit(solution)/shard_map/ppermute | solution.py:291
  10.2 1.5 %targets_kernel.1 = (f32[5,128]{1,0:T(8,128)}, f32[5,128]{1,0:T(8,128)S(1)}, bf16[1024,640]{1,0:T(8,128)(2,1)S(1)}) custom-call(f32[5,128]{1,0:T(8,128)} %bitcast.12, s32[5,128]{1,0:T(8,128)} %bitcast.13, f32[5,18,128]{2,1,0:T(8,128)} %bitcast.10, s32[5,128]{1,0:T(8,128)S(1)} %get-tuple-element.23.act.refs_0_.refs_1_, ...), custom_call_target="tpu_custom_call" | custom-call | tf_op jit(solution)/shard_map/targets_kernel/pallas_call | solution.py:42
  11.8 0.0 collective-permute-done.2.refs_6_
  11.8 0.5 collective-permute-done.1.refs_5_
  12.3 0.3 collective-permute-done.refs_4_
  12.6 0.2 weights_body.1
  12.7 2.7 %collective-permute-start.5 = (f32[8,128]{1,0:T(8,128)S(1)}, f32[8,128]{1,0:T(8,128)S(1)}, u32[]{:S(2)}, u32[]{:S(2)}) collective-permute-start(f32[8,128]{1,0:T(8,128)S(1)} %get-tuple-element.30.refs_4_), channel_id=1, source_target_pairs={{0,3},{1,0},{2,1},{3,2},{4,7},{5,4},{6,5},{7,6},{8,11},{9,8},{10,9... | collective-permute-start | bytes 12296 | tf_op jit(solution)/shard_map/ppermute | solution.py:291
  15.4 1.3 collective-permute-start.3
  16.7 0.1 pad_add_fusion.refs_0_.place
  16.8 0.0 collective-permute-done.5.refs_7_
  16.8 2.3 %collective-permute-done.4.refs_6_ = f32[8,128]{1,0:T(8,128)S(1)} collective-permute-done((f32[8,128]{1,0:T(8,128)S(1)}, f32[8,128]{1,0:T(8,128)S(1)}, u32[]{:S(2)}, u32[]{:S(2)}) %collective-permute-start.4) | collective-permute-done | bytes 4128 | tf_op jit(solution)/shard_map/ppermute | solution.py:291
  19.1 0.3 collective-permute-done.3.refs_5_
  19.4 6.8 %gradient_body.1 = (f32[32,136,128]{2,1,0:T(8,128)S(1)}, f32[32,136,128]{2,1,0:T(8,128)S(1)}) custom-call(s32[2]{0:T(128)S(1)} %pad_add_fusion.refs_0_.place, s32[5,128]{1,0:T(8,128)S(1)} %get-tuple-element.23.act.refs_0_.refs_1_, f32[48,640]{1,0:T(8,128)S(1)} %get-tuple-element.28.refs_2_, f32[24,640]{1,0:T(8,128)S(1)} %get-tuple-element.29.refs_3_, ...), custom_call_target="tpu_custom_call" | custom-call | tf_op jit(solution)/shard_map/gradient_body/pallas_call | solution.py:42
  26.2 3.9 %collective-permute-start.6 = (f32[32,136,128]{2,1,0:T(8,128)S(1)}, f32[32,136,128]{2,1,0:T(8,128)S(1)}, u32[]{:S(2)}, u32[]{:S(2)}) collective-permute-start(f32[32,136,128]{2,1,0:T(8,128)S(1)} %get-tuple-element.35), channel_id=1, source_target_pairs={{0,4},{4,0},{1,5},{5,1},{2,6},{6,2},{3,7},{7,3},{8,12},{12,8},{9,1... | collective-permute-start | bytes 6684680 | tf_op jit(solution)/shard_map/ppermute | solution.py:291
  30.1 4.0 %collective-permute-done.6 = f32[32,136,128]{2,1,0:T(8,128)S(1)} collective-permute-done((f32[32,136,128]{2,1,0:T(8,128)S(1)}, f32[32,136,128]{2,1,0:T(8,128)S(1)}, u32[]{:S(2)}, u32[]{:S(2)}) %collective-permute-start.6) | collective-permute-done | bytes 2228256 | tf_op jit(solution)/shard_map/ppermute | solution.py:291
  34.1 0.3 add.8
  34.4 37.6 %all_to_all.10.arrived = f32[32,136,128]{2,1,0:T(8,128)S(1)} all-to-all(f32[32,136,128]{2,1,0:T(8,128)S(1)} %add.8), channel_id=1, replica_groups=mesh['zh'=4,'zp'=2,'x'=4,'core'=2,'y'=4] {'zp','x','y'}, dimensions={0} | all-to-all | bytes 4456448 | tf_op jit(solution)/shard_map/all_to_all | solution.py:299
  72.0 0.1 plane_sum_kernel.1.own
  72.1 3.9 %collective-permute-start.9 = (f32[136,128]{1,0:T(8,128)S(1)}, f32[136,128]{1,0:T(8,128)S(1)}, u32[]{:S(2)}, u32[]{:S(2)}) collective-permute-start(f32[136,128]{1,0:T(8,128)S(1)} %plane_sum_kernel.1.own), channel_id=1, source_target_pairs={{0,96},{32,192},{64,160},{96,0},{128,224},{160,64},{192,32},{224,1... | collective-permute-start | bytes 208904 | tf_op jit(solution)/shard_map/ppermute | solution.py:303
  76.0 4.2 %collective-permute-start.8 = (f32[136,128]{1,0:T(8,128)S(1)}, f32[136,128]{1,0:T(8,128)S(1)}, u32[]{:S(2)}, u32[]{:S(2)}) collective-permute-start(f32[136,128]{1,0:T(8,128)S(1)} %plane_sum_kernel.1.own), channel_id=1, source_target_pairs={{0,128},{32,160},{64,192},{96,224},{128,0},{160,32},{192,64},{224,... | collective-permute-start | bytes 208904 | tf_op jit(solution)/shard_map/ppermute | solution.py:303
  80.2 0.0 collective-permute-start.7
  80.2 3.1 %collective-permute-done.8.far = f32[136,128]{1,0:T(8,128)S(1)} collective-permute-done((f32[136,128]{1,0:T(8,128)S(1)}, f32[136,128]{1,0:T(8,128)S(1)}, u32[]{:S(2)}, u32[]{:S(2)}) %collective-permute-start.8) | collective-permute-done | bytes 69664 | tf_op jit(solution)/shard_map/ppermute | solution.py:303
  83.3 2.4 %collective-permute-done.7.near = f32[136,128]{1,0:T(8,128)S(1)} collective-permute-done((f32[136,128]{1,0:T(8,128)S(1)}, f32[136,128]{1,0:T(8,128)S(1)}, u32[]{:S(2)}, u32[]{:S(2)}) %collective-permute-start.7) | collective-permute-done | bytes 69664 | tf_op jit(solution)/shard_map/ppermute | solution.py:303
  85.7 0.1 line_sum_kernel.1
  85.8 29.7 %all_to_all.11.mine = f32[32,136,128]{2,1,0:T(8,128)S(1)} all-to-all(f32[32,136,128]{2,1,0:T(8,128)S(1)} %line_sum_kernel.1), channel_id=1, replica_groups=mesh['zh'=4,'zp'=2,'x'=4,'core'=2,'y'=4] {'zp','x','y'}, dimensions={0} | all-to-all | bytes 4456448 | tf_op jit(solution)/shard_map/all_to_all | solution.py:299
  115.5 5.0 %collective-permute-start.10 = (f32[32,136,128]{2,1,0:T(8,128)S(1)}, f32[32,136,128]{2,1,0:T(8,128)S(1)}, u32[]{:S(2)}, u32[]{:S(2)}) collective-permute-start(f32[32,136,128]{2,1,0:T(8,128)S(1)} %all_to_all.11.mine), channel_id=1, source_target_pairs={{0,4},{4,0},{1,5},{5,1},{2,6},{6,2},{3,7},{7,3},{8,12},{12,8},{9,1... | collective-permute-start | bytes 6684680 | tf_op jit(solution)/shard_map/ppermute | solution.py:291
  120.5 2.0 %first_half_kernel.1 = (f32[1024,1024]{1,0:T(8,128)}, f32[64,1024]{1,0:T(8,128)S(1)}) custom-call(s32[2]{0:T(128)S(1)} %pad_add_fusion.refs_0_.place, f32[32,136,128]{2,1,0:T(8,128)S(1)} %all_to_all.11.mine), custom_call_target="tpu_custom_call" | custom-call | tf_op jit(solution)/shard_map/first_half_kernel/pallas_call | solution.py:42
  122.5 2.0 %collective-permute-done.10.other = f32[32,136,128]{2,1,0:T(8,128)S(1)} collective-permute-done((f32[32,136,128]{2,1,0:T(8,128)S(1)}, f32[32,136,128]{2,1,0:T(8,128)S(1)}, u32[]{:S(2)}, u32[]{:S(2)}) %collective-permute-start.10) | collective-permute-done | bytes 2228256 | tf_op jit(solution)/shard_map/ppermute | solution.py:291
  124.5 2.7 %second_half_kernel.1 = (f32[1024,1024]{1,0:T(8,128)}, f32[18,1024]{1,0:T(8,128)}, f32[36,1024]{1,0:T(8,128)}) custom-call(s32[2]{0:T(128)S(1)} %pad_add_fusion.refs_0_.place, f32[32,136,128]{2,1,0:T(8,128)S(1)} %collective-permute-done.10.other, f32[64,1024]{1,0:T(8,128)S(1)} %get-tuple-element.36.e_in, ...), custom_call_target="tpu_custom_call", output_to_operand_aliasing={{0}: (3, {})} | custom-call | tf_op jit(solution)/shard_map/second_half_kernel/pallas_call | solution.py:42
  (2 shorter events, 0.0 us)
Async XLA Ops:
  5.0 6.8 %collective-permute-start.2 = (f32[8,128]{1,0:T(8,128)S(1)}, f32[8,128]{1,0:T(8,128)S(1)}, u32[]{:S(2)}, u32[]{:S(2)}) collective-permute-start(f32[8,128]{1,0:T(8,128)S(1)} %get-tuple-element.27.refs_3_), channel_id=1, source_target_pairs={{0,3},{1,0},{2,1},{3,2},{4,7},{5,4},{6,5},{7,6},{8,11},{9,8},{10,9... | collective-permute-start | bytes 12296 | tf_op jit(solution)/shard_map/ppermute | solution.py:291
  8.6 3.7 %collective-permute-start.1 = (f32[8,128]{1,0:T(8,128)S(1)}, f32[8,128]{1,0:T(8,128)S(1)}, u32[]{:S(2)}, u32[]{:S(2)}) collective-permute-start(f32[8,128]{1,0:T(8,128)S(1)} %get-tuple-element.27.refs_3_), channel_id=1, source_target_pairs={{0,1},{1,2},{2,3},{3,0},{4,5},{5,6},{6,7},{7,4},{8,9},{9,10},{10,1... | collective-permute-start | bytes 12296 | tf_op jit(solution)/shard_map/ppermute | solution.py:291
  8.6 4.0 %collective-permute-start = (f32[8,128]{1,0:T(8,128)S(1)}, f32[8,128]{1,0:T(8,128)S(1)}, u32[]{:S(2)}, u32[]{:S(2)}) collective-permute-start(f32[8,128]{1,0:T(8,128)S(1)} %get-tuple-element.27.refs_3_), channel_id=1, source_target_pairs={{0,2},{1,3},{2,0},{3,1},{4,6},{5,7},{6,4},{7,5},{8,10},{9,11},{10,... | collective-permute-start | bytes 12296 | tf_op jit(solution)/shard_map/ppermute | solution.py:291
  12.7 4.0 %collective-permute-start.5 = (f32[8,128]{1,0:T(8,128)S(1)}, f32[8,128]{1,0:T(8,128)S(1)}, u32[]{:S(2)}, u32[]{:S(2)}) collective-permute-start(f32[8,128]{1,0:T(8,128)S(1)} %get-tuple-element.30.refs_4_), channel_id=1, source_target_pairs={{0,3},{1,0},{2,1},{3,2},{4,7},{5,4},{6,5},{7,6},{8,11},{9,8},{10,9... | collective-permute-start | bytes 12296 | tf_op jit(solution)/shard_map/ppermute | solution.py:291
  15.4 3.7 %collective-permute-start.4 = (f32[8,128]{1,0:T(8,128)S(1)}, f32[8,128]{1,0:T(8,128)S(1)}, u32[]{:S(2)}, u32[]{:S(2)}) collective-permute-start(f32[8,128]{1,0:T(8,128)S(1)} %get-tuple-element.30.refs_4_), channel_id=1, source_target_pairs={{0,1},{1,2},{2,3},{3,0},{4,5},{5,6},{6,7},{7,4},{8,9},{9,10},{10,1... | collective-permute-start | bytes 12296 | tf_op jit(solution)/shard_map/ppermute | solution.py:291
  15.4 4.0 %collective-permute-start.3 = (f32[8,128]{1,0:T(8,128)S(1)}, f32[8,128]{1,0:T(8,128)S(1)}, u32[]{:S(2)}, u32[]{:S(2)}) collective-permute-start(f32[8,128]{1,0:T(8,128)S(1)} %get-tuple-element.30.refs_4_), channel_id=1, source_target_pairs={{0,2},{1,3},{2,0},{3,1},{4,6},{5,7},{6,4},{7,5},{8,10},{9,11},{10,... | collective-permute-start | bytes 12296 | tf_op jit(solution)/shard_map/ppermute | solution.py:291
  26.2 7.9 %collective-permute-start.6 = (f32[32,136,128]{2,1,0:T(8,128)S(1)}, f32[32,136,128]{2,1,0:T(8,128)S(1)}, u32[]{:S(2)}, u32[]{:S(2)}) collective-permute-start(f32[32,136,128]{2,1,0:T(8,128)S(1)} %get-tuple-element.35), channel_id=1, source_target_pairs={{0,4},{4,0},{1,5},{5,1},{2,6},{6,2},{3,7},{7,3},{8,12},{12,8},{9,1... | collective-permute-start | bytes 6684680 | tf_op jit(solution)/shard_map/ppermute | solution.py:291
  72.1 8.1 %collective-permute-start.9 = (f32[136,128]{1,0:T(8,128)S(1)}, f32[136,128]{1,0:T(8,128)S(1)}, u32[]{:S(2)}, u32[]{:S(2)}) collective-permute-start(f32[136,128]{1,0:T(8,128)S(1)} %plane_sum_kernel.1.own), channel_id=1, source_target_pairs={{0,96},{32,192},{64,160},{96,0},{128,224},{160,64},{192,32},{224,1... | collective-permute-start | bytes 208904 | tf_op jit(solution)/shard_map/ppermute | solution.py:303
  76.0 7.3 %collective-permute-start.8 = (f32[136,128]{1,0:T(8,128)S(1)}, f32[136,128]{1,0:T(8,128)S(1)}, u32[]{:S(2)}, u32[]{:S(2)}) collective-permute-start(f32[136,128]{1,0:T(8,128)S(1)} %plane_sum_kernel.1.own), channel_id=1, source_target_pairs={{0,128},{32,160},{64,192},{96,224},{128,0},{160,32},{192,64},{224,... | collective-permute-start | bytes 208904 | tf_op jit(solution)/shard_map/ppermute | solution.py:303
  80.2 5.5 %collective-permute-start.7 = (f32[136,128]{1,0:T(8,128)S(1)}, f32[136,128]{1,0:T(8,128)S(1)}, u32[]{:S(2)}, u32[]{:S(2)}) collective-permute-start(f32[136,128]{1,0:T(8,128)S(1)} %plane_sum_kernel.1.own), channel_id=1, source_target_pairs={{0,224},{32,64},{64,32},{96,128},{128,96},{160,192},{192,160},{224... | collective-permute-start | bytes 208904 | tf_op jit(solution)/shard_map/ppermute | solution.py:303
  115.5 9.0 %collective-permute-start.10 = (f32[32,136,128]{2,1,0:T(8,128)S(1)}, f32[32,136,128]{2,1,0:T(8,128)S(1)}, u32[]{:S(2)}, u32[]{:S(2)}) collective-permute-start(f32[32,136,128]{2,1,0:T(8,128)S(1)} %all_to_all.11.mine), channel_id=1, source_target_pairs={{0,4},{4,0},{1,5},{5,1},{2,6},{6,2},{3,7},{7,3},{8,12},{12,8},{9,1... | collective-permute-start | bytes 6684680 | tf_op jit(solution)/shard_map/ppermute | solution.py:291

commit v5 on v4

--- a/solution.py
+++ b/solution.py
@@ -180,18 +180,18 @@
     mass_out[...] = jnp.broadcast_to(jnp.sum(mass_sum, axis=1, keepdims=True), mass_out.shape)
 
 
+def fetch_kernel(t_far, wh_far, after, t, wh, sem):
+    for copy in (started(t_far, t, sem.at[0]), started(wh_far, wh, sem.at[1])):
+        copy.wait()
+
+
 def gradient_kernel(
-    groups, count, place, act, a, b, m0, m1, m2, m3, sT, t_far, wh_far, whp,
-    mine, other, gf, g, x, oh, e, t, wh, sem,
+    groups, count, place, act, a, b, m0, m1, m2, m3, sT, t, wh, whp,
+    other, x, e, gf, g, oh,
 ):
     steps, rows = act.shape
     last = steps - 1
     spans = [slice(k * rows, (k + 1) * rows) for k in range(steps)]
-    loads = {}
-    for k in range(last - 1, -1, -1):
-        loads[k] = started(t_far.at[spans[k], :], t.at[spans[k], :], sem.at[k])
-        if k == last - 1:
-            whole = started(wh_far, wh, sem.at[last])
     total = m0[0:1, 0:1] + m1[0:1, 0:1] + m2[0:1, 0:1] + m3[0:1, 0:1]
     mean = total / (groups * rows * steps)
     gf[...] = a[...]
@@ -205,36 +205,40 @@
     e[count : 2 * count, :] = heads[Q_ROW : Q_ROW + count, :]
     r = dot_tn(g[:, spans[last]], whp[...])
     for k in range(last - 1, -1, -1):
-        loads[k].wait()
         tk = t[spans[k], :]
         xk = (r * (1.0 - tk * tk)).astype(BF16)
         x[spans[k], :] = xk
-        if k == last - 1:
-            whole.wait()
         if k > 0:
             r = r + (dot_nt(xk, wh[...]) + dot_tn(g[:, spans[k]], whp[...]))
     inner = last * rows
     e[A_ROW : A_ROW + count, :] = dot(oh[...], x[...])[0:count, :]
+    tile_half(place, 1 - place[0], sT, x, e, other)
+
+
+def tile_half(place, h, sT, x, e, out):
     hid = sT.shape[0]
     half = hid // 2
-    core, flip = place[0], place[1]
-    for out, h in ((other, 1 - core), (mine, core)):
-        left = sT[pl.ds(pl.multiple_of(h * half, half), half), :inner]
-        for j in range(0, hid, 256):
-            block = dot(left, x[:, j : j + 256])
-            for p in range(2):
-                slot = pl.ds((flip + p - 2 * flip * p) * 16, 16)
-                for c in range(2):
-                    n = j // LANES + c
-                    out[slot, n * 16 : (n + 1) * 16, :] = block[
-                        p * 256 : (p + 1) * 256, c * LANES : (c + 1) * LANES
-                    ].reshape(16, 16, LANES)
-        for i in range(4):
-            p = i // 2
-            slot = (flip + p - 2 * flip * p) * 16 + (i % 2) * 8
-            rows8 = e[pl.ds(pl.multiple_of(h * 32 + i * 8, 8), 8), :]
-            for n in range(8):
-                out[slot + n, 128:136, :] = rows8[:, n * LANES : (n + 1) * LANES]
+    flip = place[1]
+    left = sT[pl.ds(pl.multiple_of(h * half, half), half), : x.shape[0]]
+    for j in range(0, hid, 256):
+        block = dot(left, x[:, j : j + 256])
+        for p in range(2):
+            slot = pl.ds((flip + p - 2 * flip * p) * 16, 16)
+            for c in range(2):
+                n = j // LANES + c
+                out[slot, n * 16 : (n + 1) * 16, :] = block[
+                    p * 256 : (p + 1) * 256, c * LANES : (c + 1) * LANES
+                ].reshape(16, 16, LANES)
+    for i in range(4):
+        p = i // 2
+        slot = (flip + p - 2 * flip * p) * 16 + (i % 2) * 8
+        rows8 = e[pl.ds(pl.multiple_of(h * 32 + i * 8, 8), 8), :]
+        for n in range(8):
+            out[slot + n, 128:136, :] = rows8[:, n * LANES : (n + 1) * LANES]
+
+
+def mine_kernel(place, sT, x, e, out):
+    tile_half(place, place[0], sT, x, e, out)
 
 
 def plane_sum_kernel(arrived, out):
@@ -250,19 +254,21 @@
         out[i] = total
 
 
-def lay_out(place, part, h, gh_far, buf, e, sem):
-    half = gh_far.shape[0] // 2
+def lay_out(place, part, h, gh_far, e, sem):
+    units = part.shape[0]
     flip = place[1]
     copies = []
     for p in range(2):
         slot = pl.ds((flip + p - 2 * flip * p) * 16, 16)
-        here = slice(p * 256, (p + 1) * 256)
+        at = pl.ds(h * units + p * 16, 16)
         for n in range(8):
-            buf[here, n * LANES : (n + 1) * LANES] = part[
-                slot, n * 16 : (n + 1) * 16, :
-            ].reshape(256, LANES)
-        at = pl.ds(pl.multiple_of(h * half + p * 256, 256), 256)
-        copies.append(started(buf.at[here, :], gh_far.at[at, :], sem.at[p]))
+            copies.append(
+                started(
+                    part.at[slot, n * 16 : (n + 1) * 16, :],
+                    gh_far.at[at, :, n * LANES : (n + 1) * LANES],
+                    sem.at[p * 8 + n],
+                )
+            )
     for i in range(4):
         p = i // 2
         slot = (flip + p - 2 * flip * p) * 16 + (i % 2) * 8
@@ -272,16 +278,19 @@
     return copies
 
 
-def first_half_kernel(place, mine, gh_far, e, buf, sem):
-    for copy in lay_out(place, mine, place[0], gh_far, buf, e, sem):
+def first_half_kernel(place, mine, gh_far, e, sem):
+    e[...] = jnp.zeros_like(e)
+    for copy in lay_out(place, mine, place[0], gh_far, e, sem):
         copy.wait()
 
 
-def second_half_kernel(place, other, e_in, gh_in, gh_far, ga, gd, buf, e, sem):
+def second_half_kernel(place, other, e_in, gh_in, gh_far, ga_far, gd_far, e, ga, gd, sem):
     e[...] = e_in[...]
-    copies = lay_out(place, other, 1 - place[0], gh_far, buf, e, sem)
+    copies = lay_out(place, other, 1 - place[0], gh_far, e, sem)
     ga[...] = e[A_ROW : A_ROW + ga.shape[0], :]
+    copies.append(started(ga, ga_far, sem.at[16]))
     gd[...] = e[0 : gd.shape[0], :]
+    copies.append(started(gd, gd_far, sem.at[17]))
     for copy in copies:
         copy.wait()
 
@@ -370,28 +379,32 @@
     )
     masses = of_group(mass)
 
+    t, wh = kernel_call(
+        fetch_kernel,
+        [(t.shape, F32), (w_hidden.shape, BF16)],
+        (t, w_hidden, mass),
+        (pltpu.SemaphoreType.DMA((2,)),),
+        far=(0, 1),
+    )
+
     def gradient_body(*refs):
         gradient_kernel(groups, count, *refs)
 
     parts = ((32, 136, LANES), F32)
-    mine, other = kernel_call(
+    other, x, extra = kernel_call(
         gradient_body,
-        [parts, parts],
-        (place, act, a, b, *masses, sT, t, w_hidden, whp),
+        [parts, (((steps - 1) * rows, hid), BF16), ((64, hid), F32)],
+        (place, act, a, b, *masses, sT, t, wh, whp),
         (
             pltpu.VMEM((48, steps * rows), F32),
             pltpu.VMEM((48, steps * rows), BF16),
-            pltpu.VMEM(((steps - 1) * rows, hid), BF16),
             pltpu.VMEM((32, (steps - 1) * rows), BF16),
-            pltpu.VMEM((64, hid), F32),
-            pltpu.VMEM(((steps - 1) * rows, hid), F32),
-            pltpu.VMEM((hid, hid), BF16),
-            pltpu.SemaphoreType.DMA((steps,)),
         ),
         scalars=1,
-        far=(9, 10),
-    )
-    chip = mine + shifted(other, "core", 1)
+    )
+    arriving = shifted(other, "core", 1)
+    (mine,) = kernel_call(mine_kernel, [parts], (place, sT, x, extra), scalars=1)
+    chip = mine + arriving
     (own,) = kernel_call(plane_sum_kernel, [((136, LANES), F32)], (swapped(chip, NEAR),))
     far = along_z(own, across)
     both = along_z(own, lambda z: across(beside(z)))
@@ -399,26 +412,32 @@
     (whole,) = kernel_call(line_sum_kernel, [parts], (own, near, far, both))
     mine = swapped(whole, NEAR)
     other = shifted(mine, "core", 1)
-    staging = (pltpu.VMEM((hid // 2, hid), F32), pltpu.SemaphoreType.DMA((2,)))
+    copied = pltpu.SemaphoreType.DMA((16,))
+    tiles = ((64, 16, hid), F32)
     partly, extra = kernel_call(
         first_half_kernel,
-        [((hid, hid), F32), ((64, hid), F32)],
+        [tiles, ((64, hid), F32)],
         (place, mine),
-        staging,
+        (copied,),
         scalars=1,
         far_outs=(0,),
     )
     grad_hidden, grad_action, grad_heads = kernel_call(
         second_half_kernel,
-        [((hid, hid), F32), (w_action.shape, F32), (w_heads.shape[::-1], F32)],
+        [tiles, (w_action.shape, F32), (w_heads.shape[::-1], F32)],
         (place, other, extra, partly),
-        (staging[0], pltpu.VMEM((64, hid), F32), staging[1]),
+        (
+            pltpu.VMEM((64, hid), F32),
+            pltpu.VMEM(w_action.shape, F32),
+            pltpu.VMEM(w_heads.shape[::-1], F32),
+            pltpu.SemaphoreType.DMA((18,)),
+        ),
         scalars=1,
         far=(3,),
-        far_outs=(0,),
+        far_outs=(0, 1, 2),
         aliases={3: 0},
     )
-    return (grad_hidden, grad_action, grad_heads.T, targets.T)
+    return (grad_hidden.reshape(hid, hid), grad_action, grad_heads.T, targets.T)
 
 
 def solution(mesh):

time: 127 us -> 124 us (0.976)
  waiting for transfers between devices: 14.8 us -> 11.2 us
    ppermute x8, waiting for transfers between devices: 9.33 us -> 5.75 us  [shifted(): lax.ppermute(array, axis, [(i, (i + by) % size) for i in range(size)])]
    pallas_call x8 -> x10, Pallas kernels: 17.8 us -> 18.3 us  [kernel_call(): pl.pallas_call(body, out_shape=tuple((FAR(s, d) if i in far_outs else jax...]
  transfers between devices with their start and end apart: 11 -> 11, of which waited for: 8 -> 8; matrix products, arithmetic and copies ran while one was open for 0% -> 0% of each run, Pallas kernels for 3% -> 6%
where the time goes in v5:
time: 124 us
  blocking collectives  67.3 us (54%)
  starting transfers between devices  26.2 us (21%)
  Pallas kernels  18.3 us (15%)
  waiting for transfers between devices  11.2 us (9%)
    all_to_all x2, blocking collectives, swapped(): return lax.all_to_all(tiles, axis, split_axis=0, concat_axis=0, tiled=True)  67.3 us
    pallas_call x10, Pallas kernels, kernel_call(): pl.pallas_call(body, out_shape=tuple((FAR(s, d) if i in far_outs else jax...  18.3 us
    ppermute x8, starting transfers between devices, shifted(): lax.ppermute(array, axis, [(i, (i + by) % size) for i in range(size)])  18.1 us
    ppermute x3, starting transfers between devices, along_z(): return lax.ppermute(array, LINE, [(z, to(z)) for z in range(8)])  8.11 us
    ppermute x8, waiting for transfers between devices, shifted(): lax.ppermute(array, axis, [(i, (i + by) % size) for i in range(size)])  5.75 us
    ppermute x3, waiting for transfers between devices, along_z(): return lax.ppermute(array, LINE, [(z, to(z)) for z in range(8)])  5.46 us
  transfers between devices with their start and end apart: 11, of which 8 were waited for; matrix products, arithmetic and copies ran while one was open for 0% of the time, Pallas kernels for 6%

profile of v5, /device:TPU:1, one launch (start us, length us, event | category | flops | bytes accessed | tf_op | source)
XLA Modules:
  0.0 124.1 jit_solution(10828650114487190876)
XLA Ops:
  0.6 4.3 %unroll_kernel.1 = (bf16[640,1024]{1,0:T(8,128)(2,1)S(1)}, f32[512,1024]{1,0:T(8,128)}, f32[48,768]{1,0:T(8,128)S(1)}, f32[8,128]{1,0:T(8,128)S(1)}, s32[5,128]{1,0:T(8,128)S(1)}, /*index=5*/bf16[48,1024]{1,0:T(8,128)(2,1)S(1)}) custom-call(bf16[128,1024]{1,0:T(8,128)(2,1)} %emb_far.1, s32[5,128]{1,0:T(8,128)} %bitcast.13, bf16[1024,1024]{1,0:T(8,128)(2,1)} %wh_far.3, ...), custom_call_target="tpu_custom_call" | custom-call | tf_op jit(solution)/shard_map/unroll_kernel/pallas_call | solution.py:42
  5.0 3.6 %collective-permute-start.2 = (f32[8,128]{1,0:T(8,128)S(1)}, f32[8,128]{1,0:T(8,128)S(1)}, u32[]{:S(2)}, u32[]{:S(2)}) collective-permute-start(f32[8,128]{1,0:T(8,128)S(1)} %get-tuple-element.31.refs_3_), channel_id=1, source_target_pairs={{0,3},{1,0},{2,1},{3,2},{4,7},{5,4},{6,5},{7,6},{8,11},{9,8},{10,9... | collective-permute-start | bytes 12296 | tf_op jit(solution)/shard_map/ppermute | solution.py:300
  8.6 0.0 collective-permute-start.1
  8.6 1.6 %collective-permute-start = (f32[8,128]{1,0:T(8,128)S(1)}, f32[8,128]{1,0:T(8,128)S(1)}, u32[]{:S(2)}, u32[]{:S(2)}) collective-permute-start(f32[8,128]{1,0:T(8,128)S(1)} %get-tuple-element.31.refs_3_), channel_id=1, source_target_pairs={{0,2},{1,3},{2,0},{3,1},{4,6},{5,7},{6,4},{7,5},{8,10},{9,11},{10,... | collective-permute-start | bytes 12296 | tf_op jit(solution)/shard_map/ppermute | solution.py:300
  10.2 1.5 %targets_kernel.1 = (f32[5,128]{1,0:T(8,128)}, f32[5,128]{1,0:T(8,128)S(1)}, bf16[1024,640]{1,0:T(8,128)(2,1)S(1)}) custom-call(f32[5,128]{1,0:T(8,128)} %bitcast.14, s32[5,128]{1,0:T(8,128)} %bitcast.15, f32[5,18,128]{2,1,0:T(8,128)} %bitcast.12, s32[5,128]{1,0:T(8,128)S(1)} %get-tuple-element.26.act.refs_0_.refs_1_, ...), custom_call_target="tpu_custom_call" | custom-call | tf_op jit(solution)/shard_map/targets_kernel/pallas_call | solution.py:42
  11.8 0.5 collective-permute-done.1.refs_5_
  12.3 0.3 collective-permute-done.refs_4_
  12.6 0.2 weights_body.1
  12.7 2.7 %collective-permute-start.5 = (f32[8,128]{1,0:T(8,128)S(1)}, f32[8,128]{1,0:T(8,128)S(1)}, u32[]{:S(2)}, u32[]{:S(2)}) collective-permute-start(f32[8,128]{1,0:T(8,128)S(1)} %get-tuple-element.34.after.refs_4_), channel_id=1, source_target_pairs={{0,3},{1,0},{2,1},{3,2},{4,7},{5,4},{6,5},{7,6},{8,11},{9,8},{10,9... | collective-permute-start | bytes 12296 | tf_op jit(solution)/shard_map/ppermute | solution.py:300
  15.4 0.0 collective-permute-start.4
  15.4 1.3 %collective-permute-start.3 = (f32[8,128]{1,0:T(8,128)S(1)}, f32[8,128]{1,0:T(8,128)S(1)}, u32[]{:S(2)}, u32[]{:S(2)}) collective-permute-start(f32[8,128]{1,0:T(8,128)S(1)} %get-tuple-element.34.after.refs_4_), channel_id=1, source_target_pairs={{0,2},{1,3},{2,0},{3,1},{4,6},{5,7},{6,4},{7,5},{8,10},{9,11},{10,... | collective-permute-start | bytes 12296 | tf_op jit(solution)/shard_map/ppermute | solution.py:300
  16.7 0.1 pad_add_fusion.refs_0_.place
  16.8 2.2 %fetch_kernel.1 = (f32[512,1024]{1,0:T(8,128)S(1)}, bf16[1024,1024]{1,0:T(8,128)(2,1)S(1)}) custom-call(f32[512,1024]{1,0:T(8,128)} %get-tuple-element.35.t_far, bf16[1024,1024]{1,0:T(8,128)(2,1)} %wh_far.3, f32[8,128]{1,0:T(8,128)S(1)} %get-tuple-element.34.after.refs_4_), custom_call_target="tpu_custom_call" | custom-call | tf_op jit(solution)/shard_map/fetch_kernel/pallas_call | solution.py:42
  19.0 0.1 collective-permute-done.4.refs_6_
  19.1 0.3 collective-permute-done.3.refs_5_
  19.4 4.4 %gradient_body.1 = (f32[32,136,128]{2,1,0:T(8,128)S(1)}, bf16[512,1024]{1,0:T(8,128)(2,1)S(1)}, f32[64,1024]{1,0:T(8,128)S(1)}) custom-call(s32[2]{0:T(128)S(1)} %pad_add_fusion.refs_0_.place, s32[5,128]{1,0:T(8,128)S(1)} %get-tuple-element.26.act.refs_0_.refs_1_, f32[48,640]{1,0:T(8,128)S(1)} %get-tuple-element.32.refs_2_, ...), custom_call_target="tpu_custom_call" | custom-call | tf_op jit(solution)/shard_map/gradient_body/pallas_call | solution.py:42
  23.8 3.9 %collective-permute-start.6 = (f32[32,136,128]{2,1,0:T(8,128)S(1)}, f32[32,136,128]{2,1,0:T(8,128)S(1)}, u32[]{:S(2)}, u32[]{:S(2)}) collective-permute-start(f32[32,136,128]{2,1,0:T(8,128)S(1)} %get-tuple-element.41), channel_id=1, source_target_pairs={{0,4},{4,0},{1,5},{5,1},{2,6},{6,2},{3,7},{7,3},{8,12},{12,8},{9,1... | collective-permute-start | bytes 6684680 | tf_op jit(solution)/shard_map/ppermute | solution.py:300
  27.7 1.3 %mine_kernel.1 = f32[32,136,128]{2,1,0:T(8,128)S(1)} custom-call(s32[2]{0:T(128)S(1)} %pad_add_fusion.refs_0_.place, bf16[1024,640]{1,0:T(8,128)(2,1)S(1)} %get-tuple-element.29.refs_8_.sT, bf16[512,1024]{1,0:T(8,128)(2,1)S(1)} %get-tuple-element.39.x, f32[64,1024]{1,0:T(8,128)S(1)} %get-tuple-element.40.e), custom_call_target="tpu_custom_call" | custom-call | tf_op jit(solution)/shard_map/mine_kernel/pallas_call | solution.py:42
  29.0 2.6 %collective-permute-done.6 = f32[32,136,128]{2,1,0:T(8,128)S(1)} collective-permute-done((f32[32,136,128]{2,1,0:T(8,128)S(1)}, f32[32,136,128]{2,1,0:T(8,128)S(1)}, u32[]{:S(2)}, u32[]{:S(2)}) %collective-permute-start.6) | collective-permute-done | bytes 2228256 | tf_op jit(solution)/shard_map/ppermute | solution.py:300
  31.6 0.3 add.8
  31.9 37.6 %all_to_all.10.arrived = f32[32,136,128]{2,1,0:T(8,128)S(1)} all-to-all(f32[32,136,128]{2,1,0:T(8,128)S(1)} %add.8), channel_id=1, replica_groups=mesh['zh'=4,'zp'=2,'x'=4,'core'=2,'y'=4] {'zp','x','y'}, dimensions={0} | all-to-all | bytes 4456448 | tf_op jit(solution)/shard_map/all_to_all | solution.py:308
  69.5 0.1 plane_sum_kernel.1.own
  69.6 3.9 %collective-permute-start.9 = (f32[136,128]{1,0:T(8,128)S(1)}, f32[136,128]{1,0:T(8,128)S(1)}, u32[]{:S(2)}, u32[]{:S(2)}) collective-permute-start(f32[136,128]{1,0:T(8,128)S(1)} %plane_sum_kernel.1.own), channel_id=1, source_target_pairs={{0,96},{32,192},{64,160},{96,0},{128,224},{160,64},{192,32},{224,1... | collective-permute-start | bytes 208904 | tf_op jit(solution)/shard_map/ppermute | solution.py:312
  73.5 4.2 %collective-permute-start.8 = (f32[136,128]{1,0:T(8,128)S(1)}, f32[136,128]{1,0:T(8,128)S(1)}, u32[]{:S(2)}, u32[]{:S(2)}) collective-permute-start(f32[136,128]{1,0:T(8,128)S(1)} %plane_sum_kernel.1.own), channel_id=1, source_target_pairs={{0,128},{32,160},{64,192},{96,224},{128,0},{160,32},{192,64},{224,... | collective-permute-start | bytes 208904 | tf_op jit(solution)/shard_map/ppermute | solution.py:312
  77.7 3.1 %collective-permute-done.8.far = f32[136,128]{1,0:T(8,128)S(1)} collective-permute-done((f32[136,128]{1,0:T(8,128)S(1)}, f32[136,128]{1,0:T(8,128)S(1)}, u32[]{:S(2)}, u32[]{:S(2)}) %collective-permute-start.8) | collective-permute-done | bytes 69664 | tf_op jit(solution)/shard_map/ppermute | solution.py:312
  80.8 2.4 %collective-permute-done.7.near = f32[136,128]{1,0:T(8,128)S(1)} collective-permute-done((f32[136,128]{1,0:T(8,128)S(1)}, f32[136,128]{1,0:T(8,128)S(1)}, u32[]{:S(2)}, u32[]{:S(2)}) %collective-permute-start.7) | collective-permute-done | bytes 69664 | tf_op jit(solution)/shard_map/ppermute | solution.py:312
  83.2 0.1 line_sum_kernel.1
  83.3 29.7 %all_to_all.11.mine = f32[32,136,128]{2,1,0:T(8,128)S(1)} all-to-all(f32[32,136,128]{2,1,0:T(8,128)S(1)} %line_sum_kernel.1), channel_id=1, replica_groups=mesh['zh'=4,'zp'=2,'x'=4,'core'=2,'y'=4] {'zp','x','y'}, dimensions={0} | all-to-all | bytes 4456448 | tf_op jit(solution)/shard_map/all_to_all | solution.py:308
  113.0 5.0 %collective-permute-start.10 = (f32[32,136,128]{2,1,0:T(8,128)S(1)}, f32[32,136,128]{2,1,0:T(8,128)S(1)}, u32[]{:S(2)}, u32[]{:S(2)}) collective-permute-start(f32[32,136,128]{2,1,0:T(8,128)S(1)} %all_to_all.11.mine), channel_id=1, source_target_pairs={{0,4},{4,0},{1,5},{5,1},{2,6},{6,2},{3,7},{7,3},{8,12},{12,8},{9,1... | collective-permute-start | bytes 6684680 | tf_op jit(solution)/shard_map/ppermute | solution.py:300
  118.0 2.0 %first_half_kernel.1 = (f32[64,16,1024]{2,1,0:T(8,128)}, f32[64,1024]{1,0:T(8,128)S(1)}) custom-call(s32[2]{0:T(128)S(1)} %pad_add_fusion.refs_0_.place, f32[32,136,128]{2,1,0:T(8,128)S(1)} %all_to_all.11.mine), custom_call_target="tpu_custom_call" | custom-call | tf_op jit(solution)/shard_map/first_half_kernel/pallas_call | solution.py:42
  120.0 2.0 %collective-permute-done.10.other = f32[32,136,128]{2,1,0:T(8,128)S(1)} collective-permute-done((f32[32,136,128]{2,1,0:T(8,128)S(1)}, f32[32,136,128]{2,1,0:T(8,128)S(1)}, u32[]{:S(2)}, u32[]{:S(2)}) %collective-permute-start.10) | collective-permute-done | bytes 2228256 | tf_op jit(solution)/shard_map/ppermute | solution.py:300
  122.0 2.1 %second_half_kernel.1 = (f32[64,16,1024]{2,1,0:T(8,128)}, f32[18,1024]{1,0:T(8,128)}, f32[36,1024]{1,0:T(8,128)}) custom-call(s32[2]{0:T(128)S(1)} %pad_add_fusion.refs_0_.place, f32[32,136,128]{2,1,0:T(8,128)S(1)} %collective-permute-done.10.other, f32[64,1024]{1,0:T(8,128)S(1)} %get-tuple-element.42.e_in, ...), custom_call_target="tpu_custom_call", output_to_operand_aliasing={{0}: (3, {})} | custom-call | tf_op jit(solution)/shard_map/second_half_kernel/pallas_call | solution.py:42
  (4 shorter events, 0.0 us)
Async XLA Ops:
  5.0 6.8 %collective-permute-start.2 = (f32[8,128]{1,0:T(8,128)S(1)}, f32[8,128]{1,0:T(8,128)S(1)}, u32[]{:S(2)}, u32[]{:S(2)}) collective-permute-start(f32[8,128]{1,0:T(8,128)S(1)} %get-tuple-element.31.refs_3_), channel_id=1, source_target_pairs={{0,3},{1,0},{2,1},{3,2},{4,7},{5,4},{6,5},{7,6},{8,11},{9,8},{10,9... | collective-permute-start | bytes 12296 | tf_op jit(solution)/shard_map/ppermute | solution.py:300
  8.6 3.7 %collective-permute-start.1 = (f32[8,128]{1,0:T(8,128)S(1)}, f32[8,128]{1,0:T(8,128)S(1)}, u32[]{:S(2)}, u32[]{:S(2)}) collective-permute-start(f32[8,128]{1,0:T(8,128)S(1)} %get-tuple-element.31.refs_3_), channel_id=1, source_target_pairs={{0,1},{1,2},{2,3},{3,0},{4,5},{5,6},{6,7},{7,4},{8,9},{9,10},{10,1... | collective-permute-start | bytes 12296 | tf_op jit(solution)/shard_map/ppermute | solution.py:300
  8.6 4.0 %collective-permute-start = (f32[8,128]{1,0:T(8,128)S(1)}, f32[8,128]{1,0:T(8,128)S(1)}, u32[]{:S(2)}, u32[]{:S(2)}) collective-permute-start(f32[8,128]{1,0:T(8,128)S(1)} %get-tuple-element.31.refs_3_), channel_id=1, source_target_pairs={{0,2},{1,3},{2,0},{3,1},{4,6},{5,7},{6,4},{7,5},{8,10},{9,11},{10,... | collective-permute-start | bytes 12296 | tf_op jit(solution)/shard_map/ppermute | solution.py:300
  12.7 6.3 %collective-permute-start.5 = (f32[8,128]{1,0:T(8,128)S(1)}, f32[8,128]{1,0:T(8,128)S(1)}, u32[]{:S(2)}, u32[]{:S(2)}) collective-permute-start(f32[8,128]{1,0:T(8,128)S(1)} %get-tuple-element.34.after.refs_4_), channel_id=1, source_target_pairs={{0,3},{1,0},{2,1},{3,2},{4,7},{5,4},{6,5},{7,6},{8,11},{9,8},{10,9... | collective-permute-start | bytes 12296 | tf_op jit(solution)/shard_map/ppermute | solution.py:300
  15.4 3.7 %collective-permute-start.4 = (f32[8,128]{1,0:T(8,128)S(1)}, f32[8,128]{1,0:T(8,128)S(1)}, u32[]{:S(2)}, u32[]{:S(2)}) collective-permute-start(f32[8,128]{1,0:T(8,128)S(1)} %get-tuple-element.34.after.refs_4_), channel_id=1, source_target_pairs={{0,1},{1,2},{2,3},{3,0},{4,5},{5,6},{6,7},{7,4},{8,9},{9,10},{10,1... | collective-permute-start | bytes 12296 | tf_op jit(solution)/shard_map/ppermute | solution.py:300
  15.4 4.0 %collective-permute-start.3 = (f32[8,128]{1,0:T(8,128)S(1)}, f32[8,128]{1,0:T(8,128)S(1)}, u32[]{:S(2)}, u32[]{:S(2)}) collective-permute-start(f32[8,128]{1,0:T(8,128)S(1)} %get-tuple-element.34.after.refs_4_), channel_id=1, source_target_pairs={{0,2},{1,3},{2,0},{3,1},{4,6},{5,7},{6,4},{7,5},{8,10},{9,11},{10,... | collective-permute-start | bytes 12296 | tf_op jit(solution)/shard_map/ppermute | solution.py:300
  23.8 7.9 %collective-permute-start.6 = (f32[32,136,128]{2,1,0:T(8,128)S(1)}, f32[32,136,128]{2,1,0:T(8,128)S(1)}, u32[]{:S(2)}, u32[]{:S(2)}) collective-permute-start(f32[32,136,128]{2,1,0:T(8,128)S(1)} %get-tuple-element.41), channel_id=1, source_target_pairs={{0,4},{4,0},{1,5},{5,1},{2,6},{6,2},{3,7},{7,3},{8,12},{12,8},{9,1... | collective-permute-start | bytes 6684680 | tf_op jit(solution)/shard_map/ppermute | solution.py:300
  69.6 8.1 %collective-permute-start.9 = (f32[136,128]{1,0:T(8,128)S(1)}, f32[136,128]{1,0:T(8,128)S(1)}, u32[]{:S(2)}, u32[]{:S(2)}) collective-permute-start(f32[136,128]{1,0:T(8,128)S(1)} %plane_sum_kernel.1.own), channel_id=1, source_target_pairs={{0,96},{32,192},{64,160},{96,0},{128,224},{160,64},{192,32},{224,1... | collective-permute-start | bytes 208904 | tf_op jit(solution)/shard_map/ppermute | solution.py:312
  73.5 7.3 %collective-permute-start.8 = (f32[136,128]{1,0:T(8,128)S(1)}, f32[136,128]{1,0:T(8,128)S(1)}, u32[]{:S(2)}, u32[]{:S(2)}) collective-permute-start(f32[136,128]{1,0:T(8,128)S(1)} %plane_sum_kernel.1.own), channel_id=1, source_target_pairs={{0,128},{32,160},{64,192},{96,224},{128,0},{160,32},{192,64},{224,... | collective-permute-start | bytes 208904 | tf_op jit(solution)/shard_map/ppermute | solution.py:312
  77.7 5.5 %collective-permute-start.7 = (f32[136,128]{1,0:T(8,128)S(1)}, f32[136,128]{1,0:T(8,128)S(1)}, u32[]{:S(2)}, u32[]{:S(2)}) collective-permute-start(f32[136,128]{1,0:T(8,128)S(1)} %plane_sum_kernel.1.own), channel_id=1, source_target_pairs={{0,224},{32,64},{64,32},{96,128},{128,96},{160,192},{192,160},{224... | collective-permute-start | bytes 208904 | tf_op jit(solution)/shard_map/ppermute | solution.py:312
  113.0 9.0 %collective-permute-start.10 = (f32[32,136,128]{2,1,0:T(8,128)S(1)}, f32[32,136,128]{2,1,0:T(8,128)S(1)}, u32[]{:S(2)}, u32[]{:S(2)}) collective-permute-start(f32[32,136,128]{2,1,0:T(8,128)S(1)} %all_to_all.11.mine), channel_id=1, source_target_pairs={{0,4},{4,0},{1,5},{5,1},{2,6},{6,2},{3,7},{7,3},{8,12},{12,8},{9,1... | collective-permute-start | bytes 6684680 | tf_op jit(solution)/shard_map/ppermute | solution.py:300

commit v6 on v5

--- a/solution.py
+++ b/solution.py
@@ -127,7 +127,10 @@
         store.wait()
 
 
-def targets_kernel(rew_far, ends_far, beh_far, act, s, o, tg_far, tg_out, sT_out, rew, ends, beh, sem):
+def targets_kernel(
+    rew_far, ends_far, beh_far, act, s, o, tg_far, pi_out, adv_out, dq_out, sT_out,
+    rew, ends, beh, tg_out, sem,
+):
     loads = [
         started(source, target, sem.at[i])
         for i, (source, target) in enumerate(((rew_far, rew), (ends_far, ends), (beh_far, beh)))
@@ -141,22 +144,28 @@
     v_next = policy_of(o, slice(steps * rows, (steps + 1) * rows), count)[-1]
     carried = jnp.zeros((1, rows), F32)
     for k in range(steps - 1, -1, -1):
-        logits, _, _, total, v = policy_of(o, slice(k * rows, (k + 1) * rows), count)
+        at = slice(k * rows, (k + 1) * rows)
+        logits, q, pi, total, v = policy_of(o, at, count)
+        pi_out[:, at] = pi
+        adv_out[:, at] = q - v
         b = beh[k]
         b_total = jnp.sum(jnp.exp(b), axis=0, keepdims=True)
         gap = (logits - jnp.log(total)) - (b - jnp.log(b_total))
-        ratio = jnp.exp(jnp.sum(jnp.where(chosen(act, k, count), gap, 0.0), axis=0, keepdims=True))
+        oh = chosen(act, k, count)
+        ratio = jnp.exp(jnp.sum(jnp.where(oh, gap, 0.0), axis=0, keepdims=True))
         clipped = jnp.minimum(1.0, ratio)
         open_ = 1.0 - ends[k : k + 1, :].astype(F32)
         td = rew[k : k + 1, :] + DISCOUNT * open_ * v_next - v
         carried = clipped * td + DISCOUNT * TRACE_LAMBDA * open_ * clipped * carried
         tg_out[k : k + 1, :] = v + carried
+        dq_out[:, at] = jnp.where(oh, q - (v + carried), 0.0)
         v_next = v
     started(tg_out, tg_far, sem.at[3]).wait()
 
 
-def weights_kernel(groups, devices, count, act, o, tg, ssq0, ssq1, ssq2, ssq3, a_out, b_out, mass_out):
+def weights_kernel(groups, devices, act, pis, advs, dqs, ssq0, ssq1, ssq2, ssq3, a_out, b_out, mass_out):
     steps, rows = act.shape
+    count = pis.shape[0]
     spread = ssq0[0:1, 0:1] + ssq1[0:1, 0:1] + ssq2[0:1, 0:1] + ssq3[0:1, 0:1]
     scale = jnp.sqrt(spread / (groups * rows * steps * count) + EPSILON)
     norm = 1.0 / (devices * rows * steps)
@@ -165,9 +174,9 @@
     b_out[...] = jnp.zeros_like(b_out)
     for k in range(steps):
         at = slice(k * rows, (k + 1) * rows)
-        _, q, pi, _, v = policy_of(o, at, count)
+        pi = pis[:, at]
         oh = chosen(act, k, count)
-        w = jnp.exp(jnp.clip((q - v) / scale, -1.0, 1.0))
+        w = jnp.exp(jnp.clip(advs[:, at] / scale, -1.0, 1.0))
         pw = pi * w
         mass = jnp.sum(pw, axis=0, keepdims=True)
         mass_sum = mass_sum + mass
@@ -175,19 +184,23 @@
         whole = jnp.sum(cmpo, axis=0, keepdims=True)
         taken = jnp.sum(jnp.where(oh, w, 0.0), axis=0, keepdims=True)
         a_out[0:count, at] = (pi * whole - cmpo) * norm
-        a_out[Q_ROW : Q_ROW + count, at] = jnp.where(oh, q - tg[k : k + 1, :], 0.0) * norm
+        a_out[Q_ROW : Q_ROW + count, at] = dqs[:, at] * norm
         b_out[0:count, at] = taken * (pi - jnp.where(oh, 1.0, 0.0)) * norm
     mass_out[...] = jnp.broadcast_to(jnp.sum(mass_sum, axis=1, keepdims=True), mass_out.shape)
 
 
-def fetch_kernel(t_far, wh_far, after, t, wh, sem):
-    for copy in (started(t_far, t, sem.at[0]), started(wh_far, wh, sem.at[1])):
+def fetch_kernel(t_far, wh_far, act, after, t, wh, oh, sem):
+    copies = started(t_far, t, sem.at[0]), started(wh_far, wh, sem.at[1])
+    steps, rows = act.shape
+    for k in range(steps - 1):
+        oh[:, k * rows : (k + 1) * rows] = onehot_of(act, k)
+    for copy in copies:
         copy.wait()
 
 
 def gradient_kernel(
-    groups, count, place, act, a, b, m0, m1, m2, m3, sT, t, wh, whp,
-    other, x, e, gf, g, oh,
+    groups, count, place, act, a, b, m0, m1, m2, m3, s, sT, t, wh, whp, oh,
+    other, x, e, gf, g,
 ):
     steps, rows = act.shape
     last = steps - 1
@@ -197,10 +210,8 @@
     gf[...] = a[...]
     gf[0:Q_ROW, :] = a[0:Q_ROW, :] + b[...] / mean
     g[...] = gf[...].astype(BF16)
-    for k in range(last):
-        oh[:, spans[k]] = onehot_of(act, k)
     e[...] = jnp.zeros_like(e)
-    heads = dot_nt(g[...], sT[...])
+    heads = dot(g[...], s[...])
     e[0:count, :] = heads[0:count, :]
     e[count : 2 * count, :] = heads[Q_ROW : Q_ROW + count, :]
     r = dot_tn(g[:, spans[last]], whp[...])
@@ -355,14 +366,16 @@
         far_outs=(1,),
     )
     ssqs = of_group(ssq)
-    targets, tg, sT = kernel_call(
+    per_action = ((count, steps * rows), F32)
+    targets, pis, advs, dqs, sT = kernel_call(
         targets_kernel,
-        [((steps, rows), F32), ((steps, rows), F32), ((hid, steps * rows), BF16)],
+        [((steps, rows), F32), per_action, per_action, per_action, ((hid, steps * rows), BF16)],
         (rewards.T, ends.T, jnp.transpose(behaviour, (1, 2, 0)), act, s, out),
         (
             pltpu.VMEM((steps, rows), F32),
             pltpu.VMEM((steps, rows), jnp.int32),
             pltpu.VMEM((steps, count, rows), F32),
+            pltpu.VMEM((steps, rows), F32),
             pltpu.SemaphoreType.DMA((4,)),
         ),
         far=range(3),
@@ -370,19 +383,19 @@
     )
 
     def weights_body(*refs):
-        weights_kernel(groups, devices, count, *refs)
+        weights_kernel(groups, devices, *refs)
 
     a, b, mass = kernel_call(
         weights_body,
         [((48, steps * rows), F32), ((Q_ROW, steps * rows), F32), ((8, LANES), F32)],
-        (act, out, tg, *ssqs),
+        (act, pis, advs, dqs, *ssqs),
     )
     masses = of_group(mass)
 
-    t, wh = kernel_call(
+    t, wh, oh = kernel_call(
         fetch_kernel,
-        [(t.shape, F32), (w_hidden.shape, BF16)],
-        (t, w_hidden, mass),
+        [(t.shape, F32), (w_hidden.shape, BF16), ((32, (steps - 1) * rows), BF16)],
+        (t, w_hidden, act, mass),
         (pltpu.SemaphoreType.DMA((2,)),),
         far=(0, 1),
     )
@@ -394,11 +407,10 @@
     other, x, extra = kernel_call(
         gradient_body,
         [parts, (((steps - 1) * rows, hid), BF16), ((64, hid), F32)],
-        (place, act, a, b, *masses, sT, t, wh, whp),
+        (place, act, a, b, *masses, s, sT, t, wh, whp, oh),
         (
             pltpu.VMEM((48, steps * rows), F32),
             pltpu.VMEM((48, steps * rows), BF16),
-            pltpu.VMEM((32, (steps - 1) * rows), BF16),
         ),
         scalars=1,
     )

time: 124 us -> 124 us (level)
  no operation moved by 1% of the time
where the time goes in v6:
time: 124 us
  blocking collectives  67.3 us (54%)
  starting transfers between devices  26.2 us (21%)
  Pallas kernels  18.1 us (15%)
  waiting for transfers between devices  11.2 us (9%)
    all_to_all x2, blocking collectives, swapped(): return lax.all_to_all(tiles, axis, split_axis=0, concat_axis=0, tiled=True)  67.3 us
    ppermute x8, starting transfers between devices, shifted(): lax.ppermute(array, axis, [(i, (i + by) % size) for i in range(size)])  18.1 us
    pallas_call x10, Pallas kernels, kernel_call(): pl.pallas_call(body, out_shape=tuple((FAR(s, d) if i in far_outs else jax...  18.1 us
    ppermute x3, starting transfers between devices, along_z(): return lax.ppermute(array, LINE, [(z, to(z)) for z in range(8)])  8.11 us
    ppermute x8, waiting for transfers between devices, shifted(): lax.ppermute(array, axis, [(i, (i + by) % size) for i in range(size)])  5.75 us
    ppermute x3, waiting for transfers between devices, along_z(): return lax.ppermute(array, LINE, [(z, to(z)) for z in range(8)])  5.46 us
  transfers between devices with their start and end apart: 11, of which 8 were waited for; matrix products, arithmetic and copies ran while one was open for 0% of the time, Pallas kernels for 6%

profile of v6, /device:TPU:1, one launch (start us, length us, event | category | flops | bytes accessed | tf_op | source)
XLA Modules:
  0.0 123.9 jit_solution(2557458941360339796)
XLA Ops:
  0.6 4.3 %unroll_kernel.1 = (bf16[640,1024]{1,0:T(8,128)(2,1)S(1)}, f32[512,1024]{1,0:T(8,128)}, f32[48,768]{1,0:T(8,128)S(1)}, f32[8,128]{1,0:T(8,128)S(1)}, s32[5,128]{1,0:T(8,128)S(1)}, /*index=5*/bf16[48,1024]{1,0:T(8,128)(2,1)S(1)}) custom-call(bf16[128,1024]{1,0:T(8,128)(2,1)} %emb_far.1, s32[5,128]{1,0:T(8,128)} %bitcast.13, bf16[1024,1024]{1,0:T(8,128)(2,1)} %wh_far.3, ...), custom_call_target="tpu_custom_call" | custom-call | tf_op jit(solution)/shard_map/unroll_kernel/pallas_call | solution.py:42
  5.0 3.6 %collective-permute-start.2 = (f32[8,128]{1,0:T(8,128)S(1)}, f32[8,128]{1,0:T(8,128)S(1)}, u32[]{:S(2)}, u32[]{:S(2)}) collective-permute-start(f32[8,128]{1,0:T(8,128)S(1)} %get-tuple-element.36.refs_4_), channel_id=1, source_target_pairs={{0,3},{1,0},{2,1},{3,2},{4,7},{5,4},{6,5},{7,6},{8,11},{9,8},{10,9... | collective-permute-start | bytes 12296 | tf_op jit(solution)/shard_map/ppermute | solution.py:311
  8.6 0.0 collective-permute-start.1
  8.6 1.6 %collective-permute-start = (f32[8,128]{1,0:T(8,128)S(1)}, f32[8,128]{1,0:T(8,128)S(1)}, u32[]{:S(2)}, u32[]{:S(2)}) collective-permute-start(f32[8,128]{1,0:T(8,128)S(1)} %get-tuple-element.36.refs_4_), channel_id=1, source_target_pairs={{0,2},{1,3},{2,0},{3,1},{4,6},{5,7},{6,4},{7,5},{8,10},{9,11},{10,... | collective-permute-start | bytes 12296 | tf_op jit(solution)/shard_map/ppermute | solution.py:311
  10.2 1.5 %targets_kernel.1 = (f32[5,128]{1,0:T(8,128)}, f32[18,640]{1,0:T(8,128)S(1)}, f32[18,640]{1,0:T(8,128)S(1)}, f32[18,640]{1,0:T(8,128)S(1)}, bf16[1024,640]{1,0:T(8,128)(2,1)S(1)}) custom-call(f32[5,128]{1,0:T(8,128)} %bitcast.14, s32[5,128]{1,0:T(8,128)} %bitcast.15, f32[5,18,128]{2,1,0:T(8,128)} %bitcast.12, ...), custom_call_target="tpu_custom_call" | custom-call | tf_op jit(solution)/shard_map/targets_kernel/pallas_call | solution.py:42
  11.8 0.0 collective-permute-done.2.refs_7_
  11.8 0.5 collective-permute-done.1.refs_6_
  12.3 0.3 collective-permute-done.refs_5_
  12.6 0.2 weights_body.1
  12.7 2.7 %collective-permute-start.5 = (f32[8,128]{1,0:T(8,128)S(1)}, f32[8,128]{1,0:T(8,128)S(1)}, u32[]{:S(2)}, u32[]{:S(2)}) collective-permute-start(f32[8,128]{1,0:T(8,128)S(1)} %get-tuple-element.39.after.refs_4_), channel_id=1, source_target_pairs={{0,3},{1,0},{2,1},{3,2},{4,7},{5,4},{6,5},{7,6},{8,11},{9,8},{10,9... | collective-permute-start | bytes 12296 | tf_op jit(solution)/shard_map/ppermute | solution.py:311
  15.4 1.3 %collective-permute-start.3 = (f32[8,128]{1,0:T(8,128)S(1)}, f32[8,128]{1,0:T(8,128)S(1)}, u32[]{:S(2)}, u32[]{:S(2)}) collective-permute-start(f32[8,128]{1,0:T(8,128)S(1)} %get-tuple-element.39.after.refs_4_), channel_id=1, source_target_pairs={{0,2},{1,3},{2,0},{3,1},{4,6},{5,7},{6,4},{7,5},{8,10},{9,11},{10,... | collective-permute-start | bytes 12296 | tf_op jit(solution)/shard_map/ppermute | solution.py:311
  16.7 0.1 pad_add_fusion.refs_0_.place
  16.8 2.2 %fetch_kernel.1 = (f32[512,1024]{1,0:T(8,128)S(1)}, bf16[1024,1024]{1,0:T(8,128)(2,1)S(1)}, bf16[32,512]{1,0:T(8,128)(2,1)S(1)}) custom-call(f32[512,1024]{1,0:T(8,128)} %get-tuple-element.40.t_far, bf16[1024,1024]{1,0:T(8,128)(2,1)} %wh_far.3, s32[5,128]{1,0:T(8,128)S(1)} %get-tuple-element.29.act.refs_0_.refs_1_, f32[8,128]{1,0:T(8,128)S(1)} %get-tuple-element.39.after.refs_4_), custom_call_target="tpu_custom_call" | custom-call | tf_op jit(solution)/shard_map/fetch_kernel/pallas_call | solution.py:42
  19.0 0.1 collective-permute-done.4.refs_6_
  19.1 0.3 collective-permute-done.3.refs_5_
  19.4 4.2 %gradient_body.1 = (f32[32,136,128]{2,1,0:T(8,128)S(1)}, bf16[512,1024]{1,0:T(8,128)(2,1)S(1)}, f32[64,1024]{1,0:T(8,128)S(1)}) custom-call(s32[2]{0:T(128)S(1)} %pad_add_fusion.refs_0_.place, s32[5,128]{1,0:T(8,128)S(1)} %get-tuple-element.29.act.refs_0_.refs_1_, f32[48,640]{1,0:T(8,128)S(1)} %get-tuple-element.37.refs_2_, ...), custom_call_target="tpu_custom_call" | custom-call | tf_op jit(solution)/shard_map/gradient_body/pallas_call | solution.py:42
  23.6 3.9 %collective-permute-start.6 = (f32[32,136,128]{2,1,0:T(8,128)S(1)}, f32[32,136,128]{2,1,0:T(8,128)S(1)}, u32[]{:S(2)}, u32[]{:S(2)}) collective-permute-start(f32[32,136,128]{2,1,0:T(8,128)S(1)} %get-tuple-element.47), channel_id=1, source_target_pairs={{0,4},{4,0},{1,5},{5,1},{2,6},{6,2},{3,7},{7,3},{8,12},{12,8},{9,1... | collective-permute-start | bytes 6684680 | tf_op jit(solution)/shard_map/ppermute | solution.py:311
  27.5 1.3 %mine_kernel.1 = f32[32,136,128]{2,1,0:T(8,128)S(1)} custom-call(s32[2]{0:T(128)S(1)} %pad_add_fusion.refs_0_.place, bf16[1024,640]{1,0:T(8,128)(2,1)S(1)} %get-tuple-element.32.refs_9_.sT, bf16[512,1024]{1,0:T(8,128)(2,1)S(1)} %get-tuple-element.45.x, f32[64,1024]{1,0:T(8,128)S(1)} %get-tuple-element.46.e), custom_call_target="tpu_custom_call" | custom-call | tf_op jit(solution)/shard_map/mine_kernel/pallas_call | solution.py:42
  28.8 2.6 %collective-permute-done.6 = f32[32,136,128]{2,1,0:T(8,128)S(1)} collective-permute-done((f32[32,136,128]{2,1,0:T(8,128)S(1)}, f32[32,136,128]{2,1,0:T(8,128)S(1)}, u32[]{:S(2)}, u32[]{:S(2)}) %collective-permute-start.6) | collective-permute-done | bytes 2228256 | tf_op jit(solution)/shard_map/ppermute | solution.py:311
  31.5 0.3 add.8
  31.7 37.6 %all_to_all.10.arrived = f32[32,136,128]{2,1,0:T(8,128)S(1)} all-to-all(f32[32,136,128]{2,1,0:T(8,128)S(1)} %add.8), channel_id=1, replica_groups=mesh['zh'=4,'zp'=2,'x'=4,'core'=2,'y'=4] {'zp','x','y'}, dimensions={0} | all-to-all | bytes 4456448 | tf_op jit(solution)/shard_map/all_to_all | solution.py:319
  69.3 0.1 plane_sum_kernel.1.own
  69.4 3.9 %collective-permute-start.9 = (f32[136,128]{1,0:T(8,128)S(1)}, f32[136,128]{1,0:T(8,128)S(1)}, u32[]{:S(2)}, u32[]{:S(2)}) collective-permute-start(f32[136,128]{1,0:T(8,128)S(1)} %plane_sum_kernel.1.own), channel_id=1, source_target_pairs={{0,96},{32,192},{64,160},{96,0},{128,224},{160,64},{192,32},{224,1... | collective-permute-start | bytes 208904 | tf_op jit(solution)/shard_map/ppermute | solution.py:323
  73.3 4.2 %collective-permute-start.8 = (f32[136,128]{1,0:T(8,128)S(1)}, f32[136,128]{1,0:T(8,128)S(1)}, u32[]{:S(2)}, u32[]{:S(2)}) collective-permute-start(f32[136,128]{1,0:T(8,128)S(1)} %plane_sum_kernel.1.own), channel_id=1, source_target_pairs={{0,128},{32,160},{64,192},{96,224},{128,0},{160,32},{192,64},{224,... | collective-permute-start | bytes 208904 | tf_op jit(solution)/shard_map/ppermute | solution.py:323
  77.6 3.1 %collective-permute-done.8.far = f32[136,128]{1,0:T(8,128)S(1)} collective-permute-done((f32[136,128]{1,0:T(8,128)S(1)}, f32[136,128]{1,0:T(8,128)S(1)}, u32[]{:S(2)}, u32[]{:S(2)}) %collective-permute-start.8) | collective-permute-done | bytes 69664 | tf_op jit(solution)/shard_map/ppermute | solution.py:323
  80.7 2.4 %collective-permute-done.7.near = f32[136,128]{1,0:T(8,128)S(1)} collective-permute-done((f32[136,128]{1,0:T(8,128)S(1)}, f32[136,128]{1,0:T(8,128)S(1)}, u32[]{:S(2)}, u32[]{:S(2)}) %collective-permute-start.7) | collective-permute-done | bytes 69664 | tf_op jit(solution)/shard_map/ppermute | solution.py:323
  83.0 0.1 line_sum_kernel.1
  83.2 29.7 %all_to_all.11.mine = f32[32,136,128]{2,1,0:T(8,128)S(1)} all-to-all(f32[32,136,128]{2,1,0:T(8,128)S(1)} %line_sum_kernel.1), channel_id=1, replica_groups=mesh['zh'=4,'zp'=2,'x'=4,'core'=2,'y'=4] {'zp','x','y'}, dimensions={0} | all-to-all | bytes 4456448 | tf_op jit(solution)/shard_map/all_to_all | solution.py:319
  112.9 5.0 %collective-permute-start.10 = (f32[32,136,128]{2,1,0:T(8,128)S(1)}, f32[32,136,128]{2,1,0:T(8,128)S(1)}, u32[]{:S(2)}, u32[]{:S(2)}) collective-permute-start(f32[32,136,128]{2,1,0:T(8,128)S(1)} %all_to_all.11.mine), channel_id=1, source_target_pairs={{0,4},{4,0},{1,5},{5,1},{2,6},{6,2},{3,7},{7,3},{8,12},{12,8},{9,1... | collective-permute-start | bytes 6684680 | tf_op jit(solution)/shard_map/ppermute | solution.py:311
  117.9 2.0 %first_half_kernel.1 = (f32[64,16,1024]{2,1,0:T(8,128)}, f32[64,1024]{1,0:T(8,128)S(1)}) custom-call(s32[2]{0:T(128)S(1)} %pad_add_fusion.refs_0_.place, f32[32,136,128]{2,1,0:T(8,128)S(1)} %all_to_all.11.mine), custom_call_target="tpu_custom_call" | custom-call | tf_op jit(solution)/shard_map/first_half_kernel/pallas_call | solution.py:42
  119.9 2.0 %collective-permute-done.10.other = f32[32,136,128]{2,1,0:T(8,128)S(1)} collective-permute-done((f32[32,136,128]{2,1,0:T(8,128)S(1)}, f32[32,136,128]{2,1,0:T(8,128)S(1)}, u32[]{:S(2)}, u32[]{:S(2)}) %collective-permute-start.10) | collective-permute-done | bytes 2228256 | tf_op jit(solution)/shard_map/ppermute | solution.py:311
  121.8 2.1 %second_half_kernel.1 = (f32[64,16,1024]{2,1,0:T(8,128)}, f32[18,1024]{1,0:T(8,128)}, f32[36,1024]{1,0:T(8,128)}) custom-call(s32[2]{0:T(128)S(1)} %pad_add_fusion.refs_0_.place, f32[32,136,128]{2,1,0:T(8,128)S(1)} %collective-permute-done.10.other, f32[64,1024]{1,0:T(8,128)S(1)} %get-tuple-element.48.e_in, ...), custom_call_target="tpu_custom_call", output_to_operand_aliasing={{0}: (3, {})} | custom-call | tf_op jit(solution)/shard_map/second_half_kernel/pallas_call | solution.py:42
  (4 shorter events, 0.0 us)
Async XLA Ops:
  5.0 6.8 %collective-permute-start.2 = (f32[8,128]{1,0:T(8,128)S(1)}, f32[8,128]{1,0:T(8,128)S(1)}, u32[]{:S(2)}, u32[]{:S(2)}) collective-permute-start(f32[8,128]{1,0:T(8,128)S(1)} %get-tuple-element.36.refs_4_), channel_id=1, source_target_pairs={{0,3},{1,0},{2,1},{3,2},{4,7},{5,4},{6,5},{7,6},{8,11},{9,8},{10,9... | collective-permute-start | bytes 12296 | tf_op jit(solution)/shard_map/ppermute | solution.py:311
  8.6 3.7 %collective-permute-start.1 = (f32[8,128]{1,0:T(8,128)S(1)}, f32[8,128]{1,0:T(8,128)S(1)}, u32[]{:S(2)}, u32[]{:S(2)}) collective-permute-start(f32[8,128]{1,0:T(8,128)S(1)} %get-tuple-element.36.refs_4_), channel_id=1, source_target_pairs={{0,1},{1,2},{2,3},{3,0},{4,5},{5,6},{6,7},{7,4},{8,9},{9,10},{10,1... | collective-permute-start | bytes 12296 | tf_op jit(solution)/shard_map/ppermute | solution.py:311
  8.6 4.0 %collective-permute-start = (f32[8,128]{1,0:T(8,128)S(1)}, f32[8,128]{1,0:T(8,128)S(1)}, u32[]{:S(2)}, u32[]{:S(2)}) collective-permute-start(f32[8,128]{1,0:T(8,128)S(1)} %get-tuple-element.36.refs_4_), channel_id=1, source_target_pairs={{0,2},{1,3},{2,0},{3,1},{4,6},{5,7},{6,4},{7,5},{8,10},{9,11},{10,... | collective-permute-start | bytes 12296 | tf_op jit(solution)/shard_map/ppermute | solution.py:311
  12.7 6.3 %collective-permute-start.5 = (f32[8,128]{1,0:T(8,128)S(1)}, f32[8,128]{1,0:T(8,128)S(1)}, u32[]{:S(2)}, u32[]{:S(2)}) collective-permute-start(f32[8,128]{1,0:T(8,128)S(1)} %get-tuple-element.39.after.refs_4_), channel_id=1, source_target_pairs={{0,3},{1,0},{2,1},{3,2},{4,7},{5,4},{6,5},{7,6},{8,11},{9,8},{10,9... | collective-permute-start | bytes 12296 | tf_op jit(solution)/shard_map/ppermute | solution.py:311
  15.4 3.7 %collective-permute-start.4 = (f32[8,128]{1,0:T(8,128)S(1)}, f32[8,128]{1,0:T(8,128)S(1)}, u32[]{:S(2)}, u32[]{:S(2)}) collective-permute-start(f32[8,128]{1,0:T(8,128)S(1)} %get-tuple-element.39.after.refs_4_), channel_id=1, source_target_pairs={{0,1},{1,2},{2,3},{3,0},{4,5},{5,6},{6,7},{7,4},{8,9},{9,10},{10,1... | collective-permute-start | bytes 12296 | tf_op jit(solution)/shard_map/ppermute | solution.py:311
  15.4 4.0 %collective-permute-start.3 = (f32[8,128]{1,0:T(8,128)S(1)}, f32[8,128]{1,0:T(8,128)S(1)}, u32[]{:S(2)}, u32[]{:S(2)}) collective-permute-start(f32[8,128]{1,0:T(8,128)S(1)} %get-tuple-element.39.after.refs_4_), channel_id=1, source_target_pairs={{0,2},{1,3},{2,0},{3,1},{4,6},{5,7},{6,4},{7,5},{8,10},{9,11},{10,... | collective-permute-start | bytes 12296 | tf_op jit(solution)/shard_map/ppermute | solution.py:311
  23.6 7.9 %collective-permute-start.6 = (f32[32,136,128]{2,1,0:T(8,128)S(1)}, f32[32,136,128]{2,1,0:T(8,128)S(1)}, u32[]{:S(2)}, u32[]{:S(2)}) collective-permute-start(f32[32,136,128]{2,1,0:T(8,128)S(1)} %get-tuple-element.47), channel_id=1, source_target_pairs={{0,4},{4,0},{1,5},{5,1},{2,6},{6,2},{3,7},{7,3},{8,12},{12,8},{9,1... | collective-permute-start | bytes 6684680 | tf_op jit(solution)/shard_map/ppermute | solution.py:311
  69.4 8.1 %collective-permute-start.9 = (f32[136,128]{1,0:T(8,128)S(1)}, f32[136,128]{1,0:T(8,128)S(1)}, u32[]{:S(2)}, u32[]{:S(2)}) collective-permute-start(f32[136,128]{1,0:T(8,128)S(1)} %plane_sum_kernel.1.own), channel_id=1, source_target_pairs={{0,96},{32,192},{64,160},{96,0},{128,224},{160,64},{192,32},{224,1... | collective-permute-start | bytes 208904 | tf_op jit(solution)/shard_map/ppermute | solution.py:323
  73.3 7.3 %collective-permute-start.8 = (f32[136,128]{1,0:T(8,128)S(1)}, f32[136,128]{1,0:T(8,128)S(1)}, u32[]{:S(2)}, u32[]{:S(2)}) collective-permute-start(f32[136,128]{1,0:T(8,128)S(1)} %plane_sum_kernel.1.own), channel_id=1, source_target_pairs={{0,128},{32,160},{64,192},{96,224},{128,0},{160,32},{192,64},{224,... | collective-permute-start | bytes 208904 | tf_op jit(solution)/shard_map/ppermute | solution.py:323
  77.5 5.5 %collective-permute-start.7 = (f32[136,128]{1,0:T(8,128)S(1)}, f32[136,128]{1,0:T(8,128)S(1)}, u32[]{:S(2)}, u32[]{:S(2)}) collective-permute-start(f32[136,128]{1,0:T(8,128)S(1)} %plane_sum_kernel.1.own), channel_id=1, source_target_pairs={{0,224},{32,64},{64,32},{96,128},{128,96},{160,192},{192,160},{224... | collective-permute-start | bytes 208904 | tf_op jit(solution)/shard_map/ppermute | solution.py:323
  112.9 9.0 %collective-permute-start.10 = (f32[32,136,128]{2,1,0:T(8,128)S(1)}, f32[32,136,128]{2,1,0:T(8,128)S(1)}, u32[]{:S(2)}, u32[]{:S(2)}) collective-permute-start(f32[32,136,128]{2,1,0:T(8,128)S(1)} %all_to_all.11.mine), channel_id=1, source_target_pairs={{0,4},{4,0},{1,5},{5,1},{2,6},{6,2},{3,7},{7,3},{8,12},{12,8},{9,1... | collective-permute-start | bytes 6684680 | tf_op jit(solution)/shard_map/ppermute | solution.py:311
